TPU v7x, 32 devices: a 4x4x1 block of a 4x4x8 slice. The times are simulated.
32 devices in a mesh: dp: 1 (over z), sz: 4 (over y), sy: 4 (over x), sx: 2 (over core).
Axes of the slice: x: 4, y: 4, z: 1, core: 2. Of those that a mesh axis runs over, the one named last changes fastest.
The devices are a block of a 4x4x8 slice.
Arguments:
- rhs_grid: float32 [256, 256, 256], P(('dp', 'sx'), 'sy', 'sz')
- u_start: float32 [256, 256, 256], P(('dp', 'sx'), 'sy', 'sz')
Outputs:
- output: float32 [256, 256, 256], P(('dp', 'sx'), 'sy', 'sz')
All inputs are finite; a program needn't handle non-finite values.
Results may differ from a plain program's by a relative error of at most 0.001.
Values sent between devices are 32-bit elements.
A program may use at most 768 MiB of HBM per device.

v0:
```python
import functools
import jax
import jax.numpy as jnp
from jax import lax
from jax.sharding import PartitionSpec as P

AXIS_NAMES = ('sx', 'sy', 'sz')
LEVELS = 4
SMOOTH_SWEEPS = 2
COARSE_SWEEPS = 16


def send_up(plane, name, count):
    if count == 1:
        return jnp.zeros_like(plane)
    return lax.ppermute(plane, name, [(rank, rank + 1) for rank in range(count - 1)])


def send_down(plane, name, count):
    if count == 1:
        return jnp.zeros_like(plane)
    return lax.ppermute(plane, name, [(rank + 1, rank) for rank in range(count - 1)])


def edge_plane(field, axis, index):
    return lax.slice_in_dim(field, index, index + 1, axis=axis)


def neighbour_sum(field, counts):
    ghosts = []
    for axis in range(3):
        length = field.shape[axis]
        lower = send_up(edge_plane(field, axis, length - 1), AXIS_NAMES[axis], counts[axis])
        upper = send_down(edge_plane(field, axis, 0), AXIS_NAMES[axis], counts[axis])
        ghosts.append((lower, upper))
    total = jnp.zeros_like(field)
    for axis in range(3):
        length = field.shape[axis]
        lower, upper = ghosts[axis]
        total = total + jnp.concatenate([lower, lax.slice_in_dim(field, 0, length - 1, axis=axis)], axis=axis)
        total = total + jnp.concatenate([lax.slice_in_dim(field, 1, length, axis=axis), upper], axis=axis)
    return total


def residual(source, field, stiffness, counts):
    return source - stiffness * (6.0 * field - neighbour_sum(field, counts))


def jacobi_sweep(source, field, stiffness, counts):
    return field + residual(source, field, stiffness, counts) / (9.0 * stiffness)


def restrict_axis(fine, lower, axis):
    half = fine.shape[axis] // 2
    pairs = fine.reshape(fine.shape[:axis] + (half, 2) + fine.shape[axis + 1:])
    even = lax.index_in_dim(pairs, 0, axis + 1, keepdims=False)
    odd = lax.index_in_dim(pairs, 1, axis + 1, keepdims=False)
    odd_prev = jnp.concatenate([lower, lax.slice_in_dim(odd, 0, half - 1, axis=axis)], axis=axis)
    return 0.25 * (odd_prev + odd) + 0.5 * even


def prolong_axis(coarse, upper, axis):
    length = coarse.shape[axis]
    shifted = jnp.concatenate([lax.slice_in_dim(coarse, 1, length, axis=axis), upper], axis=axis)
    stacked = jnp.stack([coarse, 0.5 * (coarse + shifted)], axis=axis + 1)
    return stacked.reshape(coarse.shape[:axis] + (2 * length,) + coarse.shape[axis + 1:])


def restrict(fine, counts):
    for axis in range(3):
        lower = send_up(edge_plane(fine, axis, fine.shape[axis] - 1), AXIS_NAMES[axis], counts[axis])
        fine = restrict_axis(fine, lower, axis)
    return fine


def prolong(coarse, counts):
    for axis in range(3):
        upper = send_down(edge_plane(coarse, axis, 0), AXIS_NAMES[axis], counts[axis])
        coarse = prolong_axis(coarse, upper, axis)
    return coarse


def vcycle(level, source, field, counts, size):
    stiffness = ((size + 1) / 2 ** level) ** 2
    coarsest = level == LEVELS - 1
    sweeps = COARSE_SWEEPS if coarsest else SMOOTH_SWEEPS
    if field is None:
        field = source / (9.0 * stiffness)
        sweeps = sweeps - 1
    for sweep in range(sweeps):
        field = jacobi_sweep(source, field, stiffness, counts)
    if coarsest:
        return field
    coarse_source = restrict(residual(source, field, stiffness, counts), counts)
    correction = vcycle(level + 1, coarse_source, None, counts, size)
    field = field + prolong(correction, counts)
    for sweep in range(SMOOTH_SWEEPS):
        field = jacobi_sweep(source, field, stiffness, counts)
    return field


def solution(mesh):
    counts = (mesh.shape['sx'], mesh.shape['sy'], mesh.shape['sz'])
    spec = P(('dp', 'sx'), 'sy', 'sz')

    def run(rhs_grid, u_start):
        size = rhs_grid.shape[1]
        local_cycle = functools.partial(vcycle, 0, counts=counts, size=size)
        return jax.shard_map(local_cycle, mesh=mesh, in_specs=(spec, spec), out_specs=spec, check_vma=False)(rhs_grid, u_start)
    return run
```

profile of v0, /device:TPU:97, one launch (start us, length us, event | category | flops | bytes accessed | tf_op | source)
XLA Modules:
  0.0 1038.4 jit_solution(14054805582478826610)
XLA Ops:
  1.1 4.6 collective-permute-start.4
  12.6 5.6 copy.2290
  22.3 8.7 fusion.514
  31.1 4.7 fusion.513
  41.6 4.7 copy.2289
  46.3 4.4 copy.2288
  50.7 4.4 copy.2285
  55.2 15.9 %fusion.8 = f32[128,64,64]{2,1,0:T(8,128)S(1)} fusion(f32[128,64,64]{2,1,0:T(8,128)} %copy.2290, f32[128,64,64]{2,1,0:T(8,128)} %copy.2289, f32[127,64,64]{2,1,0:T(8,128)} %get-tuple-element.80, f32[1,64,64]{2,1,0:T(8,128)S(1)} %collective-permute-done, f32[1,64,64]{2,1,0:T(8,128)S(1)} %collective-permute-done.1, f32[127,64,64]{2,1,0:T(8,128)} %get-tuple-element.79, ...), kind=kLoop, calls=%fused_computation.9 | loop fusion | flops 8912896 | bytes 18874368 | tf_op jit(solution)/shard_map/add | solution.py:50
  71.1 4.9 fusion.508
  76.0 4.9 fusion.507
  80.9 4.7 fusion.509
  97.6 5.0 collective-permute-start.8
  106.3 5.1 collective-permute-start.10
  111.4 8.5 fusion.511
  124.3 4.4 copy.2292
  128.8 15.9 %fusion.17 = f32[128,64,64]{2,1,0:T(8,128)S(1)} fusion(f32[128,64,64]{2,1,0:T(8,128)} %copy-done.3, f32[128,64,64]{2,1,0:T(8,128)} %copy.2289, f32[127,64,64]{2,1,0:T(8,128)} %get-tuple-element.72, f32[1,64,64]{2,1,0:T(8,128)S(1)} %collective-permute-done.6, f32[1,64,64]{2,1,0:T(8,128)S(1)} %collective-permute-done.7, f32[127,64,64]{2,1,0:T(8,128)} %get-tuple-element.71, ...), kind=kLoop, calls=%fused_computation.19 | loop fusion | flops 8912896 | bytes 18874368 | tf_op jit(solution)/shard_map/add | solution.py:50
  144.7 4.7 fusion.503
  149.5 4.9 fusion.501
  154.4 4.9 fusion.502
  183.6 8.5 fusion.505
  196.6 4.4 copy.2297
  201.0 15.7 %fusion.24 = f32[128,64,64]{2,1,0:T(8,128)S(1)} fusion(f32[128,64,64]{2,1,0:T(8,128)} %copy.2289, f32[127,64,64]{2,1,0:T(8,128)} %get-tuple-element.60, f32[1,64,64]{2,1,0:T(8,128)S(1)} %collective-permute-done.12, f32[1,64,64]{2,1,0:T(8,128)S(1)} %collective-permute-done.13, f32[127,64,64]{2,1,0:T(8,128)} %get-tuple-element.59, ...), kind=kLoop, calls=%fused_computation.27 | loop fusion | flops 7864320 | bytes 18874368 | tf_op jit(solution)/shard_map/sub | solution.py:46
  273.3 6.2 collective-permute-start.22
  310.8 4.7 collective-permute-start.28
  319.9 4.7 collective-permute-start.31
  359.5 7.2 fusion.49
  406.7 6.6 collective-permute-start.37
  460.1 4.9 collective-permute-start.46
  498.6 4.7 collective-permute-start.55
  504.6 4.6 collective-permute-start.53
  759.2 4.7 collective-permute-start.145
  812.1 4.6 collective-permute-start.160
  877.1 4.5 copy.2554
  886.1 4.7 fusion.495
  890.8 4.7 fusion.494
  905.7 4.6 collective-permute-start.175
  920.7 4.5 collective-permute-start.178
  925.2 8.5 fusion.498
  933.7 4.4 copy.2558
  938.2 4.4 copy.2556
  942.6 15.9 %fusion.33 = f32[128,64,64]{2,1,0:T(8,128)S(1)} fusion(f32[128,64,64]{2,1,0:T(8,128)} %copy-done.1, f32[128,64,64]{2,1,0:T(8,128)} %copy.2289, f32[127,64,64]{2,1,0:T(8,128)} %get-tuple-element.46, f32[1,64,64]{2,1,0:T(8,128)S(1)} %collective-permute-done.174, f32[1,64,64]{2,1,0:T(8,128)S(1)} %collective-permute-done.175, ...), kind=kLoop, calls=%fused_computation.37 | loop fusion | flops 8912896 | bytes 18874368 | tf_op jit(solution)/shard_map/add | solution.py:50
  958.6 4.9 fusion.489
  963.5 4.9 fusion.488
  968.4 4.7 fusion.490
  997.8 8.5 fusion.492
  1010.8 4.4 copy.2561
  1015.2 18.0 %fusion.42 = f32[128,64,64]{2,1,0:T(8,128)} fusion(f32[128,64,64]{2,1,0:T(8,128)} %copy-done.2, f32[128,64,64]{2,1,0:T(8,128)} %copy.2289, f32[127,64,64]{2,1,0:T(8,128)} %get-tuple-element.34, f32[1,64,64]{2,1,0:T(8,128)S(1)} %collective-permute-done.180, f32[1,64,64]{2,1,0:T(8,128)S(1)} %collective-permute-done.181, f32[127,64,64]{2,1,0:T(8,128)} %get-tuple-element.33, ...), kind=kLoop, calls=%fused_computation.47 | loop fusion | flops 8912896 | bytes 18874368 | tf_op jit(solution)/shard_map/add | solution.py:50
  1033.2 4.8 copy.2565
  (846 shorter events, 725.1 us)
Async XLA Ops:
  1.1 49.6 %collective-permute-start.4 = (f32[128,64,1]{0,1,2:T(8,128)S(1)}, f32[128,64,1]{0,1,2:T(8,128)S(1)}, u32[]{:S(2)}, u32[]{:S(2)}) collective-permute-start(f32[128,64,1]{0,1,2:T(8,128)S(1)} %bitcast.915), channel_id=1, source_target_pairs={{0,8},{8,16},{16,24},{1,9},{9,17},{17,25},{2,10},{10,18},{18,26},{... | collective-permute-start | bytes 98312 | tf_op jit(solution)/shard_map/ppermute | solution.py:16
  5.7 30.1 %collective-permute-start.5 = (f32[128,64,1]{0,1,2:T(8,128)S(1)}, f32[128,64,1]{0,1,2:T(8,128)S(1)}, u32[]{:S(2)}, u32[]{:S(2)}) collective-permute-start(f32[128,64,1]{0,1,2:T(8,128)S(1)} %bitcast.916), channel_id=1, source_target_pairs={{8,0},{16,8},{24,16},{9,1},{17,9},{25,17},{10,2},{18,10},{26,18},{... | collective-permute-start | bytes 98312 | tf_op jit(solution)/shard_map/ppermute | solution.py:22
  7.9 47.3 %collective-permute-start.2 = (f32[128,1,64]{2,1,0:T(1,128)S(1)}, f32[128,1,64]{2,1,0:T(1,128)S(1)}, u32[]{:S(2)}, u32[]{:S(2)}) collective-permute-start(f32[128,1,64]{2,1,0:T(1,128)S(1)} %copy.2279), channel_id=1, source_target_pairs={{0,2},{2,4},{4,6},{1,3},{3,5},{5,7},{8,10},{10,12},{12,14},{9,11},... | collective-permute-start | bytes 98312 | tf_op jit(solution)/shard_map/ppermute | solution.py:16
  11.3 43.9 %collective-permute-start.3 = (f32[128,1,64]{2,1,0:T(1,128)S(1)}, f32[128,1,64]{2,1,0:T(1,128)S(1)}, u32[]{:S(2)}, u32[]{:S(2)}) collective-permute-start(f32[128,1,64]{2,1,0:T(1,128)S(1)} %copy.2282), channel_id=1, source_target_pairs={{2,0},{4,2},{6,4},{3,1},{5,3},{7,5},{10,8},{12,10},{14,12},{11,9},... | collective-permute-start | bytes 98312 | tf_op jit(solution)/shard_map/ppermute | solution.py:22
  19.0 36.2 %collective-permute-start.1 = (f32[1,64,64]{2,1,0:T(8,128)S(1)}, f32[1,64,64]{2,1,0:T(8,128)S(1)}, u32[]{:S(2)}, u32[]{:S(2)}) collective-permute-start(f32[1,64,64]{2,1,0:T(8,128)S(1)} %get-tuple-element.81), channel_id=1, source_target_pairs={{1,0},{3,2},{5,4},{7,6},{9,8},{11,10},{13,12},{15,14},{17,16},{19,... | collective-permute-start | bytes 49160 | tf_op jit(solution)/shard_map/ppermute | solution.py:22
  35.8 19.4 %collective-permute-start = (f32[1,64,64]{2,1,0:T(8,128)S(1)}, f32[1,64,64]{2,1,0:T(8,128)S(1)}, u32[]{:S(2)}, u32[]{:S(2)}) collective-permute-start(f32[1,64,64]{2,1,0:T(8,128)S(1)} %get-tuple-element.82), channel_id=1, source_target_pairs={{0,1},{2,3},{4,5},{6,7},{8,9},{10,11},{12,13},{14,15},{16,17},{18,... | collective-permute-start | bytes 49160 | tf_op jit(solution)/shard_map/ppermute | solution.py:16
  91.5 37.3 %collective-permute-start.7 = (f32[1,64,64]{2,1,0:T(8,128)S(1)}, f32[1,64,64]{2,1,0:T(8,128)S(1)}, u32[]{:S(2)}, u32[]{:S(2)}) collective-permute-start(f32[1,64,64]{2,1,0:T(8,128)S(1)} %get-tuple-element.73), channel_id=1, source_target_pairs={{1,0},{3,2},{5,4},{7,6},{9,8},{11,10},{13,12},{15,14},{17,16},{19,... | collective-permute-start | bytes 49160 | tf_op jit(solution)/shard_map/ppermute | solution.py:22
  94.6 34.2 %collective-permute-start.6 = (f32[1,64,64]{2,1,0:T(8,128)S(1)}, f32[1,64,64]{2,1,0:T(8,128)S(1)}, u32[]{:S(2)}, u32[]{:S(2)}) collective-permute-start(f32[1,64,64]{2,1,0:T(8,128)S(1)} %get-tuple-element.74), channel_id=1, source_target_pairs={{0,1},{2,3},{4,5},{6,7},{8,9},{10,11},{12,13},{14,15},{16,17},{18,... | collective-permute-start | bytes 49160 | tf_op jit(solution)/shard_map/ppermute | solution.py:16
  95.9 32.9 %collective-permute-start.9 = (f32[128,1,64]{2,1,0:T(1,128)S(1)}, f32[128,1,64]{2,1,0:T(1,128)S(1)}, u32[]{:S(2)}, u32[]{:S(2)}) collective-permute-start(f32[128,1,64]{2,1,0:T(1,128)S(1)} %get-tuple-element.69), channel_id=1, source_target_pairs={{2,0},{4,2},{6,4},{3,1},{5,3},{7,5},{10,8},{12,10},{14,12},{11,9},... | collective-permute-start | bytes 98312 | tf_op jit(solution)/shard_map/ppermute | solution.py:22
  97.6 31.2 %collective-permute-start.8 = (f32[128,1,64]{2,1,0:T(1,128)S(1)}, f32[128,1,64]{2,1,0:T(1,128)S(1)}, u32[]{:S(2)}, u32[]{:S(2)}) collective-permute-start(f32[128,1,64]{2,1,0:T(1,128)S(1)} %get-tuple-element.70), channel_id=1, source_target_pairs={{0,2},{2,4},{4,6},{1,3},{3,5},{5,7},{8,10},{10,12},{12,14},{9,11},... | collective-permute-start | bytes 98312 | tf_op jit(solution)/shard_map/ppermute | solution.py:16
  106.3 18.0 %collective-permute-start.10 = (f32[128,64,1]{0,1,2:T(8,128)S(1)}, f32[128,64,1]{0,1,2:T(8,128)S(1)}, u32[]{:S(2)}, u32[]{:S(2)}) collective-permute-start(f32[128,64,1]{0,1,2:T(8,128)S(1)} %copy.2291), channel_id=1, source_target_pairs={{0,8},{8,16},{16,24},{1,9},{9,17},{17,25},{2,10},{10,18},{18,26},{... | collective-permute-start | bytes 98312 | tf_op jit(solution)/shard_map/ppermute | solution.py:16
  165.1 35.9 %collective-permute-start.13 = (f32[1,64,64]{2,1,0:T(8,128)S(1)}, f32[1,64,64]{2,1,0:T(8,128)S(1)}, u32[]{:S(2)}, u32[]{:S(2)}) collective-permute-start(f32[1,64,64]{2,1,0:T(8,128)S(1)} %get-tuple-element.61), channel_id=1, source_target_pairs={{1,0},{3,2},{5,4},{7,6},{9,8},{11,10},{13,12},{15,14},{17,16},{19,... | collective-permute-start | bytes 49160 | tf_op jit(solution)/shard_map/ppermute | solution.py:22
  168.7 32.3 %collective-permute-start.12 = (f32[1,64,64]{2,1,0:T(8,128)S(1)}, f32[1,64,64]{2,1,0:T(8,128)S(1)}, u32[]{:S(2)}, u32[]{:S(2)}) collective-permute-start(f32[1,64,64]{2,1,0:T(8,128)S(1)} %get-tuple-element.62), channel_id=1, source_target_pairs={{0,1},{2,3},{4,5},{6,7},{8,9},{10,11},{12,13},{14,15},{16,17},{18,... | collective-permute-start | bytes 49160 | tf_op jit(solution)/shard_map/ppermute | solution.py:16
  170.0 31.0 %collective-permute-start.15 = (f32[128,1,64]{2,1,0:T(1,128)S(1)}, f32[128,1,64]{2,1,0:T(1,128)S(1)}, u32[]{:S(2)}, u32[]{:S(2)}) collective-permute-start(f32[128,1,64]{2,1,0:T(1,128)S(1)} %get-tuple-element.57), channel_id=1, source_target_pairs={{2,0},{4,2},{6,4},{3,1},{5,3},{7,5},{10,8},{12,10},{14,12},{11,9},... | collective-permute-start | bytes 98312 | tf_op jit(solution)/shard_map/ppermute | solution.py:22
  171.3 29.7 %collective-permute-start.14 = (f32[128,1,64]{2,1,0:T(1,128)S(1)}, f32[128,1,64]{2,1,0:T(1,128)S(1)}, u32[]{:S(2)}, u32[]{:S(2)}) collective-permute-start(f32[128,1,64]{2,1,0:T(1,128)S(1)} %get-tuple-element.58), channel_id=1, source_target_pairs={{0,2},{2,4},{4,6},{1,3},{3,5},{5,7},{8,10},{10,12},{12,14},{9,11},... | collective-permute-start | bytes 98312 | tf_op jit(solution)/shard_map/ppermute | solution.py:16
  179.3 17.3 %collective-permute-start.16 = (f32[128,64,1]{0,1,2:T(8,128)S(1)}, f32[128,64,1]{0,1,2:T(8,128)S(1)}, u32[]{:S(2)}, u32[]{:S(2)}) collective-permute-start(f32[128,64,1]{0,1,2:T(8,128)S(1)} %copy.2296), channel_id=1, source_target_pairs={{0,8},{8,16},{16,24},{1,9},{9,17},{17,25},{2,10},{10,18},{18,26},{... | collective-permute-start | bytes 98312 | tf_op jit(solution)/shard_map/ppermute | solution.py:16
  261.5 37.9 %collective-permute-start.24 = (f32[64,1,32]{0,2,1:T(8,128)S(1)}, f32[64,1,32]{0,2,1:T(8,128)S(1)}, u32[]{:S(2)}, u32[]{:S(2)}) collective-permute-start(f32[64,1,32]{0,2,1:T(8,128)S(1)} %get-tuple-element.172), channel_id=1, source_target_pairs={{2,0},{4,2},{6,4},{3,1},{5,3},{7,5},{10,8},{12,10},{14,12},{11,9},... | collective-permute-start | bytes 24584 | tf_op jit(solution)/shard_map/ppermute | solution.py:22
  262.8 36.6 %collective-permute-start.23 = (f32[64,1,32]{0,2,1:T(8,128)S(1)}, f32[64,1,32]{0,2,1:T(8,128)S(1)}, u32[]{:S(2)}, u32[]{:S(2)}) collective-permute-start(f32[64,1,32]{0,2,1:T(8,128)S(1)} %get-tuple-element.173), channel_id=1, source_target_pairs={{0,2},{2,4},{4,6},{1,3},{3,5},{5,7},{8,10},{10,12},{12,14},{9,11},... | collective-permute-start | bytes 24584 | tf_op jit(solution)/shard_map/ppermute | solution.py:16
  266.9 32.6 %collective-permute-start.26 = (f32[64,32,1]{0,2,1:T(1,128)S(1)}, f32[64,32,1]{0,2,1:T(1,128)S(1)}, u32[]{:S(2)}, u32[]{:S(2)}) collective-permute-start(f32[64,32,1]{0,2,1:T(1,128)S(1)} %get-tuple-element.170), channel_id=1, source_target_pairs={{8,0},{16,8},{24,16},{9,1},{17,9},{25,17},{10,2},{18,10},{26,18},{... | collective-permute-start | bytes 24584 | tf_op jit(solution)/shard_map/ppermute | solution.py:22
  268.2 31.3 %collective-permute-start.25 = (f32[64,32,1]{0,2,1:T(1,128)S(1)}, f32[64,32,1]{0,2,1:T(1,128)S(1)}, u32[]{:S(2)}, u32[]{:S(2)}) collective-permute-start(f32[64,32,1]{0,2,1:T(1,128)S(1)} %get-tuple-element.171), channel_id=1, source_target_pairs={{0,8},{8,16},{16,24},{1,9},{9,17},{17,25},{2,10},{10,18},{18,26},{... | collective-permute-start | bytes 24584 | tf_op jit(solution)/shard_map/ppermute | solution.py:16
  273.3 26.1 %collective-permute-start.22 = (f32[1,32,32]{0,2,1:T(8,128)}, f32[1,32,32]{0,2,1:T(8,128)}, u32[]{:S(2)}, u32[]{:S(2)}) collective-permute-start(f32[1,32,32]{0,2,1:T(8,128)} %get-tuple-element.169), channel_id=1, source_target_pairs={{1,0},{3,2},{5,4},{7,6},{9,8},{11,10},{13,12},{15,14},{17,16},{19,... | collective-permute-start | bytes 12296 | tf_op jit(solution)/shard_map/ppermute | solution.py:22
  306.2 40.8 %collective-permute-start.29 = (f32[64,1,32]{0,2,1:T(8,128)S(1)}, f32[64,1,32]{0,2,1:T(8,128)S(1)}, u32[]{:S(2)}, u32[]{:S(2)}) collective-permute-start(f32[64,1,32]{0,2,1:T(8,128)S(1)} %get-tuple-element.163), channel_id=1, source_target_pairs={{0,2},{2,4},{4,6},{1,3},{3,5},{5,7},{8,10},{10,12},{12,14},{9,11},... | collective-permute-start | bytes 24584 | tf_op jit(solution)/shard_map/ppermute | solution.py:16
  309.5 36.2 %collective-permute-start.27 = (f32[1,32,32]{0,2,1:T(8,128)}, f32[1,32,32]{0,2,1:T(8,128)}, u32[]{:S(2)}, u32[]{:S(2)}) collective-permute-start(f32[1,32,32]{0,2,1:T(8,128)} %get-tuple-element.164), channel_id=1, source_target_pairs={{0,1},{2,3},{4,5},{6,7},{8,9},{10,11},{12,13},{14,15},{16,17},{18,... | collective-permute-start | bytes 12296 | tf_op jit(solution)/shard_map/ppermute | solution.py:16
  310.8 36.3 %collective-permute-start.28 = (f32[1,32,32]{0,2,1:T(8,128)}, f32[1,32,32]{0,2,1:T(8,128)}, u32[]{:S(2)}, u32[]{:S(2)}) collective-permute-start(f32[1,32,32]{0,2,1:T(8,128)} %get-tuple-element.165), channel_id=1, source_target_pairs={{1,0},{3,2},{5,4},{7,6},{9,8},{11,10},{13,12},{15,14},{17,16},{19,... | collective-permute-start | bytes 12296 | tf_op jit(solution)/shard_map/ppermute | solution.py:22
  318.6 31.5 %collective-permute-start.32 = (f32[64,32,1]{0,2,1:T(1,128)S(1)}, f32[64,32,1]{0,2,1:T(1,128)S(1)}, u32[]{:S(2)}, u32[]{:S(2)}) collective-permute-start(f32[64,32,1]{0,2,1:T(1,128)S(1)} %get-tuple-element.158), channel_id=1, source_target_pairs={{8,0},{16,8},{24,16},{9,1},{17,9},{25,17},{10,2},{18,10},{26,18},{... | collective-permute-start | bytes 24584 | tf_op jit(solution)/shard_map/ppermute | solution.py:22
  319.9 31.7 %collective-permute-start.31 = (f32[64,32,1]{0,2,1:T(1,128)S(1)}, f32[64,32,1]{0,2,1:T(1,128)S(1)}, u32[]{:S(2)}, u32[]{:S(2)}) collective-permute-start(f32[64,32,1]{0,2,1:T(1,128)S(1)} %get-tuple-element.159), channel_id=1, source_target_pairs={{0,8},{8,16},{16,24},{1,9},{9,17},{17,25},{2,10},{10,18},{18,26},{... | collective-permute-start | bytes 24584 | tf_op jit(solution)/shard_map/ppermute | solution.py:16
  395.3 30.3 %collective-permute-start.41 = (f32[32,16,1]{0,2,1:T(1,128)}, f32[32,16,1]{0,2,1:T(1,128)S(1)}, u32[]{:S(2)}, u32[]{:S(2)}) collective-permute-start(f32[32,16,1]{0,2,1:T(1,128)} %get-tuple-element.251), channel_id=1, source_target_pairs={{8,0},{16,8},{24,16},{9,1},{17,9},{25,17},{10,2},{18,10},{26,18},{... | collective-permute-start | bytes 6152 | tf_op jit(solution)/shard_map/ppermute | solution.py:22
  396.6 29.0 %collective-permute-start.40 = (f32[32,16,1]{0,2,1:T(1,128)}, f32[32,16,1]{0,2,1:T(1,128)S(1)}, u32[]{:S(2)}, u32[]{:S(2)}) collective-permute-start(f32[32,16,1]{0,2,1:T(1,128)} %get-tuple-element.252), channel_id=1, source_target_pairs={{0,8},{8,16},{16,24},{1,9},{9,17},{17,25},{2,10},{10,18},{18,26},{... | collective-permute-start | bytes 6152 | tf_op jit(solution)/shard_map/ppermute | solution.py:16
  400.7 24.9 %collective-permute-start.39 = (f32[32,1,16]{0,2,1:T(8,128)}, f32[32,1,16]{0,2,1:T(8,128)S(1)}, u32[]{:S(2)}, u32[]{:S(2)}) collective-permute-start(f32[32,1,16]{0,2,1:T(8,128)} %get-tuple-element.253), channel_id=1, source_target_pairs={{2,0},{4,2},{6,4},{3,1},{5,3},{7,5},{10,8},{12,10},{14,12},{11,9},... | collective-permute-start | bytes 6152 | tf_op jit(solution)/shard_map/ppermute | solution.py:22
  402.0 23.7 %collective-permute-start.38 = (f32[32,1,16]{0,2,1:T(8,128)}, f32[32,1,16]{0,2,1:T(8,128)S(1)}, u32[]{:S(2)}, u32[]{:S(2)}) collective-permute-start(f32[32,1,16]{0,2,1:T(8,128)} %get-tuple-element.254), channel_id=1, source_target_pairs={{0,2},{2,4},{4,6},{1,3},{3,5},{5,7},{8,10},{10,12},{12,14},{9,11},... | collective-permute-start | bytes 6152 | tf_op jit(solution)/shard_map/ppermute | solution.py:16
  406.7 18.9 %collective-permute-start.37 = (f32[1,16,16]{0,2,1:T(8,128)}, f32[1,16,16]{0,2,1:T(8,128)}, u32[]{:S(2)}, u32[]{:S(2)}) collective-permute-start(f32[1,16,16]{0,2,1:T(8,128)} %get-tuple-element.250), channel_id=1, source_target_pairs={{1,0},{3,2},{5,4},{7,6},{9,8},{11,10},{13,12},{15,14},{17,16},{19,... | collective-permute-start | bytes 3080 | tf_op jit(solution)/shard_map/ppermute | solution.py:22
  429.8 35.2 %collective-permute-start.44 = (f32[32,1,16]{0,2,1:T(8,128)}, f32[32,1,16]{0,2,1:T(8,128)}, u32[]{:S(2)}, u32[]{:S(2)}) collective-permute-start(f32[32,1,16]{0,2,1:T(8,128)} %get-tuple-element.244), channel_id=1, source_target_pairs={{0,2},{2,4},{4,6},{1,3},{3,5},{5,7},{8,10},{10,12},{12,14},{9,11},... | collective-permute-start | bytes 6152 | tf_op jit(solution)/shard_map/ppermute | solution.py:16
  437.9 32.6 %collective-permute-start.45 = (f32[32,1,16]{0,2,1:T(8,128)}, f32[32,1,16]{0,2,1:T(8,128)}, u32[]{:S(2)}, u32[]{:S(2)}) collective-permute-start(f32[32,1,16]{0,2,1:T(8,128)} %get-tuple-element.243), channel_id=1, source_target_pairs={{2,0},{4,2},{6,4},{3,1},{5,3},{7,5},{10,8},{12,10},{14,12},{11,9},... | collective-permute-start | bytes 6152 | tf_op jit(solution)/shard_map/ppermute | solution.py:22
  439.2 29.5 %collective-permute-start.47 = (f32[32,16,1]{0,2,1:T(1,128)}, f32[32,16,1]{0,2,1:T(1,128)}, u32[]{:S(2)}, u32[]{:S(2)}) collective-permute-start(f32[32,16,1]{0,2,1:T(1,128)} %get-tuple-element.239), channel_id=1, source_target_pairs={{8,0},{16,8},{24,16},{9,1},{17,9},{25,17},{10,2},{18,10},{26,18},{... | collective-permute-start | bytes 6152 | tf_op jit(solution)/shard_map/ppermute | solution.py:22
  442.2 17.8 %collective-permute-start.42 = (f32[1,16,16]{0,2,1:T(8,128)}, f32[1,16,16]{0,2,1:T(8,128)}, u32[]{:S(2)}, u32[]{:S(2)}) collective-permute-start(f32[1,16,16]{0,2,1:T(8,128)} %get-tuple-element.245), channel_id=1, source_target_pairs={{0,1},{2,3},{4,5},{6,7},{8,9},{10,11},{12,13},{14,15},{16,17},{18,... | collective-permute-start | bytes 3080 | tf_op jit(solution)/shard_map/ppermute | solution.py:16
  443.5 21.4 %collective-permute-start.43 = (f32[1,16,16]{0,2,1:T(8,128)}, f32[1,16,16]{0,2,1:T(8,128)}, u32[]{:S(2)}, u32[]{:S(2)}) collective-permute-start(f32[1,16,16]{0,2,1:T(8,128)} %get-tuple-element.246), channel_id=1, source_target_pairs={{1,0},{3,2},{5,4},{7,6},{9,8},{11,10},{13,12},{15,14},{17,16},{19,... | collective-permute-start | bytes 3080 | tf_op jit(solution)/shard_map/ppermute | solution.py:22
  493.0 19.3 %collective-permute-start.56 = (f32[16,8,1]{0,2,1:T(1,128)S(1)}, f32[16,8,1]{0,2,1:T(1,128)S(1)}, u32[]{:S(2)}, u32[]{:S(2)}) collective-permute-start(f32[16,8,1]{0,2,1:T(1,128)S(1)} %get-tuple-element.521), channel_id=1, source_target_pairs={{8,0},{16,8},{24,16},{9,1},{17,9},{25,17},{10,2},{18,10},{26,18},{... | collective-permute-start | bytes 1544 | tf_op jit(solution)/shard_map/ppermute | solution.py:22
  903.6 17.1 %collective-permute-start.179 = (f32[128,64,1]{0,1,2:T(8,128)S(1)}, f32[128,64,1]{0,1,2:T(8,128)S(1)}, u32[]{:S(2)}, u32[]{:S(2)}) collective-permute-start(f32[128,64,1]{0,1,2:T(8,128)S(1)} %copy.2557), channel_id=1, source_target_pairs={{8,0},{16,8},{24,16},{9,1},{17,9},{25,17},{10,2},{18,10},{26,18},{... | collective-permute-start | bytes 98312 | tf_op jit(solution)/shard_map/ppermute | solution.py:22
  905.7 36.9 %collective-permute-start.175 = (f32[1,64,64]{2,1,0:T(8,128)S(1)}, f32[1,64,64]{2,1,0:T(8,128)S(1)}, u32[]{:S(2)}, u32[]{:S(2)}) collective-permute-start(f32[1,64,64]{2,1,0:T(8,128)S(1)} %get-tuple-element.47), channel_id=1, source_target_pairs={{1,0},{3,2},{5,4},{7,6},{9,8},{11,10},{13,12},{15,14},{17,16},{19,... | collective-permute-start | bytes 49160 | tf_op jit(solution)/shard_map/ppermute | solution.py:22
  910.3 32.3 %collective-permute-start.174 = (f32[1,64,64]{2,1,0:T(8,128)S(1)}, f32[1,64,64]{2,1,0:T(8,128)S(1)}, u32[]{:S(2)}, u32[]{:S(2)}) collective-permute-start(f32[1,64,64]{2,1,0:T(8,128)S(1)} %get-tuple-element.48), channel_id=1, source_target_pairs={{0,1},{2,3},{4,5},{6,7},{8,9},{10,11},{12,13},{14,15},{16,17},{18,... | collective-permute-start | bytes 49160 | tf_op jit(solution)/shard_map/ppermute | solution.py:16
  911.6 31.0 %collective-permute-start.177 = (f32[128,1,64]{2,1,0:T(1,128)S(1)}, f32[128,1,64]{2,1,0:T(1,128)S(1)}, u32[]{:S(2)}, u32[]{:S(2)}) collective-permute-start(f32[128,1,64]{2,1,0:T(1,128)S(1)} %get-tuple-element.43), channel_id=1, source_target_pairs={{2,0},{4,2},{6,4},{3,1},{5,3},{7,5},{10,8},{12,10},{14,12},{11,9},... | collective-permute-start | bytes 98312 | tf_op jit(solution)/shard_map/ppermute | solution.py:22
  912.9 29.7 %collective-permute-start.176 = (f32[128,1,64]{2,1,0:T(1,128)S(1)}, f32[128,1,64]{2,1,0:T(1,128)S(1)}, u32[]{:S(2)}, u32[]{:S(2)}) collective-permute-start(f32[128,1,64]{2,1,0:T(1,128)S(1)} %get-tuple-element.44), channel_id=1, source_target_pairs={{0,2},{2,4},{4,6},{1,3},{3,5},{5,7},{8,10},{10,12},{12,14},{9,11},... | collective-permute-start | bytes 98312 | tf_op jit(solution)/shard_map/ppermute | solution.py:16
  920.7 17.5 %collective-permute-start.178 = (f32[128,64,1]{0,1,2:T(8,128)S(1)}, f32[128,64,1]{0,1,2:T(8,128)S(1)}, u32[]{:S(2)}, u32[]{:S(2)}) collective-permute-start(f32[128,64,1]{0,1,2:T(8,128)S(1)} %copy.2555), channel_id=1, source_target_pairs={{0,8},{8,16},{16,24},{1,9},{9,17},{17,25},{2,10},{10,18},{18,26},{... | collective-permute-start | bytes 98312 | tf_op jit(solution)/shard_map/ppermute | solution.py:16
  978.9 36.3 %collective-permute-start.181 = (f32[1,64,64]{2,1,0:T(8,128)S(1)}, f32[1,64,64]{2,1,0:T(8,128)S(1)}, u32[]{:S(2)}, u32[]{:S(2)}) collective-permute-start(f32[1,64,64]{2,1,0:T(8,128)S(1)} %get-tuple-element.35), channel_id=1, source_target_pairs={{1,0},{3,2},{5,4},{7,6},{9,8},{11,10},{13,12},{15,14},{17,16},{19,... | collective-permute-start | bytes 49160 | tf_op jit(solution)/shard_map/ppermute | solution.py:22
  982.8 32.4 %collective-permute-start.180 = (f32[1,64,64]{2,1,0:T(8,128)S(1)}, f32[1,64,64]{2,1,0:T(8,128)S(1)}, u32[]{:S(2)}, u32[]{:S(2)}) collective-permute-start(f32[1,64,64]{2,1,0:T(8,128)S(1)} %get-tuple-element.36), channel_id=1, source_target_pairs={{0,1},{2,3},{4,5},{6,7},{8,9},{10,11},{12,13},{14,15},{16,17},{18,... | collective-permute-start | bytes 49160 | tf_op jit(solution)/shard_map/ppermute | solution.py:16
  984.1 31.1 %collective-permute-start.183 = (f32[128,1,64]{2,1,0:T(1,128)S(1)}, f32[128,1,64]{2,1,0:T(1,128)S(1)}, u32[]{:S(2)}, u32[]{:S(2)}) collective-permute-start(f32[128,1,64]{2,1,0:T(1,128)S(1)} %get-tuple-element.31), channel_id=1, source_target_pairs={{2,0},{4,2},{6,4},{3,1},{5,3},{7,5},{10,8},{12,10},{14,12},{11,9},... | collective-permute-start | bytes 98312 | tf_op jit(solution)/shard_map/ppermute | solution.py:22
  985.5 29.8 %collective-permute-start.182 = (f32[128,1,64]{2,1,0:T(1,128)S(1)}, f32[128,1,64]{2,1,0:T(1,128)S(1)}, u32[]{:S(2)}, u32[]{:S(2)}) collective-permute-start(f32[128,1,64]{2,1,0:T(1,128)S(1)} %get-tuple-element.32), channel_id=1, source_target_pairs={{0,2},{2,4},{4,6},{1,3},{3,5},{5,7},{8,10},{10,12},{12,14},{9,11},... | collective-permute-start | bytes 98312 | tf_op jit(solution)/shard_map/ppermute | solution.py:16
  993.5 17.3 %collective-permute-start.184 = (f32[128,64,1]{0,1,2:T(8,128)S(1)}, f32[128,64,1]{0,1,2:T(8,128)S(1)}, u32[]{:S(2)}, u32[]{:S(2)}) collective-permute-start(f32[128,64,1]{0,1,2:T(8,128)S(1)} %copy.2560), channel_id=1, source_target_pairs={{0,8},{8,16},{16,24},{1,9},{9,17},{17,25},{2,10},{10,18},{18,26},{... | collective-permute-start | bytes 98312 | tf_op jit(solution)/shard_map/ppermute | solution.py:16
  (196 other events, 3422.4 us)
where the time goes:
time: 1050 us; the launch traced here: 1040 us
  starting transfers between devices  473 us (45%)
  local copies, waits for them, and re-layouts  362 us (34%)
  other arithmetic  145 us (14%)
  waiting for transfers between devices  53.8 us (5%)
    ppermute x93, starting transfers between devices, send_up(): lax.ppermute(plane, name, [(rank, rank + 1) for rank in range(count - 1)])  297 us
    ppermute x93, starting transfers between devices, send_down(): lax.ppermute(plane, name, [(rank + 1, rank) for rank in range(count - 1)])  176 us
    slice x27, local copies, waits for them, and re-layouts, neighbour_sum(): lax.slice_in_dim(field, 1, length, axis=axis)  101 us
    add x25, other arithmetic, jacobi_sweep(): field + residual(source, field, stiffness, counts) / (9.0 * stiffness)  74 us
    slice x101, local copies, waits for them, and re-layouts, edge_plane(): return lax.slice_in_dim(field, index, index + 1, axis=axis)  63.7 us
    ppermute x93, waiting for transfers between devices, send_up(): lax.ppermute(plane, name, [(rank, rank + 1) for rank in range(count - 1)])  35 us
    concatenate x75, local copies, waits for them, and re-layouts, neighbour_sum(): jnp.concatenate([lower, lax.slice_in_dim(field, 0, length - 1, axis=axis)...  35 us
    ppermute x23, local copies, waits for them, and re-layouts, send_up(): lax.ppermute(plane, name, [(rank, rank + 1) for rank in range(count - 1)])  30.8 us
  transfers between devices with their start and end apart: 186, of which 29 were waited for; matrix products, arithmetic and copies ran while one was open for 26% of the time, Pallas kernels for 0%

commit v1 on v0

v1 whole, which is shorter than its diff:
```python
import functools
import types
import jax
import jax.numpy as jnp
from jax import lax
from jax.experimental import pallas as pl
from jax.experimental.pallas import tpu as pltpu
from jax.sharding import PartitionSpec as P

F32 = jnp.float32
MESH = pl.DeviceIdType.MESH
HX = 8
TOP = 8
COARSE_SWEEPS = 16
CHUNK = 16
OPPOSITE = (1, 0, 3, 2, 7, 6, 5, 4)
STEP_Y = (-1, 1, 0, 0, -1, -1, 1, 1)
STEP_Z = (0, 0, -1, 1, -1, 1, -1, 1)


def make_level(nx, ny, nz, y0, rows, wide):
    lv = types.SimpleNamespace(nx=nx, ny=ny, nz=nz, y0=y0, rows=rows, wide=wide)
    lv.depth = rows + 16
    lv.planes = nx + 2 * HX
    lv.packs = 128 // nz
    lv.groups = nx // 16
    lv.own = pl.ds(y0, ny)
    lv.all = pl.ds(TOP, rows)
    return lv


def lanes_of(shape):
    return lax.broadcasted_iota(jnp.int32, shape, 1)


def rows_of(shape):
    return lax.broadcasted_iota(jnp.int32, shape, 0)


def roll(x, shift, axis=1):
    return pltpu.roll(x, shift, axis)


def signed(lane):
    return jnp.where(lane < 96, lane, lane - 128)


def kernel(cfg, rhs, start, out, *scratch):
    (stage_u, stage_f, u0, v0, f0, a1, b1, p1, a2, b2, p2, e3, pz, pb, s3, p3, slots, message,
     sy0, sz0, sd0, ry0, rz0, rd0, sy1, sz1, sd1, ry1, rz1, rd1, sy2, sz2, sd2, ry2, rz2, rd2,
     load_sem, out_sem, send_sem, recv_sem, xs_sem, xr_sem, gs_sem, gr_sem) = scratch
    l0, l1, l2 = cfg.levels
    n_x, n_y, n_z = cfg.counts
    cx, cy, cz = lax.axis_index('sx'), lax.axis_index('sy'), lax.axis_index('sz')
    total = n_x * n_y * n_z
    rank = (cz * n_y + cy) * n_x + cx
    turn = cy * n_z + cz

    def load(c, which):
        src, dst = ((start, stage_u), (rhs, stage_f))[which]
        return pltpu.make_async_copy(src.at[pl.ds(c * CHUNK, CHUNK)], dst.at[pl.ds(c * CHUNK, CHUNK)], load_sem.at[which, c])

    n_chunks = l0.nx // CHUNK
    for c in range(n_chunks):
        load(c, 0).start()
        load(c, 1).start()

    def peer(p):
        r = lax.rem(rank + p, total)
        return {'sz': r // (n_x * n_y), 'sy': (r // n_x) % n_y, 'sx': r % n_x}

    barrier = pltpu.get_barrier_semaphore()

    @pl.loop(1, total)
    def _(p):
        pl.semaphore_signal(barrier, inc=1, device_id=peer(p), device_id_type=MESH)

    comm = ((l0, (sy0, sz0, sd0), (ry0, rz0, rd0)), (l1, (sy1, sz1, sd1), (ry1, rz1, rd1)), (l2, (sy2, sz2, sd2), (ry2, rz2, rd2)))

    def exists(d):
        ok = None
        for step, at, count in ((STEP_Y[d], cy, n_y), (STEP_Z[d], cz, n_z)):
            if step:
                one = (at > 0) if step < 0 else (at < count - 1)
                ok = one if ok is None else jnp.logical_and(ok, one)
        return ok

    def buffer(bufs, d):
        return bufs[0].at[d] if d < 2 else bufs[1].at[d - 2] if d < 4 else bufs[2].at[d - 4]

    for lv, _, recv in comm:
        for d in range(8):
            @pl.when(jnp.logical_not(exists(d)))
            def _(recv=recv, d=d):
                buf = buffer(recv, d)

                @pl.loop(0, buf.shape[0])
                def _(i):
                    buf[i] = jnp.zeros(buf.shape[1:], F32)

    for lv, arrays in ((l0, (u0, v0)), (l1, (a1, b1)), (l2, (a2, b2))):
        zero = jnp.zeros((8, 128), F32)
        for arr in arrays:
            @pl.loop(0, lv.planes)
            def _(x, arr=arr, lv=lv):
                arr[x, pl.ds(0, 8)] = zero
                arr[x, pl.ds(TOP + lv.rows, 8)] = zero

            @pl.when(cx == 0)
            def _(arr=arr, lv=lv):
                arr[HX - 1, lv.all] = jnp.zeros((lv.rows, 128), F32)

            @pl.when(cx == n_x - 1)
            def _(arr=arr, lv=lv):
                arr[HX + lv.nx, lv.all] = jnp.zeros((lv.rows, 128), F32)

    pl.semaphore_wait(barrier, total - 1)

    def domain(lv):
        shape = (lv.rows, 128)
        y = rows_of(shape) + (TOP - lv.y0) + cy * lv.ny
        k = signed(lanes_of(shape))
        z = k + cz * lv.nz
        ok = (y >= 0) & (y < n_y * lv.ny) & (z >= 0) & (z < n_z * lv.nz) & (k >= -8) & (k < lv.nz + 8)
        return jnp.where(ok, 1.0, 0.0).astype(F32)

    def first_plane(lv, wide):
        return HX - cx * wide

    def start_send(lv_index, d):
        _, send, recv = comm[lv_index]

        @pl.when(exists(d))
        def _():
            halo_copy(lv_index, d).start()

    def halo_copy(lv_index, d):
        _, send, recv = comm[lv_index]
        return pltpu.make_async_remote_copy(
            src_ref=buffer(send, d), dst_ref=buffer(recv, OPPOSITE[d]),
            send_sem=send_sem.at[lv_index, d], recv_sem=recv_sem.at[lv_index, OPPOSITE[d]],
            device_id={'sy': cy + STEP_Y[d], 'sz': cz + STEP_Z[d]}, device_id_type=MESH)

    def arrival(lv_index, d):
        _, send, recv = comm[lv_index]
        return pltpu.make_async_remote_copy(
            src_ref=buffer(send, d), dst_ref=buffer(recv, d),
            send_sem=send_sem.at[lv_index, d], recv_sem=recv_sem.at[lv_index, d],
            device_id={'sy': cy + STEP_Y[d], 'sz': cz + STEP_Z[d]}, device_id_type=MESH)

    def wait_recv(lv_index, d):
        @pl.when(exists(d))
        def _():
            arrival(lv_index, d).wait_recv()

    def wait_send(lv_index, d):
        @pl.when(exists(d))
        def _():
            halo_copy(lv_index, d).wait_send()

    def faces(lv_index, x):
        lv = comm[lv_index][0]
        if lv_index == 0:
            upper = rows_of((8, 128)) >= 4
            lo = jnp.where(upper, f0[HX + x, pl.ds(lv.y0 - 4, 8)], u0[HX + x, pl.ds(lv.y0, 8)])
            hi = jnp.where(upper, f0[HX + x, pl.ds(lv.y0 + lv.ny - 8, 8)], u0[HX + x, pl.ds(lv.y0 + lv.ny - 4, 8)])
            return lo, hi
        phi = (p1, p2)[lv_index - 1]
        return phi[HX + x, pl.ds(lv.y0, 8)], phi[HX + x, pl.ds(lv.y0 + lv.ny - 8, 8)]

    def pack_rows(lv_index):
        lv, send, _ = comm[lv_index]
        per = lv.nx // lv.packs
        lane = lanes_of((8, 128)) // lv.nz

        @pl.loop(0, per)
        def _(j):
            lo, hi = faces(lv_index, j)
            for q in range(1, lv.packs):
                more = faces(lv_index, j + q * per)
                lo = jnp.where(lane == q, roll(more[0], q * lv.nz), lo)
                hi = jnp.where(lane == q, roll(more[1], q * lv.nz), hi)
            send[0][0, j] = lo
            send[0][1, j] = hi

    def pack_corners(lv_index):
        lv, send, _ = comm[lv_index]
        lane = lanes_of((8, 128)) // 8

        @pl.loop(0, lv.groups)
        def _(g):
            def body(i, acc):
                lo, hi = faces(lv_index, g * 16 + i)
                here = lane == i
                up, down = 8 * i, (8 * i + 128 - (lv.nz - 8)) % 128
                return (jnp.where(here, roll(lo, up), acc[0]), jnp.where(here, roll(lo, down), acc[1]),
                        jnp.where(here, roll(hi, up), acc[2]), jnp.where(here, roll(hi, down), acc[3]))
            acc = lax.fori_loop(0, 16, body, (jnp.zeros((8, 128), F32),) * 4)
            for d in range(4):
                send[2][d, g] = acc[d]

    def pack_lanes(lv_index):
        lv, send, _ = comm[lv_index]
        phi = (p1, p2)[lv_index - 1]
        lane = lanes_of((lv.ny, 128)) // 8

        @pl.loop(0, lv.groups)
        def _(g):
            def body(i, acc):
                t = phi[HX + g * 16 + i, lv.own]
                here = lane == i
                return (jnp.where(here, roll(t, 8 * i), acc[0]),
                        jnp.where(here, roll(t, (8 * i + 128 - (lv.nz - 8)) % 128), acc[1]))
            acc = lax.fori_loop(0, 16, body, (jnp.zeros((lv.ny, 128), F32),) * 2)
            send[1][0, g] = acc[0]
            send[1][1, g] = acc[1]

    def unpack_rows(lv_index):
        lv, _, recv = comm[lv_index]
        per = lv.nx // lv.packs
        lane = lanes_of((8, 128))
        below, above = lane >= 120, (lane >= lv.nz) & (lane < lv.nz + 8)
        inside = lane < lv.nz

        @pl.loop(0, per)
        def _(j):
            for side in range(2):
                tile = recv[0][side, j]
                for q in range(lv.packs):
                    x = j + q * per
                    g, i = x // 16, x % 16
                    t = roll(tile, (128 - q * lv.nz) % 128) if q else tile
                    t = jnp.where(inside, t, 0.0)
                    t = jnp.where(below, roll(recv[2][2 * side, g], (120 + 128 - 8 * i) % 128), t)
                    t = jnp.where(above, roll(recv[2][2 * side + 1, g], (lv.nz + 128 - 8 * i) % 128), t)
                    if lv_index == 0:
                        row = lv.y0 + lv.ny if side else lv.y0 - 4
                        u0[HX + x, pl.ds(row, 4)] = t[:4]
                        f0[HX + x, pl.ds(row, 4)] = t[4:]
                    else:
                        row = lv.y0 + lv.ny if side else lv.y0 - 8
                        (p1, p2)[lv_index - 1][HX + x, pl.ds(row, 8)] = t

    def unpack_lanes(lv_index):
        lv, _, recv = comm[lv_index]
        lane = lanes_of((lv.ny, 128))
        if lv_index == 0:
            below, above = lane >= 124, (lane >= lv.nz) & (lane < lv.nz + 4)
            targets = ((u0, 124, lv.nz), (f0, 120, lv.nz - 4))
        else:
            below, above = lane >= 120, (lane >= lv.nz) & (lane < lv.nz + 8)
            targets = (((p1, p2)[lv_index - 1], 120, lv.nz),)

        @pl.loop(0, lv.groups)
        def _(g):
            lo, hi = recv[1][0, g], recv[1][1, g]

            @pl.loop(0, 16)
            def _(i):
                x = HX + g * 16 + i
                for arr, at_lo, at_hi in targets:
                    t = arr[x, lv.own]
                    t = jnp.where(below, roll(lo, (at_lo + 128 - 8 * i) % 128), t)
                    t = jnp.where(above, roll(hi, (at_hi + 128 - 8 * i) % 128), t)
                    arr[x, lv.own] = t

    def partner_copy(k, arr, lv, wide, up):
        src, dst = (HX + lv.nx - wide, HX - wide) if up else (HX, HX + lv.nx)
        return pltpu.make_async_remote_copy(
            src_ref=arr.at[pl.ds(src, wide), lv.all], dst_ref=arr.at[pl.ds(dst, wide), lv.all],
            send_sem=xs_sem.at[k], recv_sem=xr_sem.at[k],
            device_id={'sx': cx + 1 if up else cx - 1}, device_id_type=MESH)

    def partner_arrival(k, arr, lv, wide, up):
        planes = arr.at[pl.ds(HX + lv.nx if up else HX - wide, wide), lv.all]
        return pltpu.make_async_remote_copy(
            src_ref=planes, dst_ref=planes, send_sem=xs_sem.at[k], recv_sem=xr_sem.at[k],
            device_id={'sx': cx + 1 if up else cx - 1}, device_id_type=MESH)

    def partner_exchange(first, arrays, lv, wide):
        for up, here in ((True, cx < n_x - 1), (False, cx > 0)):
            @pl.when(here)
            def _(up=up):
                for k, arr in enumerate(arrays):
                    partner_copy(first + k, arr, lv, wide, up).start()
        for up, here in ((True, cx < n_x - 1), (False, cx > 0)):
            @pl.when(here)
            def _(up=up):
                for k, arr in enumerate(arrays):
                    partner_copy(first + k, arr, lv, wide, up).wait_send()
                    partner_arrival(first + k, arr, lv, wide, up).wait_recv()

    def exchange(lv_index, arrays, first, wide):
        for d in range(4, 8):
            start_send(lv_index, d)
        for d in range(4):
            start_send(lv_index, d)
        for d in range(8):
            wait_recv(lv_index, d)
        unpack_rows(lv_index)
        unpack_lanes(lv_index)
        partner_exchange(first, arrays, comm[lv_index][0], wide)
        for d in range(8):
            wait_send(lv_index, d)

    def neighbours(xm, c, xp, src, x, row, n):
        around = (xm + xp) + (src[x, pl.ds(row - 1, n)] + src[x, pl.ds(row + 1, n)])
        return around + (roll(c, 1) + roll(c, 127))

    def sweep(src, dst, phi, lv, wide, coef):
        begin = first_plane(lv, wide)

        def one(x, xm, c):
            xp = src[x + 1, lv.all]
            t = neighbours(xm, c, xp, src, x, TOP, lv.rows) + 3.0 * c + phi[x, lv.all]
            dst[x, lv.all] = t * coef
            return c, xp

        def body(i, carry):
            x = begin + 2 * i
            return one(x + 1, *one(x, *carry))
        lax.fori_loop(0, (lv.nx + wide) // 2, body, (src[begin - 1, lv.all], src[begin, lv.all]))

    def first_sweep(dst, phi, lv, wide, coef):
        begin = first_plane(lv, wide)

        @pl.loop(0, lv.nx + wide)
        def _(i):
            dst[begin + i, lv.all] = phi[begin + i, lv.all] * coef

    def last_sweep(src, phi, lv):
        shape = (lv.ny, 128)

        def copy_out(c):
            return pltpu.make_async_copy(stage_u.at[pl.ds(c * CHUNK, CHUNK)], out.at[pl.ds(c * CHUNK, CHUNK)], out_sem.at[c])

        def one(x, xm, c):
            xp = src[HX + x + 1, lv.own]
            t = neighbours(xm, c, xp, src, HX + x, lv.y0, lv.ny) + 3.0 * c + phi[HX + x, lv.own]
            stage_u[x] = (t * (1.0 / 9.0))[:, :lv.nz]
            return c, xp

        carry = (src[HX - 1, lv.own], src[HX, lv.own])
        for c in range(n_chunks):
            def body(i, carry, c=c):
                x = c * CHUNK + 2 * i
                return one(x + 1, *one(x, *carry))
            carry = lax.fori_loop(0, CHUNK // 2, body, carry)
            copy_out(c).start()
        for c in range(n_chunks):
            copy_out(c).wait()

    def restrict_planes(src, phi, lv, mask):
        def res(x, xm, c, xp):
            return neighbours(xm, c, xp, src, x, TOP, lv.rows) + phi[x, lv.all] - 6.0 * c

        def plane(x):
            return src[x, lv.all]
        pm2, pm1, pc = plane(HX - 2), plane(HX - 1), plane(HX)
        before = res(HX - 1, pm2, pm1, pc) * jnp.where(cx > 0, 1.0, 0.0).astype(F32)
        before = jnp.where(cx > 0, before, jnp.zeros_like(before))

        def body(i, carry):
            prev, xm, c = carry
            x = HX + 2 * i
            x1, x2 = plane(x + 1), plane(x + 2)
            even = res(x, xm, c, x1)
            odd = res(x + 1, c, x1, x2)
            pb[i, lv.all] = ((prev + odd) + (even + even)) * mask
            return odd, x1, x2
        lax.fori_loop(0, lv.nx // 2, body, (before, pm1, pc))

    def restricted_rows(i, lv):
        half = lv.ny // 2
        return ((pb[i, pl.ds(lv.y0 - 1, half, stride=2)] + pb[i, pl.ds(lv.y0 + 1, half, stride=2)])
                + 2.0 * pb[i, pl.ds(lv.y0, half, stride=2)])

    def restrict_weights(outside):
        fine = signed(rows_of((128, 128)))
        lane = lanes_of((128, 128))
        coarse = lane % 8 if outside is None else lane
        near = fine - 2 * coarse
        w = jnp.where(near == 0, 2.0, jnp.where((near == 1) | (near == -1), 1.0, 0.0)) * (1.0 / 16.0)
        if outside is not None:
            w = jnp.where(lane < outside, w, 0.0)
        return w.astype(F32)

    def dot(x, w):
        return jnp.dot(x, w, precision=lax.Precision.HIGHEST, preferred_element_type=F32)

    def restrict_level(src, phi, lv, mask, coarse_phi, coarse):
        restrict_planes(src, phi, lv, mask)
        w = restrict_weights(coarse.nz)
        step = 8

        @pl.loop(0, coarse.nx // step)
        def _(c):
            q = jnp.concatenate([restricted_rows(c * step + k, lv) for k in range(step)], axis=0)
            got = dot(q, w)
            for k in range(step):
                coarse_phi[HX + c * step + k, coarse.own] = got[k * coarse.ny:(k + 1) * coarse.ny]

    def prolong_level(e, e_hx, e_y0, e_rows, n_coarse, chunk, dst, lv, wide, mask):
        half = wide // 2
        begin = e_hx - cx * half
        near = signed(lanes_of((128, 128))) - 2 * signed(rows_of((128, 128)))
        w = jnp.where(near == 0, 1.0, jnp.where((near == 1) | (near == -1), 0.5, 0.0)).astype(F32)
        count = n_coarse + half + 1

        @pl.loop(0, count // chunk)
        def _(c):
            at = begin + c * chunk
            got = dot(e[pl.ds(at, chunk), pl.ds(8, e_rows)].reshape(chunk * e_rows, 128), w)
            pz[pl.ds(at, chunk), pl.ds(8, e_rows)] = got.reshape(chunk, e_rows, 128)
        row = e_y0 - (lv.y0 - TOP) // 2
        n = lv.rows // 2

        @pl.loop(0, count)
        def _(i):
            x = begin + i
            a = pz[x, pl.ds(row, n)]
            b = pz[x, pl.ds(row + 1, n)]
            pb[i, pl.ds(TOP, n, stride=2)] = a
            pb[i, pl.ds(TOP + 1, n, stride=2)] = 0.5 * (a + b)
        fine = first_plane(lv, wide)

        def body(i, a):
            b = pb[i + 1, lv.all]
            x = fine + 2 * i
            dst[x, lv.all] = (dst[x, lv.all] + a) * mask
            dst[x + 1, lv.all] = (dst[x + 1, lv.all] + 0.5 * (a + b)) * mask
            return b
        lax.fori_loop(0, n_coarse + half, body, pb[0, lv.all])

    lane0 = lanes_of((l0.ny, 128)) // 4
    pad = jnp.zeros((l0.ny, 128 - l0.nz), F32)

    @pl.loop(0, l0.groups)
    def _(g):
        load(g, 0).wait()
        load(g, 1).wait()

        def body(i, acc):
            lo, hi = acc
            x = g * 16 + i
            u = jnp.concatenate([stage_u[x], pad], axis=1)
            f = jnp.concatenate([stage_f[x], pad], axis=1) * cfg.scale
            u0[HX + x, l0.own] = u
            f0[HX + x, l0.own] = f
            at_u, at_f = lane0 == 2 * i, lane0 == 2 * i + 1
            lo = jnp.where(at_u, roll(u, 8 * i), jnp.where(at_f, roll(f, 8 * i + 4), lo))
            hi = jnp.where(at_u, roll(u, (8 * i + 128 - (l0.nz - 4)) % 128),
                           jnp.where(at_f, roll(f, (8 * i + 4 + 128 - (l0.nz - 4)) % 128), hi))
            return lo, hi
        lo, hi = lax.fori_loop(0, 16, body, (jnp.zeros((l0.ny, 128), F32),) * 2)
        sz0[0, g] = lo
        sz0[1, g] = hi
    pack_rows(0)
    pack_corners(0)
    exchange(0, (u0, f0), 0, 4)

    mask0 = domain(l0)
    sweep(u0, v0, f0, l0, 4, mask0 * (1.0 / 9.0))
    sweep(v0, u0, f0, l0, 2, mask0 * (1.0 / 9.0))
    restrict_level(u0, f0, l0, mask0, p1, l1)

    pack_rows(1)
    pack_lanes(1)
    pack_corners(1)
    exchange(1, (p1,), 2, 5)
    mask1 = domain(l1)
    first_sweep(a1, p1, l1, 6, mask1 * (1.0 / 9.0))
    sweep(a1, b1, p1, l1, 4, mask1 * (1.0 / 9.0))
    restrict_level(b1, p1, l1, mask1, p2, l2)

    pack_rows(2)
    pack_lanes(2)
    pack_corners(2)
    exchange(2, (p2,), 3, 6)
    mask2 = domain(l2)
    first_sweep(a2, p2, l2, 8, mask2 * (1.0 / 9.0))
    sweep(a2, b2, p2, l2, 6, mask2 * (1.0 / 9.0))

    restrict_planes(b2, p2, l2, mask2)
    nx3, ny3, nz3 = l2.nx // 2, l2.ny // 2, l2.nz // 2
    q = jnp.concatenate([restricted_rows(k, l2) for k in range(nx3)], axis=0)
    got = dot(q, restrict_weights(None))
    lane = lanes_of((8, 128))
    block = lane // 8
    packed = jnp.zeros((8, 128), F32)
    for k in range(nx3):
        packed = jnp.where(block == k, got[k * ny3:(k + 1) * ny3], packed)
    packed = roll(packed, 8 * turn)
    message[...] = packed
    slot = cx * (n_y * n_z) + turn
    slots[slot] = packed

    def gather_copy(p):
        return pltpu.make_async_remote_copy(
            src_ref=message, dst_ref=slots.at[slot], send_sem=gs_sem.at[p], recv_sem=gr_sem.at[slot],
            device_id=peer(p), device_id_type=MESH)

    @pl.loop(1, total)
    def _(p):
        gather_copy(p).start()

    @pl.loop(1, total)
    def _(p):
        who = peer(p)
        theirs = who['sx'] * (n_y * n_z) + who['sy'] * n_z + who['sz']
        pltpu.make_async_remote_copy(
            src_ref=message, dst_ref=slots.at[theirs], send_sem=gs_sem.at[p], recv_sem=gr_sem.at[theirs],
            device_id=who, device_id_type=MESH).wait_recv()

    span = nz3 * n_z
    turns = n_y * n_z
    whole = n_x * nx3
    for s in range(2):
        @pl.loop(0, 8)
        def _(i, s=s):
            s3[s, i] = jnp.zeros((8, 128), F32)
            s3[s, 8 + whole + i] = jnp.zeros((8, 128), F32)

    live = lane < 8 * turns

    @pl.loop(0, n_x)
    def _(half):
        @pl.loop(0, nx3)
        def _(k):
            which = (block + 128 - k) % 16
            acc = jnp.zeros((8, 128), F32)
            for t in range(turns):
                acc = jnp.where((block + (16 - t)) % 16 == k, slots[half * turns + t], acc)
            acc = jnp.where(live, roll(acc, (128 - 8 * k) % 128), 0.0)
            p3[half * nx3 + k] = acc
            s3[0, 8 + half * nx3 + k] = acc * (1.0 / 9.0)

    sub = rows_of((8, 128))
    z_first, z_last = lane % span == 0, lane % span == span - 1
    top_row, end_row = sub == 0, sub == 7
    y_first, y_last = top_row & (lane < span), end_row & (lane >= span * (n_y - 1))

    def coarse_sweep(k, carry):
        old, new = k % 2, (k + 1) % 2
        xm, c = s3[old, 7], s3[old, 8]
        for x in range(whole):
            xp = s3[old, 9 + x]
            down, up = roll(c, 1, 0), roll(c, 7, 0)
            ym = jnp.where(y_first, 0.0, jnp.where(top_row, roll(down, span % 128), down))
            yp = jnp.where(y_last, 0.0, jnp.where(end_row, roll(up, (128 - span) % 128), up))
            zm = jnp.where(z_first, 0.0, roll(c, 1))
            zp = jnp.where(z_last, 0.0, roll(c, 127))
            t = (xm + xp) + (ym + yp) + (zm + zp) + 3.0 * c + p3[x]
            s3[new, 8 + x] = t * (1.0 / 9.0)
            xm, c = c, xp
        return carry
    lax.fori_loop(0, COARSE_SWEEPS - 1, coarse_sweep, 0)
    last = (COARSE_SWEEPS - 1) % 2

    gz = signed(lane) + cz * nz3
    z_ok = (gz >= 0) & (gz < span) & (signed(lane) >= -8) & (signed(lane) < nz3 + 8)

    @pl.loop(0, nx3 + 8)
    def _(i):
        c = s3[last, cx * nx3 + i + 4]
        for k in range(3):
            t = roll(c, (256 - 8 * turn - (k - 1) * span) % 128)
            ok = z_ok
            if k == 0:
                ok = ok & (cy > 0)
            if k == 2:
                ok = ok & (cy < n_y - 1)
            e3[i, pl.ds(8 + 8 * k, 8)] = jnp.where(ok, t, 0.0)

    prolong_level(e3, 4, 16, 24, nx3, 5, b2, l2, 6, mask2)
    sweep(b2, a2, p2, l2, 4, mask2 * (1.0 / 9.0))
    sweep(a2, b2, p2, l2, 4, mask2 * (1.0 / 9.0))
    prolong_level(b2, HX, l2.y0, l2.rows, l2.nx, 7, b1, l1, 4, mask1)
    sweep(b1, a1, p1, l1, 4, mask1 * (1.0 / 9.0))
    sweep(a1, b1, p1, l1, 2, mask1 * (1.0 / 9.0))
    prolong_level(b1, HX, l1.y0, l1.rows, l1.nx, 6, u0, l0, 2, mask0)
    sweep(u0, v0, f0, l0, 2, mask0 * (1.0 / 9.0))
    last_sweep(v0, f0, l0)

    @pl.loop(1, total)
    def _(p):
        gather_copy(p).wait_send()


def local_cycle(rhs, start, counts, size):
    nx, ny, nz = rhs.shape
    levels = (make_level(nx, ny, nz, 12, ny + 8, 4), make_level(nx // 2, ny // 2, nz // 2, 16, ny // 2 + 16, 5),
              make_level(nx // 4, ny // 4, nz // 4, 16, ny // 4 + 16, 6))
    l0, l1, l2 = levels
    cfg = types.SimpleNamespace(levels=levels, counts=counts, scale=1.0 / (size + 1) ** 2)
    total = counts[0] * counts[1] * counts[2]

    def vmem(*shape):
        return pltpu.VMEM(shape, F32)

    def ext(lv):
        return vmem(lv.planes, lv.depth, 128)

    def messages(lv):
        return [vmem(2, lv.nx // lv.packs, 8, 128), vmem(2, lv.groups, lv.ny, 128), vmem(4, lv.groups, 8, 128)] * 2

    whole = counts[0] * (l2.nx // 2)
    scratch = [vmem(nx, ny, nz), vmem(nx, ny, nz), ext(l0), ext(l0), ext(l0), ext(l1), ext(l1), ext(l1), ext(l2), ext(l2), ext(l2),
               vmem(l2.nx // 2 + 8, 40, 128), vmem(l1.planes, l1.depth, 128), vmem(l1.planes, l0.depth, 128),
               vmem(2, whole + 16, 8, 128), vmem(whole, 8, 128), vmem(total, 8, 128), vmem(8, 128)]
    scratch += messages(l0) + messages(l1) + messages(l2)
    dma = pltpu.SemaphoreType.DMA
    scratch += [dma((2, nx // CHUNK)), dma((nx // CHUNK,)), dma((3, 8)), dma((3, 8)), dma((4,)), dma((4,)), dma((total,)), dma((total,))]
    return pl.pallas_call(
        functools.partial(kernel, cfg),
        out_shape=jax.ShapeDtypeStruct(rhs.shape, F32),
        in_specs=[pl.BlockSpec(memory_space=pl.ANY)] * 2,
        out_specs=pl.BlockSpec(memory_space=pl.ANY),
        scratch_shapes=scratch,
        compiler_params=pltpu.CompilerParams(collective_id=0, has_side_effects=True, vmem_limit_bytes=62 << 20),
    )(rhs, start)


def solution(mesh):
    counts = (mesh.shape['sx'], mesh.shape['sy'], mesh.shape['sz'])
    spec = P(('dp', 'sx'), 'sy', 'sz')

    def run(rhs_grid, u_start):
        size = rhs_grid.shape[0] // mesh.shape['dp']
        cycle = functools.partial(local_cycle, counts=counts, size=size)
        return jax.shard_map(cycle, mesh=mesh, in_specs=(spec, spec), out_specs=spec, check_vma=False)(rhs_grid, u_start)
    return run
```

time: 1050 us -> 198 us (0.19); the launches traced: 1040 us -> 198 us
  starting transfers between devices: 473 us -> 0 us
  local copies, waits for them, and re-layouts: 362 us -> 15 us
  Pallas kernels: 0 us -> 183 us
  other arithmetic: 145 us -> 0 us
  waiting for transfers between devices: 53.8 us -> 0 us
    ppermute x186 -> x0, starting transfers between devices: 473 us -> none  [the longest x93 297 us: send_up(): lax.ppermute(plane, name, [(rank, rank + 1) for rank in range(count - 1)])]
    slice x151 -> x0, local copies, waits for them, and re-layouts: 188 us -> none  [the longest x27 101 us: neighbour_sum(): lax.slice_in_dim(field, 1, length, axis=axis)]
    pallas_call x0 -> x1, Pallas kernels: none -> 183 us  [local_cycle(): pl.pallas_call(functools.partial(kernel, cfg), out_shape=jax.ShapeDtypeSt...]
    add x42 -> x0, other arithmetic: 95.1 us -> none  [the longest x25 74 us: jacobi_sweep(): field + residual(source, field, stiffness, counts) / (9.0 * stiffness)]
    concatenate x113 -> x0, local copies, waits for them, and re-layouts: 71 us -> none  [the longest x75 35 us: neighbour_sum(): jnp.concatenate([lower, lax.slice_in_dim(field, 0, length - 1, axis=axis)...]
    ppermute x36 -> x0, local copies, waits for them, and re-layouts: 56.1 us -> none  [the longest x23 30.8 us: send_up(): lax.ppermute(plane, name, [(rank, rank + 1) for rank in range(count - 1)])]
    ppermute x186 -> x0, waiting for transfers between devices: 53.8 us -> none  [the longest x93 35 us: send_up(): lax.ppermute(plane, name, [(rank, rank + 1) for rank in range(count - 1)])]
    sub x5 -> x0, other arithmetic: 30.6 us -> none  [residual(): return source - stiffness * (6.0 * field - neighbour_sum(field, counts))]
  transfers between devices with their start and end apart: 186 -> 0, of which waited for: 29 -> 0; matrix products, arithmetic and copies ran while one was open for 26% -> 0% of each run, Pallas kernels for 0% -> 0%
where the time goes in v1:
time: 198 us
  Pallas kernels  183 us (92%)
  local copies, waits for them, and re-layouts  15 us (8%)
    pallas_call x1, Pallas kernels, local_cycle(): pl.pallas_call(functools.partial(kernel, cfg), out_shape=jax.ShapeDtypeSt...  183 us
    unnamed x4, local copies, waits for them, and re-layouts  10.2 us
    pallas_call x1, local copies, waits for them, and re-layouts, local_cycle(): pl.pallas_call(functools.partial(kernel, cfg), out_shape=jax.ShapeDtypeSt...  4.77 us

profile of v1, /device:TPU:97, one launch (start us, length us, event | category | flops | bytes accessed | tf_op | source)
XLA Modules:
  0.0 198.0 jit_solution(2244134722360689707)
XLA Ops:
  0.0 0.0 copy-start
  0.0 5.7 %copy.3.rhs = f32[128,64,64]{2,1,0:T(8,128)} copy(f32[128,64,64]{0,2,1:T(8,128)} %param.2) | data formatting | bytes 4194304 | tf_op args[0]
  5.7 0.0 copy-done
  5.7 4.5 %copy.4.start = f32[128,64,64]{2,1,0:T(8,128)} copy(f32[128,64,64]{0,2,1:T(8,128)S(1)} %copy-done) | data formatting | bytes 4194304 | tf_op args[1]
  10.2 183.0 %shard_map.28 = f32[128,64,64]{2,1,0:T(8,128)} custom-call(f32[128,64,64]{2,1,0:T(8,128)} %copy.3.rhs, f32[128,64,64]{2,1,0:T(8,128)} %copy.4.start), custom_call_target="tpu_custom_call" | custom-call | tf_op jit(solution)/shard_map/pallas_call | solution.py:614
  193.2 4.8 %copy.5 = f32[128,64,64]{0,2,1:T(8,128)} copy(f32[128,64,64]{2,1,0:T(8,128)} %shard_map.28) | data formatting | bytes 4194304 | tf_op jit(solution)/shard_map/pallas_call | solution.py:614
Async XLA Ops:
  0.0 5.7 %copy-start = (f32[128,64,64]{0,2,1:T(8,128)S(1)}, f32[128,64,64]{0,2,1:T(8,128)}, u32[]{:S(2)}) copy-start(f32[128,64,64]{0,2,1:T(8,128)} %param.3) | copy-start | bytes 6291460

commit v2 on v0

v2 whole, which is shorter than its diff:
```python
import functools
import types
import jax
import jax.numpy as jnp
from jax import lax
from jax.experimental import pallas as pl
from jax.experimental.pallas import tpu as pltpu
from jax.sharding import PartitionSpec as P

F32 = jnp.float32
MESH = pl.DeviceIdType.MESH
LANES = 128
TILE = 8
NINTH = 1.0 / 9.0
COARSE_SWEEPS = 16
OPPOSITE = (1, 0, 3, 2, 7, 6, 5, 4)
STEP_Y = (-1, 1, 0, 0, -1, -1, 1, 1)
STEP_Z = (0, 0, -1, 1, -1, 1, -1, 1)
SIDES = range(len(STEP_Y))


def make_level(shape, hx, z0, top, rows, begin, group, count, wide, block):
    ny, nz, nx = shape
    lv = types.SimpleNamespace(ny=ny, nz=nz, nx=nx, hx=hx, z0=z0, top=top, rows=rows, begin=begin, group=group, count=count, wide=wide)
    lv.planes = ny + 2 * hx
    lv.depth = nz + 2 * z0
    lv.parts = max(nx // LANES, 1)
    lv.own = pl.ds(z0, nz)
    lv.all = pl.ds(top, rows)
    lv.blocks = [(top + i, min(block, rows - i)) for i in range(0, rows, block)]
    return lv


def lanes_of(shape):
    return lax.broadcasted_iota(jnp.int32, shape, len(shape) - 1)


def rows_of(shape):
    return lax.broadcasted_iota(jnp.int32, shape, len(shape) - 2)


def roll(x, shift):
    return pltpu.roll(x, shift, 1)


def from_below(x):
    return jnp.where(lanes_of(x.shape) == 0, 0.0, roll(x, 1))


def from_above(x):
    return jnp.where(lanes_of(x.shape) == LANES - 1, 0.0, roll(x, LANES - 1))


def halves(x):
    return x[:, :LANES], x[:, LANES:]


def get(ref, p, rows, lv):
    return [ref[p, h, rows] for h in range(lv.parts)]


def put(ref, p, rows, values):
    for h, value in enumerate(values):
        ref[p, h, rows] = value


def every(f, *lists):
    return [f(*values) for values in zip(*lists)]


def join(*parts):
    return jnp.concatenate(parts, axis=1)


def stack(parts):
    return jnp.concatenate(parts, axis=0)


def back(shift):
    return (4 * LANES - shift) % LANES


def flag(condition):
    return jnp.where(condition, 1, 0)


def dot(x, w):
    return jnp.dot(x, w, precision=lax.Precision.HIGHEST, preferred_element_type=F32)


def kernel(cfg, rhs, start, out, *scratch):
    (u0, v0, f0, a1, b1, g1, a2, b2, g2, e3, pz, pb, stage_u, stage_f, part_u, part_f, s3, g3, slots, message, mask0, mask1, mask2,
     send_z, recv_z, recv_d, recv_yu, recv_yf, wide_in, wide_nat, wide_out,
     load_sem, out_sem, fine_s, fine_r, send_sem, recv_sem, all_s, all_r) = scratch
    l0, l1, l2 = levels = cfg.levels
    masks = (mask0, mask1, mask2)
    n_x, n_y, n_z = cfg.counts
    cx, cy, cz = lax.axis_index('sx'), lax.axis_index('sy'), lax.axis_index('sz')
    total = n_x * n_y * n_z
    rank = (cz * n_y + cy) * n_x + cx
    row_blocks = n_x * n_y
    yb = cy * n_x + cx

    inner = pl.ds(TILE, l0.nz)
    loads = [pltpu.make_async_copy(src, dst.at[:, inner], load_sem.at[k]) for k, (src, dst) in enumerate(((start, stage_u), (rhs, stage_f)))]
    for copy in loads:
        copy.start()

    def peer(p):
        r = lax.rem(rank + p, total)
        return {'sz': r // row_blocks, 'sy': (r // n_x) % n_y, 'sx': r % n_x}

    barrier = pltpu.get_barrier_semaphore()

    @pl.loop(1, total)
    def _(p):
        pl.semaphore_signal(barrier, inc=1, device_id=peer(p), device_id_type=MESH)

    def inside(step, at, count):
        if step == 0:
            return True
        return at > 0 if step < 0 else at < count - 1

    def exists(d):
        return jnp.logical_and(inside(STEP_Y[d], yb, row_blocks), inside(STEP_Z[d], cz, n_z))

    def zero(ref):
        @pl.loop(0, ref.shape[0])
        def _(i):
            ref[i] = jnp.zeros(ref.shape[1:], F32)

    def span(step, first, n, wide, own):
        if step == 0:
            return pl.ds(first, n)
        if step < 0:
            return pl.ds(first if own else first - wide, wide)
        return pl.ds(first + n - wide if own else first + n, wide)

    def region(index, d, own):
        lv, arr = levels[index], (None, g1, g2)[index]
        return arr.at[span(STEP_Y[d], lv.hx, lv.ny, lv.wide, own), 0, span(STEP_Z[d], lv.z0, lv.nz, TILE, own)]

    def halo_copy(index, d, arriving):
        k = index - 1
        at = yb + STEP_Y[d]
        return pltpu.make_async_remote_copy(
            src_ref=region(index, d, not arriving), dst_ref=region(index, d if arriving else OPPOSITE[d], False),
            send_sem=send_sem.at[k, d], recv_sem=recv_sem.at[k, d if arriving else OPPOSITE[d]],
            device_id={'sx': at % n_x, 'sy': at // n_x, 'sz': cz + STEP_Z[d]}, device_id_type=MESH)

    def each(act):
        for d in (4, 5, 6, 7, 2, 3, 0, 1):
            @pl.when(exists(d))
            def _(d=d):
                act(d)

    def exchange(index):
        each(lambda d: halo_copy(index, d, False).start())
        each(lambda d: halo_copy(index, d, True).wait_recv())

    def drain(index):
        each(lambda d: halo_copy(index, d, False).wait_send())

    chip_y = n_x * l0.ny
    reach = l0.ny + l0.wide
    outer = 2 * cx - 1

    def fine_copies():
        got = []

        def add(sends, arrives, src, dst, arrival, k, theirs, **to):
            made = [pltpu.make_async_remote_copy(
                src_ref=a, dst_ref=b, send_sem=fine_s.at[k], recv_sem=fine_r.at[r], device_id=to, device_id_type=MESH)
                for a, b, r in ((src, dst, theirs[0]), (arrival, arrival, theirs[1]))]
            got.append((sends, arrives, *made))
        n = 0
        for z_side, z_step in enumerate((-1, 1)):
            for y_side, y_step in enumerate((-1, 1)):
                edge = pl.ds(0 if y_step < 0 else chip_y - l0.wide, l0.wide)
                to_z = jnp.logical_and(inside(y_step, cy, n_y), inside(z_step, cz, n_z))
                in_z = jnp.logical_and(jnp.logical_and((cy + outer >= 0) & (cy + outer < n_y), inside(z_step, cz, n_z)), True)
                add(to_z, in_z, send_z.at[z_side, edge], recv_d.at[1 - z_side, cx], recv_d.at[z_side, y_side], n,
                    (8 + 2 * (1 - z_side) + cx, 8 + 2 * z_side + y_side), sx=1 - y_side, sy=cy + y_step, sz=cz + z_step)
                n += 1
        for z_side, z_step in enumerate((-1, 1)):
            for core in range(n_x):
                there = inside(z_step, cz, n_z)
                add(there, there, send_z.at[z_side, pl.ds(core * (chip_y - reach), reach)], recv_z.at[1 - z_side, cx],
                    recv_z.at[z_side, core], n, (12 + 2 * (1 - z_side) + cx, 12 + 2 * z_side + core), sx=core, sz=cz + z_step)
                n += 1
        return got

    def row_copies():
        got = []
        here = (cy + outer >= 0) & (cy + outer < n_y)
        for y_side, y_step in enumerate((-1, 1)):
            edge = pl.ds(0 if y_step < 0 else chip_y - l0.wide, l0.wide)
            for k, (stage, buf) in enumerate(((stage_u, recv_yu), (stage_f, recv_yf))):
                made = [pltpu.make_async_remote_copy(
                    src_ref=a, dst_ref=b, send_sem=fine_s.at[8 + 2 * y_side + k], recv_sem=fine_r.at[2 * r + k],
                    device_id={'sx': 1 - y_side, 'sy': cy + y_step}, device_id_type=MESH)
                    for a, b, r in ((stage.at[edge, inner], buf.at[cx], cx), (buf.at[y_side], buf.at[y_side], y_side))]
                got.append((inside(y_step, cy, n_y), here, *made))
        return got

    def partner_copies():
        other = pl.ds((1 - cx) * (chip_y - reach), reach)
        return [pltpu.make_async_remote_copy(
            src_ref=stage.at[other, inner], dst_ref=buf, send_sem=fine_s.at[12 + k], recv_sem=fine_r.at[4 + k],
            device_id={'sx': 1 - cx}, device_id_type=MESH) for k, (stage, buf) in enumerate(((stage_u, part_u), (stage_f, part_f)))]

    def begin(copies):
        for sends, _, copy, _ in copies:
            @pl.when(sends)
            def _(copy=copy):
                copy.start()

    def arrive(copies):
        for _, arrives, _, copy in copies:
            @pl.when(arrives)
            def _(copy=copy):
                copy.wait_recv()

    def finish(copies):
        for sends, _, copy, _ in copies:
            @pl.when(sends)
            def _(copy=copy):
                copy.wait_send()

    @pl.when(jnp.logical_not((cy + outer >= 0) & (cy + outer < n_y)))
    def _():
        for buf in (recv_yu, recv_yf, recv_d):
            for k in range(2):
                zero(buf.at[k])
    for z_side, z_step in enumerate((-1, 1)):
        @pl.when(jnp.logical_not(inside(z_step, cz, n_z)))
        def _(z_side=z_side):
            for core in range(n_x):
                zero(recv_z.at[z_side, core])
            zero(recv_d.at[z_side])
    for index in (1, 2):
        for d in SIDES:
            @pl.when(jnp.logical_not(exists(d)))
            def _(index=index, d=d):
                zero(region(index, d, False))

    for lv, arrays in ((l0, (u0, v0)), (l1, (a1, b1)), (l2, (a2, b2))):
        for arr in arrays:
            for plane, outside in ((lv.hx - 1, yb == 0), (lv.hx + lv.ny, yb == row_blocks - 1)):
                @pl.when(outside)
                def _(arr=arr, lv=lv, plane=plane):
                    put(arr, plane, lv.all, [jnp.zeros((lv.rows, LANES), F32)] * lv.parts)

    for lv, table in zip(levels, masks):
        shape = (lv.rows, LANES)
        z = rows_of(shape) + (lv.top - lv.z0) + cz * lv.nz
        ok = (z >= 0) & (z < n_z * lv.nz) & (lanes_of(shape) < lv.nx)
        table[0] = jnp.zeros(shape, F32)
        table[1] = jnp.where(ok, 1.0, 0.0).astype(F32)
        table[2] = jnp.where(ok, NINTH, 0.0).astype(F32)

    def valid(lv, p):
        y = p + (yb * lv.ny - lv.hx)
        return flag((y >= 0) & (y < row_blocks * lv.ny))

    big = (2 * LANES, 2 * LANES)
    r, c = rows_of(big), lanes_of(big)

    def cell(k):
        return jnp.where(k < LANES, 2 * k, 2 * k - (2 * LANES - 1))

    def mine(k):
        return (k + LANES * cx) % (2 * LANES)
    wide_in[...] = jnp.where(mine(r) == cell(c), 1.0, 0.0).astype(F32)
    wide_nat[...] = jnp.where(r == cell(c), 1.0, 0.0).astype(F32)
    wide_out[...] = jnp.where(cell(r) == mine(c), 1.0, 0.0).astype(F32)
    pl.semaphore_wait(barrier, total - 1)

    def across(c, lv):
        if lv.parts > 1:
            even, odd = c
            return [odd + from_below(odd), even + from_above(even)]
        if lv.nx == LANES:
            return [from_below(c[0]) + from_above(c[0])]
        return [roll(c[0], 1) + roll(c[0], LANES - 1)]

    def neighbours(src, p, xm, c, xp, lv, top, n):
        zm, zp = get(src, p, pl.ds(top - 1, n), lv), get(src, p, pl.ds(top + 1, n), lv)
        return every(lambda a, b, d, e, f: ((a + b) + (d + e)) + f, xm, xp, zm, zp, across(c, lv))

    def table_rows(table, k, lv, top, n):
        return table[k, pl.ds(top - lv.top, n)]

    def sweep(src, dst, rhs_ref, lv, table, scale=None):
        @pl.loop(0, lv.count)
        def _(g):
            base = lv.begin + g * lv.group
            for top, n in lv.blocks:
                rows = pl.ds(top, n)
                xm, c = get(src, base - 1, rows, lv), get(src, base, rows, lv)
                for j in range(lv.group):
                    p = base + j
                    xp = get(src, p + 1, rows, lv)
                    t = every(lambda a, b: a + 3.0 * b, neighbours(src, p, xm, c, xp, lv, top, n), c)
                    if scale is not None:
                        t = [x * scale for x in t]
                    keep = table_rows(table, 2 * valid(lv, p), lv, top, n)
                    put(dst, p, rows, every(lambda a, b: (a + b) * keep, t, get(rhs_ref, p, rows, lv)))
                    xm, c = c, xp

    def first_sweep(dst, rhs_ref, lv, table):
        @pl.loop(0, lv.count)
        def _(g):
            for j in range(lv.group):
                p = lv.begin + g * lv.group + j
                dst[p, 0, lv.all] = rhs_ref[p, 0, lv.all] * table[2 * valid(lv, p)]

    def restrict_planes(src, rhs_ref, lv, table, group):
        def res(p, xm, c, xp, top, n):
            return every(lambda a, b, d: a + b - 6.0 * d, neighbours(src, p, xm, c, xp, lv, top, n), get(rhs_ref, p, pl.ds(top, n), lv), c)

        @pl.loop(0, lv.ny // 2 // group)
        def _(i):
            for top, n in lv.blocks:
                rows = pl.ds(top, n)
                p = lv.hx + 2 * group * i
                xm, c = get(src, p - 1, rows, lv), get(src, p, rows, lv)
                prev = res(p - 1, get(src, p - 2, rows, lv), xm, c, top, n)
                prev = [jnp.where((yb > 0) | (i > 0), x, 0.0) for x in prev]
                keep = table_rows(table, 1, lv, top, n)
                for j in range(group):
                    x1, x2 = get(src, p + 1, rows, lv), get(src, p + 2, rows, lv)
                    even = res(p, xm, c, x1, top, n)
                    odd = res(p + 1, c, x1, x2, top, n)
                    for h in range(lv.parts):
                        pb[h, i * group + j, rows] = ((prev[h] + odd[h]) + (even[h] + even[h])) * keep
                    prev, xm, c, p = odd, x1, x2, p + 2

    def restricted_rows(i, lv, h=0):
        half = lv.nz // 2
        return ((pb[h, i, pl.ds(lv.z0 - 1, half, stride=2)] + pb[h, i, pl.ds(lv.z0 + 1, half, stride=2)])
                + 2.0 * pb[h, i, pl.ds(lv.z0, half, stride=2)])

    def weights(near, one, other):
        return jnp.where(near == 0, one, jnp.where((near == 1) | (near == -1), other, 0.0)).astype(F32)

    square = (LANES, LANES)
    eighth = 1.0 / (TILE * TILE)

    def restrict_level(src, rhs_ref, lv, table, coarse_rhs, coarse, group, step):
        restrict_planes(src, rhs_ref, lv, table, group)
        lane = lanes_of(square)
        w = jnp.where(lane < coarse.nx, weights(rows_of(square) - 2 * lane, 2.0 * eighth, eighth), 0.0)

        @pl.loop(0, coarse.ny // step)
        def _(i):
            got = [restricted_rows(i * step + j, lv) for j in range(step)]
            if lv.parts > 1:
                odds = [restricted_rows(i * step + j, lv, 1) for j in range(step)]
                got = [((odd + from_below(odd)) + 2.0 * even) * eighth for even, odd in zip(got, odds)]
            else:
                got = dot(stack(got), w)
                got = [got[j * coarse.nz:(j + 1) * coarse.nz] for j in range(step)]
            for j in range(step):
                coarse_rhs[coarse.hx + i * step + j, 0, coarse.own] = got[j]

    def prolong_planes(e, first, e_z0, e_top, e_rows, e_nx, chunk, n_chunks, lv):
        lane, below = lanes_of(square), rows_of(square)
        w = jnp.where(below < e_nx, weights(lane - 2 * below, 4.0, 2.0), 0.0)
        row = e_z0 - e_top - (lv.z0 - lv.top) // 2
        n = lv.rows // 2

        @pl.loop(0, n_chunks)
        def _(i):
            planes = pl.ds(first + i * chunk, chunk)
            got = e[planes, 0, pl.ds(e_top, e_rows)]
            if lv.parts == 1:
                got = dot(got.reshape(chunk * e_rows, LANES), w).reshape(chunk, e_rows, LANES)
            else:
                got = got * 4.0
            pz[pl.ds(i * chunk, chunk), pl.ds(0, e_rows)] = got

        @pl.loop(0, n_chunks)
        def _(i):
            for j in range(chunk):
                a = pz[i * chunk + j, pl.ds(row, n)]
                b = pz[i * chunk + j, pl.ds(row + 1, n)]
                pb[0, i * chunk + j, pl.ds(lv.top, n, stride=2)] = a
                pb[0, i * chunk + j, pl.ds(lv.top + 1, n, stride=2)] = 0.5 * (a + b)

    def correct(dst, lv, table, pairs):
        def load(at, rows):
            a = pb[0, at, rows]
            return [a, 0.5 * (a + from_above(a))] if lv.parts > 1 else [a]

        @pl.loop(0, lv.group * lv.count // (2 * pairs))
        def _(i):
            for top, n in lv.blocks:
                rows = pl.ds(top, n)
                a = load(i * pairs, rows)
                for j in range(pairs):
                    b = load(i * pairs + j + 1, rows)
                    p = lv.begin + 2 * (pairs * i + j)
                    between = every(lambda x, y: 0.5 * (x + y), a, b)
                    for q, add in ((p, a), (p + 1, between)):
                        keep = table_rows(table, valid(lv, q), lv, top, n)
                        put(dst, q, rows, every(lambda x, y: (x + y) * keep, get(dst, q, rows, lv), add))
                    a = b

    partner, row_halo, halo = partner_copies(), row_copies(), fine_copies()
    for copy in loads:
        copy.wait()
    begin(row_halo)
    for copy in partner:
        copy.start()
    half = TILE // 2
    upper = rows_of((TILE, LANES)) >= half

    @pl.loop(0, chip_y // TILE)
    def _(i):
        for j in range(TILE):
            y = i * TILE + j
            for side, row in enumerate((TILE, TILE + l0.nz - half)):
                send_z[side, y] = jnp.where(upper, stage_f[y, pl.ds(row - half, TILE)], stage_u[y, pl.ds(row, TILE)])
    begin(halo)

    step = 2
    for copy in partner:
        copy.wait_recv()
    for stage, buf, dst in ((stage_u, part_u, u0), (stage_f, part_f, f0)):
        @pl.loop(0, reach // step)
        def _(i, stage=stage, buf=buf, dst=dst):
            planes = pl.ds(cx * (chip_y - reach) + i * step, step)
            mine_, theirs = stage[planes, inner], buf[pl.ds(i * step, step)]
            got = dot(join(mine_.reshape(step * l0.nz, LANES), theirs.reshape(step * l0.nz, LANES)), wide_in[...])
            put(dst, pl.ds(l0.hx - cx * l0.wide + i * step, step), l0.own, [x.reshape(step, l0.nz, LANES) for x in halves(got)])
    arrive(row_halo)
    arrive(halo)
    finish(row_halo)
    finish(halo)
    for copy in partner:
        copy.wait_send()
    outer_plane = l0.hx - l0.wide + cx * reach

    def together(buf, at, n):
        return join(buf[0, at].reshape(n, LANES), buf[1, at].reshape(n, LANES))
    for buf, dst in ((recv_yu, u0), (recv_yf, f0)):
        @pl.loop(0, l0.wide // step)
        def _(i, buf=buf, dst=dst):
            got = dot(together(buf, pl.ds(i * step, step), step * l0.nz), wide_nat[...])
            put(dst, pl.ds(outer_plane + i * step, step), l0.own, [x.reshape(step, l0.nz, LANES) for x in halves(got)])

    def put_rows(p, side, tile):
        row = l0.z0 + l0.nz if side else l0.z0 - half
        for h, part in enumerate(halves(tile)):
            pltpu.store(u0.at[p, h, pl.ds(row, TILE)], part, mask=jnp.logical_not(upper))
            pltpu.store(f0.at[p, h, pl.ds(row - half, TILE)], part, mask=upper)
    some = reach // 3
    for side in range(2):
        @pl.loop(0, reach // some)
        def _(i, side=side):
            got = dot(together(recv_z.at[side], pl.ds(i * some, some), some * TILE), wide_nat[...])
            for j in range(some):
                put_rows(l0.hx - cx * l0.wide + i * some + j, side, got[j * TILE:(j + 1) * TILE])
        got = dot(together(recv_d.at[side], pl.ds(0, l0.wide), l0.wide * TILE), wide_nat[...])
        for j in range(l0.wide):
            put_rows(outer_plane + j, side, got[j * TILE:(j + 1) * TILE])
    sweep(u0, v0, f0, l0, mask0, cfg.stiffness)
    sweep(v0, u0, f0, l0, mask0)
    restrict_level(u0, f0, l0, mask0, g1, l1, 4, 4)

    exchange(1)
    first_sweep(a1, g1, l1, mask1)
    sweep(a1, b1, g1, l1, mask1)
    restrict_level(b1, g1, l1, mask1, g2, l2, 8, 8)
    exchange(2)
    first_sweep(a2, g2, l2, mask2)
    sweep(a2, b2, g2, l2, mask2)

    restrict_planes(b2, g2, l2, mask2, 4)
    ny3, nz3, width = l2.ny // 2, l2.nz // 2, l2.nx // 2
    near = rows_of(square) - 2 * (lanes_of(square) % width)
    got = dot(stack([restricted_rows(j, l2) for j in range(ny3)]), weights(near, 2.0 * eighth, eighth))
    tile = (TILE, LANES)
    lane = lanes_of(tile)
    block = lane // width
    blocks = LANES // width
    packed = got[:nz3]
    for j in range(1, ny3):
        packed = jnp.where(block == j, got[j * nz3:(j + 1) * nz3], packed)
    packed = roll(packed, width * cz)
    message[...] = packed
    slot = yb * n_z + cz
    slots[slot] = packed

    def gather_copy(p, at):
        return pltpu.make_async_remote_copy(
            src_ref=message, dst_ref=slots.at[at], send_sem=all_s.at[p], recv_sem=all_r.at[at], device_id=peer(p), device_id_type=MESH)

    @pl.loop(1, total)
    def _(p):
        gather_copy(p, slot).start()

    @pl.loop(1, total)
    def _(p):
        who = peer(p)
        gather_copy(p, (who['sy'] * n_x + who['sx']) * n_z + who['sz']).wait_recv()

    data = pl.ds(TILE, TILE)
    whole = row_blocks * ny3
    for s in range(2):
        @pl.loop(0, TILE)
        def _(i, s=s):
            for at in (i, TILE + whole + i):
                s3[s, at, data] = jnp.zeros(tile, F32)
    live = lane < width * n_z

    @pl.loop(0, row_blocks)
    def _(part):
        for j in range(ny3):
            acc = jnp.zeros(tile, F32)
            for t in range(n_z):
                acc = jnp.where((block + 2 * blocks - t - j) % blocks == 0, slots[part * n_z + t], acc)
            acc = jnp.where(live, roll(acc, back(width * j)), 0.0)
            g3[part * ny3 + j] = acc
            s3[0, TILE + part * ny3 + j, data] = acc * NINTH

    row = rows_of(tile)
    x_first, x_last = lane % width == 0, lane % width == width - 1
    top, bottom = row == 0, row == TILE - 1
    z_first, z_last = lane < width, lane >= width * (n_z - 1)

    def coarse_sweep(k, carry):
        old, new = k % 2, (k + 1) % 2
        xm, c = s3[old, TILE - 1, data], s3[old, TILE, data]
        for y in range(whole):
            at = TILE + y
            xp = s3[old, at + 1, data]
            above = jnp.where(z_first, 0.0, roll(s3[old, at, pl.ds(2 * TILE - 1, TILE)], width % LANES))
            below = jnp.where(z_last, 0.0, roll(s3[old, at, pl.ds(1, TILE)], back(width)))
            zm = jnp.where(top, above, s3[old, at, pl.ds(TILE - 1, TILE)])
            zp = jnp.where(bottom, below, s3[old, at, pl.ds(TILE + 1, TILE)])
            left = jnp.where(x_first, 0.0, roll(c, 1))
            right = jnp.where(x_last, 0.0, roll(c, LANES - 1))
            t = (xm + xp) + (zm + zp) + (left + right) + 3.0 * c + g3[y]
            s3[new, at, data] = t * NINTH
            xm, c = c, xp
        return carry
    lax.fori_loop(0, COARSE_SWEEPS - 1, coarse_sweep, 0)

    first = (l2.begin - l2.hx) // 2
    for i in range(e3.shape[0]):
        c = s3[(COARSE_SWEEPS - 1) % 2, yb * ny3 + (TILE + i + first), data]
        for k in range(3):
            ok = (lane < width) & (cz + k > 0) & (cz + k < n_z + 1)
            e3[i, 0, pl.ds(TILE * k, TILE)] = jnp.where(ok, roll(c, back((cz + k) * width + LANES - width)), 0.0)

    prolong_planes(e3, 0, TILE, 0, 3 * TILE, width, 6, 2, l2)
    correct(b2, l2, mask2, 5)
    sweep(b2, a2, g2, l2, mask2)
    sweep(a2, b2, g2, l2, mask2)
    prolong_planes(b2, l2.hx + (l1.begin - l1.hx) // 2, l2.z0, l2.top, l2.rows, l2.nx, 8, 2, l1)
    correct(b1, l1, mask1, 7)
    sweep(b1, a1, g1, l1, mask1)
    sweep(a1, b1, g1, l1, mask1)
    prolong_planes(b1, l1.hx + (l0.begin - l0.hx) // 2, l1.z0, l1.top, l1.rows, l1.nx, 8, 3, l0)
    correct(u0, l0, mask0, 4)
    sweep(u0, v0, f0, l0, mask0)

    def results(i):
        here, there = pl.ds(i * step, step), pl.ds(cx * l0.ny + i * step, step)
        return (pltpu.make_async_copy(stage_u.at[here, inner], out.at[there], out_sem.at[0, i]),
                pltpu.make_async_remote_copy(
                    src_ref=stage_f.at[here, inner], dst_ref=out.at[there], send_sem=out_sem.at[1, i], recv_sem=out_sem.at[2, i],
                    device_id={'sx': 1 - cx}, device_id_type=MESH))

    @pl.loop(0, l0.ny // step)
    def _(i):
        got = []
        for j in range(step):
            p = l0.hx + i * step + j
            c = get(v0, p, l0.own, l0)
            around = neighbours(v0, p, get(v0, p - 1, l0.own, l0), c, get(v0, p + 1, l0.own, l0), l0, l0.z0, l0.nz)
            got.append(join(*every(lambda x, y, g: x + 3.0 * y + g, around, c, get(f0, p, l0.own, l0))))
        mine_, theirs = halves(dot(stack(got) * (NINTH / cfg.stiffness), wide_out[...]))
        here = pl.ds(i * step, step)
        stage_u[here, inner] = mine_.reshape(step, l0.nz, LANES)
        stage_f[here, inner] = theirs.reshape(step, l0.nz, LANES)
        for copy in results(i):
            copy.start()

    @pl.loop(0, l0.ny // step)
    def _(i):
        local, remote = results(i)
        local.wait()
        remote.wait()
    drain(1)
    drain(2)

    @pl.loop(1, total)
    def _(p):
        gather_copy(p, slot).wait_send()


def local_cycle(rhs, start, counts, size):
    rhs, start = (jnp.transpose(x, (1, 2, 0)) for x in (rhs, start))
    n_x, n_y, n_z = counts
    chip_y, nz, nx = rhs.shape
    shapes = [(chip_y // n_x >> k, nz >> k, nx * n_x >> k) for k in range(3)]
    l0 = make_level(shapes[0], 6, 8, 4, nz + 8, 2, 8, (shapes[0][0] + 8) // 8, 4, 24)
    l1 = make_level(shapes[1], 8, 16, 8, shapes[1][1] + 16, 2, 14, (shapes[1][0] + 12) // 14, 5, 24)
    l2 = make_level(shapes[2], 8, 16, 8, shapes[2][1] + 16, 2, 10, (shapes[2][0] + 12) // 10, 6, 32)
    cfg = types.SimpleNamespace(levels=(l0, l1, l2), counts=counts, stiffness=float((size + 1) ** 2))
    total = n_x * n_y * n_z

    def vmem(*shape):
        return pltpu.VMEM(shape, F32)

    scratch = [vmem(lv.planes, lv.parts, lv.depth, LANES) for lv in (l0, l1, l2) for _ in range(3)]
    whole = n_x * n_y * (l2.ny // 2)
    reach = l0.ny + l0.wide
    scratch += [vmem(12, 1, 3 * TILE, LANES), vmem(l1.ny + 8, l1.rows, LANES), vmem(2, l1.ny + 8, l0.depth, LANES)]
    scratch += [vmem(chip_y, l0.depth, LANES)] * 2 + [vmem(reach, nz, LANES)] * 2
    scratch += [vmem(2, whole + 2 * TILE, 3 * TILE, LANES), vmem(whole, TILE, LANES), vmem(total, TILE, LANES), vmem(TILE, LANES)]
    scratch += [vmem(3, lv.rows, LANES) for lv in (l0, l1, l2)]
    scratch += [vmem(2, chip_y, TILE, LANES), vmem(2, n_x, reach, TILE, LANES), vmem(2, 2, l0.wide, TILE, LANES)]
    scratch += [vmem(2, l0.wide, nz, LANES)] * 2 + [vmem(2 * LANES, 2 * LANES)] * 3
    sems = [(2,), (3, l0.ny // 2), (16,), (16,), (2, len(SIDES)), (2, len(SIDES)), (total,), (total,)]
    scratch += [pltpu.SemaphoreType.DMA(shape) for shape in sems]
    got = pl.pallas_call(
        functools.partial(kernel, cfg),
        out_shape=jax.ShapeDtypeStruct(rhs.shape, F32),
        in_specs=[pl.BlockSpec(memory_space=pl.ANY)] * 2,
        out_specs=pl.BlockSpec(memory_space=pl.ANY),
        scratch_shapes=scratch,
        compiler_params=pltpu.CompilerParams(collective_id=0, has_side_effects=True, vmem_limit_bytes=60 * 2 ** 20),
    )(rhs, start)
    return jnp.transpose(got, (2, 0, 1))


def solution(mesh):
    counts = (mesh.shape['sx'], mesh.shape['sy'], mesh.shape['sz'])
    spec = P(('dp', 'sx'), 'sy', 'sz')

    def run(rhs_grid, u_start):
        size = rhs_grid.shape[0] // mesh.shape['dp']
        cycle = functools.partial(local_cycle, counts=counts, size=size)
        return jax.shard_map(cycle, mesh=mesh, in_specs=(spec, spec), out_specs=spec, check_vma=False)(rhs_grid, u_start)
    return run
```

time: 1050 us -> 66.4 us (0.06); the launches traced: 1040 us -> 66.3 us
  starting transfers between devices: 473 us -> 0 us
  local copies, waits for them, and re-layouts: 362 us -> 3.16 us
  other arithmetic: 145 us -> 0 us
  Pallas kernels: 0 us -> 63.2 us
  waiting for transfers between devices: 53.8 us -> 0 us
    ppermute x186 -> x0, starting transfers between devices: 473 us -> none  [the longest x93 297 us: send_up(): lax.ppermute(plane, name, [(rank, rank + 1) for rank in range(count - 1)])]
    slice x151 -> x0, local copies, waits for them, and re-layouts: 188 us -> none  [the longest x27 101 us: neighbour_sum(): lax.slice_in_dim(field, 1, length, axis=axis)]
    add x42 -> x0, other arithmetic: 95.1 us -> none  [the longest x25 74 us: jacobi_sweep(): field + residual(source, field, stiffness, counts) / (9.0 * stiffness)]
    concatenate x113 -> x0, local copies, waits for them, and re-layouts: 71 us -> none  [the longest x75 35 us: neighbour_sum(): jnp.concatenate([lower, lax.slice_in_dim(field, 0, length - 1, axis=axis)...]
    pallas_call x0 -> x1, Pallas kernels: none -> 63.2 us  [local_cycle(): pl.pallas_call(functools.partial(kernel, cfg), out_shape=jax.ShapeDtypeSt...]
    ppermute x36 -> x0, local copies, waits for them, and re-layouts: 56.1 us -> none  [the longest x23 30.8 us: send_up(): lax.ppermute(plane, name, [(rank, rank + 1) for rank in range(count - 1)])]
    ppermute x186 -> x0, waiting for transfers between devices: 53.8 us -> none  [the longest x93 35 us: send_up(): lax.ppermute(plane, name, [(rank, rank + 1) for rank in range(count - 1)])]
    sub x5 -> x0, other arithmetic: 30.6 us -> none  [residual(): return source - stiffness * (6.0 * field - neighbour_sum(field, counts))]
  transfers between devices with their start and end apart: 186 -> 0, of which waited for: 29 -> 0; matrix products, arithmetic and copies ran while one was open for 26% -> 0% of each run, Pallas kernels for 0% -> 0%
where the time goes in v2:
time: 66.4 us; the launch traced here: 66.3 us
  Pallas kernels  63.2 us (95%)
  local copies, waits for them, and re-layouts  3.16 us (5%)
    pallas_call x1, Pallas kernels, local_cycle(): pl.pallas_call(functools.partial(kernel, cfg), out_shape=jax.ShapeDtypeSt...  63.2 us
    unnamed x1, local copies, waits for them, and re-layouts  3.16 us

profile of v2, /device:TPU:97, one launch (start us, length us, event | category | flops | bytes accessed | tf_op | source)
XLA Modules:
  0.0 66.3 jit_solution(10553080354798835337)
XLA Ops:
  0.0 63.2 %shard_map.28 = f32[64,64,128]{2,1,0:T(8,128)} custom-call(f32[64,64,128]{2,1,0:T(8,128)} %bitcast.4, f32[64,64,128]{2,1,0:T(8,128)} %bitcast.5), custom_call_target="tpu_custom_call" | custom-call | tf_op jit(solution)/shard_map/pallas_call | solution.py:630
  63.2 3.2 %copy.4 = f32[128,64,64]{0,2,1:T(8,128)} copy(f32[128,64,64]{0,2,1:T(8,128)} %bitcast.3) | data formatting | bytes 4194304

commit v3 on v2

--- a/solution.py
+++ b/solution.py
@@ -84,20 +84,23 @@
     return jnp.where(condition, 1, 0)
 
 
+def pick(x, index):
+    return jnp.take_along_axis(x, index, axis=1, mode='promise_in_bounds')
+
+
 def dot(x, w):
     return jnp.dot(x, w, precision=lax.Precision.HIGHEST, preferred_element_type=F32)
 
 
 def kernel(cfg, rhs, start, out, *scratch):
     (u0, v0, f0, a1, b1, g1, a2, b2, g2, e3, pz, pb, stage_u, stage_f, part_u, part_f, s3, g3, slots, message, mask0, mask1, mask2,
-     send_z, recv_z, recv_d, recv_yu, recv_yf, wide_in, wide_nat, wide_out,
+     send_z, recv_z, recv_d, recv_yu, recv_yf,
      load_sem, out_sem, fine_s, fine_r, send_sem, recv_sem, all_s, all_r) = scratch
     l0, l1, l2 = levels = cfg.levels
     masks = (mask0, mask1, mask2)
     n_x, n_y, n_z = cfg.counts
     cx, cy, cz = lax.axis_index('sx'), lax.axis_index('sy'), lax.axis_index('sz')
     total = n_x * n_y * n_z
-    rank = (cz * n_y + cy) * n_x + cx
     row_blocks = n_x * n_y
     yb = cy * n_x + cx
 
@@ -106,15 +109,14 @@
     for copy in loads:
         copy.start()
 
-    def peer(p):
-        r = lax.rem(rank + p, total)
-        return {'sz': r // row_blocks, 'sy': (r // n_x) % n_y, 'sx': r % n_x}
+    offsets = [(dz, dy, dx) for dz in range(n_z) for dy in range(n_y) for dx in range(n_x)][1:]
+
+    def peer(offset):
+        return {name: lax.rem(at + d, n) for name, at, n, d in zip(('sz', 'sy', 'sx'), (cz, cy, cx), (n_z, n_y, n_x), offset)}
 
     barrier = pltpu.get_barrier_semaphore()
-
-    @pl.loop(1, total)
-    def _(p):
-        pl.semaphore_signal(barrier, inc=1, device_id=peer(p), device_id_type=MESH)
+    for offset in offsets:
+        pl.semaphore_signal(barrier, inc=1, device_id=peer(offset), device_id_type=MESH)
 
     def inside(step, at, count):
         if step == 0:
@@ -263,17 +265,24 @@
         y = p + (yb * lv.ny - lv.hx)
         return flag((y >= 0) & (y < row_blocks * lv.ny))
 
-    big = (2 * LANES, 2 * LANES)
-    r, c = rows_of(big), lanes_of(big)
-
-    def cell(k):
-        return jnp.where(k < LANES, 2 * k, 2 * k - (2 * LANES - 1))
-
-    def mine(k):
-        return (k + LANES * cx) % (2 * LANES)
-    wide_in[...] = jnp.where(mine(r) == cell(c), 1.0, 0.0).astype(F32)
-    wide_nat[...] = jnp.where(r == cell(c), 1.0, 0.0).astype(F32)
-    wide_out[...] = jnp.where(cell(r) == mine(c), 1.0, 0.0).astype(F32)
+    middle = LANES // 2
+
+    def lower(shape, core):
+        return lanes_of(shape) // middle == core
+
+    def split_x(first, second, core):
+        lane = lanes_of(first.shape)
+        pair = 2 * (lane % middle)
+        first, second = pick(first, pair + (lane // middle + core) % 2), pick(second, pair + (lane // middle + 1 - core) % 2)
+        here = lower(first.shape, core)
+        return [jnp.where(here, first, second), roll(jnp.where(here, second, first), middle)]
+
+    def merge_x(even, odd, core):
+        lane = lanes_of(even.shape)
+        odd = roll(odd, middle)
+        here = lower(even.shape, core)
+        spot = lane // 2 + middle * ((lane + core) % 2)
+        return pick(jnp.where(here, even, odd), spot), pick(jnp.where(here, odd, even), (spot + middle) % LANES)
     pl.semaphore_wait(barrier, total - 1)
 
     def across(c, lv):
@@ -424,16 +433,15 @@
                 send_z[side, y] = jnp.where(upper, stage_f[y, pl.ds(row - half, TILE)], stage_u[y, pl.ds(row, TILE)])
     begin(halo)
 
-    step = 2
+    step = 4
     for copy in partner:
         copy.wait_recv()
     for stage, buf, dst in ((stage_u, part_u, u0), (stage_f, part_f, f0)):
         @pl.loop(0, reach // step)
         def _(i, stage=stage, buf=buf, dst=dst):
-            planes = pl.ds(cx * (chip_y - reach) + i * step, step)
-            mine_, theirs = stage[planes, inner], buf[pl.ds(i * step, step)]
-            got = dot(join(mine_.reshape(step * l0.nz, LANES), theirs.reshape(step * l0.nz, LANES)), wide_in[...])
-            put(dst, pl.ds(l0.hx - cx * l0.wide + i * step, step), l0.own, [x.reshape(step, l0.nz, LANES) for x in halves(got)])
+            for j in range(step):
+                k = i * step + j
+                put(dst, l0.hx - cx * l0.wide + k, l0.own, split_x(stage[cx * (chip_y - reach) + k, inner], buf[k], cx))
     arrive(row_halo)
     arrive(halo)
     finish(row_halo)
@@ -442,29 +450,27 @@
         copy.wait_send()
     outer_plane = l0.hx - l0.wide + cx * reach
 
-    def together(buf, at, n):
-        return join(buf[0, at].reshape(n, LANES), buf[1, at].reshape(n, LANES))
     for buf, dst in ((recv_yu, u0), (recv_yf, f0)):
-        @pl.loop(0, l0.wide // step)
+        @pl.loop(0, l0.wide // 2)
         def _(i, buf=buf, dst=dst):
-            got = dot(together(buf, pl.ds(i * step, step), step * l0.nz), wide_nat[...])
-            put(dst, pl.ds(outer_plane + i * step, step), l0.own, [x.reshape(step, l0.nz, LANES) for x in halves(got)])
-
-    def put_rows(p, side, tile):
+            for j in range(2):
+                put(dst, outer_plane + 2 * i + j, l0.own, split_x(buf[0, 2 * i + j], buf[1, 2 * i + j], 0))
+
+    def put_rows(p, side, buf, k):
         row = l0.z0 + l0.nz if side else l0.z0 - half
-        for h, part in enumerate(halves(tile)):
+        for h, part in enumerate(split_x(buf[0, k], buf[1, k], 0)):
             pltpu.store(u0.at[p, h, pl.ds(row, TILE)], part, mask=jnp.logical_not(upper))
             pltpu.store(f0.at[p, h, pl.ds(row - half, TILE)], part, mask=upper)
     some = reach // 3
+
+    @pl.loop(0, reach // some)
+    def _(i):
+        for j in range(some):
+            for side in range(2):
+                put_rows(l0.hx - cx * l0.wide + i * some + j, side, recv_z.at[side], i * some + j)
     for side in range(2):
-        @pl.loop(0, reach // some)
-        def _(i, side=side):
-            got = dot(together(recv_z.at[side], pl.ds(i * some, some), some * TILE), wide_nat[...])
-            for j in range(some):
-                put_rows(l0.hx - cx * l0.wide + i * some + j, side, got[j * TILE:(j + 1) * TILE])
-        got = dot(together(recv_d.at[side], pl.ds(0, l0.wide), l0.wide * TILE), wide_nat[...])
         for j in range(l0.wide):
-            put_rows(outer_plane + j, side, got[j * TILE:(j + 1) * TILE])
+            put_rows(outer_plane + j, side, recv_d.at[side], j)
     sweep(u0, v0, f0, l0, mask0, cfg.stiffness)
     sweep(v0, u0, f0, l0, mask0)
     restrict_level(u0, f0, l0, mask0, g1, l1, 4, 4)
@@ -493,18 +499,15 @@
     slot = yb * n_z + cz
     slots[slot] = packed
 
-    def gather_copy(p, at):
+    def gather_copy(k, at):
         return pltpu.make_async_remote_copy(
-            src_ref=message, dst_ref=slots.at[at], send_sem=all_s.at[p], recv_sem=all_r.at[at], device_id=peer(p), device_id_type=MESH)
-
-    @pl.loop(1, total)
-    def _(p):
-        gather_copy(p, slot).start()
-
-    @pl.loop(1, total)
-    def _(p):
-        who = peer(p)
-        gather_copy(p, (who['sy'] * n_x + who['sx']) * n_z + who['sz']).wait_recv()
+            src_ref=message, dst_ref=slots.at[at], send_sem=all_s.at[k], recv_sem=all_r.at[at], device_id=peer(offsets[k]), device_id_type=MESH)
+
+    for k in range(total - 1):
+        gather_copy(k, slot).start()
+    for k, offset in enumerate(offsets):
+        who = peer(offset)
+        gather_copy(k, (who['sy'] * n_x + who['sx']) * n_z + who['sz']).wait_recv()
 
     data = pl.ds(TILE, TILE)
     whole = row_blocks * ny3
@@ -576,16 +579,13 @@
 
     @pl.loop(0, l0.ny // step)
     def _(i):
-        got = []
         for j in range(step):
-            p = l0.hx + i * step + j
+            k = i * step + j
+            p = l0.hx + k
             c = get(v0, p, l0.own, l0)
             around = neighbours(v0, p, get(v0, p - 1, l0.own, l0), c, get(v0, p + 1, l0.own, l0), l0, l0.z0, l0.nz)
-            got.append(join(*every(lambda x, y, g: x + 3.0 * y + g, around, c, get(f0, p, l0.own, l0))))
-        mine_, theirs = halves(dot(stack(got) * (NINTH / cfg.stiffness), wide_out[...]))
-        here = pl.ds(i * step, step)
-        stage_u[here, inner] = mine_.reshape(step, l0.nz, LANES)
-        stage_f[here, inner] = theirs.reshape(step, l0.nz, LANES)
+            got = every(lambda x, y, g: (x + 3.0 * y + g) * (NINTH / cfg.stiffness), around, c, get(f0, p, l0.own, l0))
+            stage_u[k, inner], stage_f[k, inner] = merge_x(*got, cx)
         for copy in results(i):
             copy.start()
 
@@ -597,9 +597,8 @@
     drain(1)
     drain(2)
 
-    @pl.loop(1, total)
-    def _(p):
-        gather_copy(p, slot).wait_send()
+    for k in range(total - 1):
+        gather_copy(k, slot).wait_send()
 
 
 def local_cycle(rhs, start, counts, size):
@@ -624,8 +623,8 @@
     scratch += [vmem(2, whole + 2 * TILE, 3 * TILE, LANES), vmem(whole, TILE, LANES), vmem(total, TILE, LANES), vmem(TILE, LANES)]
     scratch += [vmem(3, lv.rows, LANES) for lv in (l0, l1, l2)]
     scratch += [vmem(2, chip_y, TILE, LANES), vmem(2, n_x, reach, TILE, LANES), vmem(2, 2, l0.wide, TILE, LANES)]
-    scratch += [vmem(2, l0.wide, nz, LANES)] * 2 + [vmem(2 * LANES, 2 * LANES)] * 3
-    sems = [(2,), (3, l0.ny // 2), (16,), (16,), (2, len(SIDES)), (2, len(SIDES)), (total,), (total,)]
+    scratch += [vmem(2, l0.wide, nz, LANES)] * 2
+    sems = [(2,), (3, l0.ny // 4), (16,), (16,), (2, len(SIDES)), (2, len(SIDES)), (total,), (total,)]
     scratch += [pltpu.SemaphoreType.DMA(shape) for shape in sems]
     got = pl.pallas_call(
         functools.partial(kernel, cfg),

time: 66.4 us -> 57.2 us (0.86)
  Pallas kernels: 63.2 us -> 53.9 us
    pallas_call x1, Pallas kernels: 63.2 us -> 53.9 us  [local_cycle(): pl.pallas_call(functools.partial(kernel, cfg), out_shape=jax.ShapeDtypeSt...]
where the time goes in v3:
time: 57.2 us; the launch traced here: 57.1 us
  Pallas kernels  53.9 us (94%)
  local copies, waits for them, and re-layouts  3.16 us (6%)
    pallas_call x1, Pallas kernels, local_cycle(): pl.pallas_call(functools.partial(kernel, cfg), out_shape=jax.ShapeDtypeSt...  53.9 us
    unnamed x1, local copies, waits for them, and re-layouts  3.16 us

profile of v3, /device:TPU:97, one launch (start us, length us, event | category | flops | bytes accessed | tf_op | source)
XLA Modules:
  0.0 57.1 jit_solution(10049928844771359549)
XLA Ops:
  0.0 53.9 %shard_map.28 = f32[64,64,128]{2,1,0:T(8,128)} custom-call(f32[64,64,128]{2,1,0:T(8,128)} %bitcast.4, f32[64,64,128]{2,1,0:T(8,128)} %bitcast.5), custom_call_target="tpu_custom_call" | custom-call | tf_op jit(solution)/shard_map/pallas_call | solution.py:629
  53.9 3.2 %copy.4 = f32[128,64,64]{0,2,1:T(8,128)} copy(f32[128,64,64]{0,2,1:T(8,128)} %bitcast.3) | data formatting | bytes 4194304

commit v4 on v3

--- a/solution.py
+++ b/solution.py
@@ -95,7 +95,7 @@
 def kernel(cfg, rhs, start, out, *scratch):
     (u0, v0, f0, a1, b1, g1, a2, b2, g2, e3, pz, pb, stage_u, stage_f, part_u, part_f, s3, g3, slots, message, mask0, mask1, mask2,
      send_z, recv_z, recv_d, recv_yu, recv_yf,
-     load_sem, out_sem, fine_s, fine_r, send_sem, recv_sem, all_s, all_r) = scratch
+     load_sem, out_sem, fine_s, fine_r, send_sem, recv_sem, all_s, all_r, ready) = scratch
     l0, l1, l2 = levels = cfg.levels
     masks = (mask0, mask1, mask2)
     n_x, n_y, n_z = cfg.counts
@@ -110,18 +110,22 @@
         copy.start()
 
     offsets = [(dz, dy, dx) for dz in range(n_z) for dy in range(n_y) for dx in range(n_x)][1:]
+    offsets.sort(key=lambda o: -2 * (min(o[0], n_z - o[0]) + min(o[1], n_y - o[1])) - o[2])
 
     def peer(offset):
         return {name: lax.rem(at + d, n) for name, at, n, d in zip(('sz', 'sy', 'sx'), (cz, cy, cx), (n_z, n_y, n_x), offset)}
-
-    barrier = pltpu.get_barrier_semaphore()
-    for offset in offsets:
-        pl.semaphore_signal(barrier, inc=1, device_id=peer(offset), device_id_type=MESH)
 
     def inside(step, at, count):
         if step == 0:
             return True
         return at > 0 if step < 0 else at < count - 1
+
+    around_me = [o for o in offsets if o[0] in (0, 1, n_z - 1) and o[1] in (0, 1, n_y - 1)]
+    barrier = pltpu.get_barrier_semaphore()
+    for offset in around_me:
+        pl.semaphore_signal(barrier, inc=1, device_id=peer(offset), device_id_type=MESH)
+    outer = 2 * cx - 1
+    has_outer = (cy + outer >= 0) & (cy + outer < n_y)
 
     def exists(d):
         return jnp.logical_and(inside(STEP_Y[d], yb, row_blocks), inside(STEP_Z[d], cz, n_z))
@@ -165,7 +169,6 @@
 
     chip_y = n_x * l0.ny
     reach = l0.ny + l0.wide
-    outer = 2 * cx - 1
 
     def fine_copies():
         got = []
@@ -180,7 +183,7 @@
             for y_side, y_step in enumerate((-1, 1)):
                 edge = pl.ds(0 if y_step < 0 else chip_y - l0.wide, l0.wide)
                 to_z = jnp.logical_and(inside(y_step, cy, n_y), inside(z_step, cz, n_z))
-                in_z = jnp.logical_and(jnp.logical_and((cy + outer >= 0) & (cy + outer < n_y), inside(z_step, cz, n_z)), True)
+                in_z = jnp.logical_and(has_outer, inside(z_step, cz, n_z))
                 add(to_z, in_z, send_z.at[z_side, edge], recv_d.at[1 - z_side, cx], recv_d.at[z_side, y_side], n,
                     (8 + 2 * (1 - z_side) + cx, 8 + 2 * z_side + y_side), sx=1 - y_side, sy=cy + y_step, sz=cz + z_step)
                 n += 1
@@ -194,7 +197,6 @@
 
     def row_copies():
         got = []
-        here = (cy + outer >= 0) & (cy + outer < n_y)
         for y_side, y_step in enumerate((-1, 1)):
             edge = pl.ds(0 if y_step < 0 else chip_y - l0.wide, l0.wide)
             for k, (stage, buf) in enumerate(((stage_u, recv_yu), (stage_f, recv_yf))):
@@ -202,7 +204,7 @@
                     src_ref=a, dst_ref=b, send_sem=fine_s.at[8 + 2 * y_side + k], recv_sem=fine_r.at[2 * r + k],
                     device_id={'sx': 1 - y_side, 'sy': cy + y_step}, device_id_type=MESH)
                     for a, b, r in ((stage.at[edge, inner], buf.at[cx], cx), (buf.at[y_side], buf.at[y_side], y_side))]
-                got.append((inside(y_step, cy, n_y), here, *made))
+                got.append((inside(y_step, cy, n_y), has_outer, *made))
         return got
 
     def partner_copies():
@@ -229,7 +231,7 @@
             def _(copy=copy):
                 copy.wait_send()
 
-    @pl.when(jnp.logical_not((cy + outer >= 0) & (cy + outer < n_y)))
+    @pl.when(jnp.logical_not(has_outer))
     def _():
         for buf in (recv_yu, recv_yf, recv_d):
             for k in range(2):
@@ -283,7 +285,7 @@
         here = lower(even.shape, core)
         spot = lane // 2 + middle * ((lane + core) % 2)
         return pick(jnp.where(here, even, odd), spot), pick(jnp.where(here, odd, even), (spot + middle) % LANES)
-    pl.semaphore_wait(barrier, total - 1)
+    pl.semaphore_wait(barrier, len(around_me))
 
     def across(c, lv):
         if lv.parts > 1:
@@ -432,8 +434,11 @@
             for side, row in enumerate((TILE, TILE + l0.nz - half)):
                 send_z[side, y] = jnp.where(upper, stage_f[y, pl.ds(row - half, TILE)], stage_u[y, pl.ds(row, TILE)])
     begin(halo)
+    for offset in around_me:
+        pl.semaphore_signal(ready, inc=1, device_id=peer(offset), device_id_type=MESH)
 
     step = 4
+    some = reach // 3
     for copy in partner:
         copy.wait_recv()
     for stage, buf, dst in ((stage_u, part_u, u0), (stage_f, part_f, f0)):
@@ -443,25 +448,22 @@
                 k = i * step + j
                 put(dst, l0.hx - cx * l0.wide + k, l0.own, split_x(stage[cx * (chip_y - reach) + k, inner], buf[k], cx))
     arrive(row_halo)
+    outer_plane = l0.hx - l0.wide + cx * reach
+
+    for buf, dst in ((recv_yu, u0), (recv_yf, f0)):
+        for j in range(l0.wide):
+            put(dst, outer_plane + j, l0.own, split_x(buf[0, j], buf[1, j], 0))
     arrive(halo)
     finish(row_halo)
     finish(halo)
     for copy in partner:
         copy.wait_send()
-    outer_plane = l0.hx - l0.wide + cx * reach
-
-    for buf, dst in ((recv_yu, u0), (recv_yf, f0)):
-        @pl.loop(0, l0.wide // 2)
-        def _(i, buf=buf, dst=dst):
-            for j in range(2):
-                put(dst, outer_plane + 2 * i + j, l0.own, split_x(buf[0, 2 * i + j], buf[1, 2 * i + j], 0))
 
     def put_rows(p, side, buf, k):
         row = l0.z0 + l0.nz if side else l0.z0 - half
         for h, part in enumerate(split_x(buf[0, k], buf[1, k], 0)):
             pltpu.store(u0.at[p, h, pl.ds(row, TILE)], part, mask=jnp.logical_not(upper))
             pltpu.store(f0.at[p, h, pl.ds(row - half, TILE)], part, mask=upper)
-    some = reach // 3
 
     @pl.loop(0, reach // some)
     def _(i):
@@ -494,7 +496,7 @@
     packed = got[:nz3]
     for j in range(1, ny3):
         packed = jnp.where(block == j, got[j * nz3:(j + 1) * nz3], packed)
-    packed = roll(packed, width * cz)
+    packed = roll(packed, width * cy)
     message[...] = packed
     slot = yb * n_z + cz
     slots[slot] = packed
@@ -503,60 +505,60 @@
         return pltpu.make_async_remote_copy(
             src_ref=message, dst_ref=slots.at[at], send_sem=all_s.at[k], recv_sem=all_r.at[at], device_id=peer(offsets[k]), device_id_type=MESH)
 
+    pl.semaphore_wait(ready, len(around_me))
     for k in range(total - 1):
         gather_copy(k, slot).start()
     for k, offset in enumerate(offsets):
         who = peer(offset)
         gather_copy(k, (who['sy'] * n_x + who['sx']) * n_z + who['sz']).wait_recv()
 
-    data = pl.ds(TILE, TILE)
-    whole = row_blocks * ny3
-    for s in range(2):
-        @pl.loop(0, TILE)
-        def _(i, s=s):
-            for at in (i, TILE + whole + i):
-                s3[s, at, data] = jnp.zeros(tile, F32)
-    live = lane < width * n_z
-
-    @pl.loop(0, row_blocks)
-    def _(part):
+    tall = nz3 * n_z
+    data = pl.ds(TILE, tall)
+    for which in range(2):
+        for y in range(TILE):
+            for at in (0, TILE + tall):
+                s3[which, y, pl.ds(at, TILE)] = jnp.zeros(tile, F32)
+    live = lane < width * n_y
+
+    @pl.loop(0, n_x)
+    def _(core):
         for j in range(ny3):
-            acc = jnp.zeros(tile, F32)
-            for t in range(n_z):
-                acc = jnp.where((block + 2 * blocks - t - j) % blocks == 0, slots[part * n_z + t], acc)
-            acc = jnp.where(live, roll(acc, back(width * j)), 0.0)
-            g3[part * ny3 + j] = acc
-            s3[0, TILE + part * ny3 + j, data] = acc * NINTH
-
-    row = rows_of(tile)
-    x_first, x_last = lane % width == 0, lane % width == width - 1
-    top, bottom = row == 0, row == TILE - 1
-    z_first, z_last = lane < width, lane >= width * (n_z - 1)
+            for z in range(n_z):
+                acc = jnp.zeros(tile, F32)
+                for t in range(n_y):
+                    acc = jnp.where((block + 2 * blocks - t - j) % blocks == 0, slots[(t * n_x + core) * n_z + z], acc)
+                acc = jnp.where(live, roll(acc, back(width * j)), 0.0)
+                rows = pl.ds(TILE + nz3 * z, nz3)
+                g3[core * ny3 + j, rows] = acc
+                s3[0, core * ny3 + j, rows] = acc * NINTH
+
+    long = (tall, LANES)
+    along = lanes_of(long)
+    x_first, x_last = along % width == 0, along % width == width - 1
+    y_first, y_last = along < width, along >= width * (n_y - 1)
 
     def coarse_sweep(k, carry):
         old, new = k % 2, (k + 1) % 2
-        xm, c = s3[old, TILE - 1, data], s3[old, TILE, data]
-        for y in range(whole):
-            at = TILE + y
-            xp = s3[old, at + 1, data]
-            above = jnp.where(z_first, 0.0, roll(s3[old, at, pl.ds(2 * TILE - 1, TILE)], width % LANES))
-            below = jnp.where(z_last, 0.0, roll(s3[old, at, pl.ds(1, TILE)], back(width)))
-            zm = jnp.where(top, above, s3[old, at, pl.ds(TILE - 1, TILE)])
-            zp = jnp.where(bottom, below, s3[old, at, pl.ds(TILE + 1, TILE)])
+        lowest, highest = s3[old, 0, data], s3[old, TILE - 1, data]
+        c = lowest
+        ym = jnp.where(y_first, 0.0, roll(highest, width % LANES))
+        beyond = jnp.where(y_last, 0.0, roll(lowest, back(width)))
+        for y in range(TILE):
+            yp = s3[old, y + 1, data] if y < TILE - 1 else beyond
+            around = (ym + yp) + (s3[old, y, pl.ds(TILE - 1, tall)] + s3[old, y, pl.ds(TILE + 1, tall)])
             left = jnp.where(x_first, 0.0, roll(c, 1))
             right = jnp.where(x_last, 0.0, roll(c, LANES - 1))
-            t = (xm + xp) + (zm + zp) + (left + right) + 3.0 * c + g3[y]
-            s3[new, at, data] = t * NINTH
-            xm, c = c, xp
+            s3[new, y, data] = (around + (left + right) + 3.0 * c + g3[y, data]) * NINTH
+            ym, c = c, yp
         return carry
     lax.fori_loop(0, COARSE_SWEEPS - 1, coarse_sweep, 0)
 
     first = (l2.begin - l2.hx) // 2
     for i in range(e3.shape[0]):
-        c = s3[(COARSE_SWEEPS - 1) % 2, yb * ny3 + (TILE + i + first), data]
-        for k in range(3):
-            ok = (lane < width) & (cz + k > 0) & (cz + k < n_z + 1)
-            e3[i, 0, pl.ds(TILE * k, TILE)] = jnp.where(ok, roll(c, back((cz + k) * width + LANES - width)), 0.0)
+        y = yb * ny3 + (i + first)
+        c = s3[(COARSE_SWEEPS - 1) % 2, (y + TILE) % TILE, pl.ds(pl.multiple_of(cz * nz3, TILE), 3 * TILE)]
+        ok = (lanes_of(c.shape) < width) & (y >= 0) & (y < row_blocks * ny3)
+        e3[i, 0] = jnp.where(ok, roll(c, back((y + TILE) // TILE * width + LANES - width)), 0.0)
 
     prolong_planes(e3, 0, TILE, 0, 3 * TILE, width, 6, 2, l2)
     correct(b2, l2, mask2, 5)
@@ -572,10 +574,9 @@
 
     def results(i):
         here, there = pl.ds(i * step, step), pl.ds(cx * l0.ny + i * step, step)
-        return (pltpu.make_async_copy(stage_u.at[here, inner], out.at[there], out_sem.at[0, i]),
-                pltpu.make_async_remote_copy(
-                    src_ref=stage_f.at[here, inner], dst_ref=out.at[there], send_sem=out_sem.at[1, i], recv_sem=out_sem.at[2, i],
-                    device_id={'sx': 1 - cx}, device_id_type=MESH))
+        return pltpu.make_async_remote_copy(
+            src_ref=stage_f.at[here, inner], dst_ref=out.at[there], send_sem=out_sem.at[0, i], recv_sem=out_sem.at[1, i],
+            device_id={'sx': 1 - cx}, device_id_type=MESH)
 
     @pl.loop(0, l0.ny // step)
     def _(i):
@@ -585,20 +586,22 @@
             c = get(v0, p, l0.own, l0)
             around = neighbours(v0, p, get(v0, p - 1, l0.own, l0), c, get(v0, p + 1, l0.own, l0), l0, l0.z0, l0.nz)
             got = every(lambda x, y, g: (x + 3.0 * y + g) * (NINTH / cfg.stiffness), around, c, get(f0, p, l0.own, l0))
-            stage_u[k, inner], stage_f[k, inner] = merge_x(*got, cx)
-        for copy in results(i):
-            copy.start()
+            out[cx * l0.ny + k], stage_f[k, inner] = merge_x(*got, cx)
+        results(i).start()
 
     @pl.loop(0, l0.ny // step)
     def _(i):
-        local, remote = results(i)
-        local.wait()
-        remote.wait()
+        results(i).wait()
     drain(1)
     drain(2)
 
     for k in range(total - 1):
         gather_copy(k, slot).wait_send()
+
+
+def write_out(held, out, sem):
+    pltpu.make_async_copy(held, out, sem).start()
+    pltpu.make_async_copy(held, out, sem).wait()
 
 
 def local_cycle(rhs, start, counts, size):
@@ -616,24 +619,30 @@
         return pltpu.VMEM(shape, F32)
 
     scratch = [vmem(lv.planes, lv.parts, lv.depth, LANES) for lv in (l0, l1, l2) for _ in range(3)]
-    whole = n_x * n_y * (l2.ny // 2)
     reach = l0.ny + l0.wide
     scratch += [vmem(12, 1, 3 * TILE, LANES), vmem(l1.ny + 8, l1.rows, LANES), vmem(2, l1.ny + 8, l0.depth, LANES)]
     scratch += [vmem(chip_y, l0.depth, LANES)] * 2 + [vmem(reach, nz, LANES)] * 2
-    scratch += [vmem(2, whole + 2 * TILE, 3 * TILE, LANES), vmem(whole, TILE, LANES), vmem(total, TILE, LANES), vmem(TILE, LANES)]
+    scratch += [vmem(2, TILE, l2.nz // 2 * n_z + 2 * TILE, LANES), vmem(TILE, l2.nz // 2 * n_z + 2 * TILE, LANES), vmem(total, TILE, LANES), vmem(TILE, LANES)]
     scratch += [vmem(3, lv.rows, LANES) for lv in (l0, l1, l2)]
     scratch += [vmem(2, chip_y, TILE, LANES), vmem(2, n_x, reach, TILE, LANES), vmem(2, 2, l0.wide, TILE, LANES)]
     scratch += [vmem(2, l0.wide, nz, LANES)] * 2
-    sems = [(2,), (3, l0.ny // 4), (16,), (16,), (2, len(SIDES)), (2, len(SIDES)), (total,), (total,)]
-    scratch += [pltpu.SemaphoreType.DMA(shape) for shape in sems]
+    sems = [(2,), (2, l0.ny // 4), (16,), (16,), (2, len(SIDES)), (2, len(SIDES)), (total,), (total,)]
+    scratch += [pltpu.SemaphoreType.DMA(shape) for shape in sems] + [pltpu.SemaphoreType.REGULAR]
     got = pl.pallas_call(
         functools.partial(kernel, cfg),
-        out_shape=jax.ShapeDtypeStruct(rhs.shape, F32),
+        out_shape=pltpu.VMEM(rhs.shape, F32),
         in_specs=[pl.BlockSpec(memory_space=pl.ANY)] * 2,
-        out_specs=pl.BlockSpec(memory_space=pl.ANY),
+        out_specs=pl.BlockSpec(memory_space=pltpu.VMEM),
         scratch_shapes=scratch,
         compiler_params=pltpu.CompilerParams(collective_id=0, has_side_effects=True, vmem_limit_bytes=60 * 2 ** 20),
     )(rhs, start)
+    got = pl.pallas_call(
+        write_out,
+        out_shape=jax.ShapeDtypeStruct(rhs.shape, F32),
+        in_specs=[pl.BlockSpec(memory_space=pltpu.VMEM)],
+        out_specs=pl.BlockSpec(memory_space=pl.ANY),
+        scratch_shapes=[pltpu.SemaphoreType.DMA],
+    )(pltpu.with_memory_space_constraint(got, pltpu.VMEM))
     return jnp.transpose(got, (2, 0, 1))
 
 

time: 57.2 us -> 53 us (0.927)
  local copies, waits for them, and re-layouts: 3.16 us -> 0 us
  Pallas kernels: 53.9 us -> 53 us
    unnamed x1 -> x0, local copies, waits for them, and re-layouts: 3.16 us -> none
    pallas_call x1 -> x2, Pallas kernels: 53.9 us -> 53 us  [the longest x1 51.6 us: local_cycle(): pl.pallas_call(functools.partial(kernel, cfg), out_shape=pltpu.VMEM(rhs.s...]
where the time goes in v4:
time: 53 us
  Pallas kernels  53 us (100%)
    pallas_call x1, Pallas kernels, local_cycle(): pl.pallas_call(functools.partial(kernel, cfg), out_shape=pltpu.VMEM(rhs.s...  51.6 us
    pallas_call x1, Pallas kernels, local_cycle(): pl.pallas_call(write_out, out_shape=jax.ShapeDtypeStruct(rhs.shape, F32),...  1.33 us

profile of v4, /device:TPU:97, one launch (start us, length us, event | category | flops | bytes accessed | tf_op | source)
XLA Modules:
  0.0 53.0 jit_solution(14788946913162328584)
XLA Ops:
  0.0 51.6 %shard_map.28.held = f32[64,64,128]{2,1,0:T(8,128)S(1)} custom-call(f32[64,64,128]{2,1,0:T(8,128)} %bitcast.3, f32[64,64,128]{2,1,0:T(8,128)} %bitcast.4), custom_call_target="tpu_custom_call" | custom-call | tf_op jit(solution)/shard_map/pallas_call | solution.py:631
  51.6 1.3 %shard_map.29 = f32[64,64,128]{2,1,0:T(8,128)} custom-call(f32[64,64,128]{2,1,0:T(8,128)S(1)} %shard_map.28.held), custom_call_target="tpu_custom_call" | custom-call | tf_op jit(solution)/shard_map/pallas_call | solution.py:639

commit v5 on v4

--- a/solution.py
+++ b/solution.py
@@ -105,7 +105,20 @@
     yb = cy * n_x + cx
 
     inner = pl.ds(TILE, l0.nz)
-    loads = [pltpu.make_async_copy(src, dst.at[:, inner], load_sem.at[k]) for k, (src, dst) in enumerate(((start, stage_u), (rhs, stage_f)))]
+    chip_y = n_x * l0.ny
+
+    def load(planes, rows):
+        shifted = pl.ds(rows.start + TILE, rows.size)
+        k = len(loads)
+        loads.append(pltpu.make_async_copy(start.at[planes, rows], stage_u.at[planes, shifted], load_sem.at[k]))
+        loads.append(pltpu.make_async_copy(rhs.at[planes, rows], stage_f.at[planes, shifted], load_sem.at[k + 1]))
+    loads = []
+    between = pl.ds(TILE, l0.nz - 2 * TILE)
+    for row in (0, l0.nz - TILE):
+        load(pl.ds(0, chip_y), pl.ds(row, TILE))
+    for plane in (0, chip_y - l0.wide):
+        load(pl.ds(plane, l0.wide), between)
+    load(pl.ds(l0.wide, chip_y - 2 * l0.wide), between)
     for copy in loads:
         copy.start()
 
@@ -167,7 +180,6 @@
     def drain(index):
         each(lambda d: halo_copy(index, d, False).wait_send())
 
-    chip_y = n_x * l0.ny
     reach = l0.ny + l0.wide
 
     def fine_copies():
@@ -419,11 +431,8 @@
                     a = b
 
     partner, row_halo, halo = partner_copies(), row_copies(), fine_copies()
-    for copy in loads:
+    for copy in loads[:4]:
         copy.wait()
-    begin(row_halo)
-    for copy in partner:
-        copy.start()
     half = TILE // 2
     upper = rows_of((TILE, LANES)) >= half
 
@@ -434,6 +443,13 @@
             for side, row in enumerate((TILE, TILE + l0.nz - half)):
                 send_z[side, y] = jnp.where(upper, stage_f[y, pl.ds(row - half, TILE)], stage_u[y, pl.ds(row, TILE)])
     begin(halo)
+    for copy in loads[4:8]:
+        copy.wait()
+    begin(row_halo)
+    for copy in loads[8:]:
+        copy.wait()
+    for copy in partner:
+        copy.start()
     for offset in around_me:
         pl.semaphore_signal(ready, inc=1, device_id=peer(offset), device_id_type=MESH)
 
@@ -578,16 +594,26 @@
             src_ref=stage_f.at[here, inner], dst_ref=out.at[there], send_sem=out_sem.at[0, i], recv_sem=out_sem.at[1, i],
             device_id={'sx': 1 - cx}, device_id_type=MESH)
 
+    def merge_group(i):
+        for j in range(step):
+            k = i * step + j
+            out[cx * l0.ny + k], stage_f[k, inner] = merge_x(*get(u0, l0.hx + k, l0.own, l0), cx)
+
     @pl.loop(0, l0.ny // step)
     def _(i):
+        before = (i + l0.ny // step - 1) % (l0.ny // step)
+        merge_group(before)
         for j in range(step):
-            k = i * step + j
-            p = l0.hx + k
+            p = l0.hx + i * step + j
             c = get(v0, p, l0.own, l0)
             around = neighbours(v0, p, get(v0, p - 1, l0.own, l0), c, get(v0, p + 1, l0.own, l0), l0, l0.z0, l0.nz)
-            got = every(lambda x, y, g: (x + 3.0 * y + g) * (NINTH / cfg.stiffness), around, c, get(f0, p, l0.own, l0))
-            out[cx * l0.ny + k], stage_f[k, inner] = merge_x(*got, cx)
-        results(i).start()
+            put(u0, p, l0.own, every(lambda x, y, g: (x + 3.0 * y + g) * (NINTH / cfg.stiffness), around, c, get(f0, p, l0.own, l0)))
+
+        @pl.when(i > 0)
+        def _():
+            results(before).start()
+    merge_group(l0.ny // step - 1)
+    results(l0.ny // step - 1).start()
 
     @pl.loop(0, l0.ny // step)
     def _(i):
@@ -626,7 +652,7 @@
     scratch += [vmem(3, lv.rows, LANES) for lv in (l0, l1, l2)]
     scratch += [vmem(2, chip_y, TILE, LANES), vmem(2, n_x, reach, TILE, LANES), vmem(2, 2, l0.wide, TILE, LANES)]
     scratch += [vmem(2, l0.wide, nz, LANES)] * 2
-    sems = [(2,), (2, l0.ny // 4), (16,), (16,), (2, len(SIDES)), (2, len(SIDES)), (total,), (total,)]
+    sems = [(10,), (2, l0.ny // 4), (16,), (16,), (2, len(SIDES)), (2, len(SIDES)), (total,), (total,)]
     scratch += [pltpu.SemaphoreType.DMA(shape) for shape in sems] + [pltpu.SemaphoreType.REGULAR]
     got = pl.pallas_call(
         functools.partial(kernel, cfg),

time: 53 us -> 54.5 us (1.028)
  Pallas kernels: 53 us -> 54.4 us
    pallas_call x1, Pallas kernels: 51.6 us -> 53 us  [local_cycle(): pl.pallas_call(functools.partial(kernel, cfg), out_shape=pltpu.VMEM(rhs.s...]
where the time goes in v5:
time: 54.5 us; the launch traced here: 54.4 us
  Pallas kernels  54.4 us (100%)
    pallas_call x1, Pallas kernels, local_cycle(): pl.pallas_call(functools.partial(kernel, cfg), out_shape=pltpu.VMEM(rhs.s...  53 us
    pallas_call x1, Pallas kernels, local_cycle(): pl.pallas_call(write_out, out_shape=jax.ShapeDtypeStruct(rhs.shape, F32),...  1.33 us

profile of v5, /device:TPU:97, one launch (start us, length us, event | category | flops | bytes accessed | tf_op | source)
XLA Modules:
  0.0 54.4 jit_solution(17512615264738793143)
XLA Ops:
  0.0 53.0 %shard_map.28.held = f32[64,64,128]{2,1,0:T(8,128)S(1)} custom-call(f32[64,64,128]{2,1,0:T(8,128)} %bitcast.3, f32[64,64,128]{2,1,0:T(8,128)} %bitcast.4), custom_call_target="tpu_custom_call" | custom-call | tf_op jit(solution)/shard_map/pallas_call | solution.py:657
  53.1 1.3 %shard_map.29 = f32[64,64,128]{2,1,0:T(8,128)} custom-call(f32[64,64,128]{2,1,0:T(8,128)S(1)} %shard_map.28.held), custom_call_target="tpu_custom_call" | custom-call | tf_op jit(solution)/shard_map/pallas_call | solution.py:665

commit v6 on v4

--- a/solution.py
+++ b/solution.py
@@ -13,6 +13,7 @@
 TILE = 8
 NINTH = 1.0 / 9.0
 COARSE_SWEEPS = 16
+PARTS = 3
 OPPOSITE = (1, 0, 3, 2, 7, 6, 5, 4)
 STEP_Y = (-1, 1, 0, 0, -1, -1, 1, 1)
 STEP_Z = (0, 0, -1, 1, -1, 1, -1, 1)
@@ -95,7 +96,7 @@
 def kernel(cfg, rhs, start, out, *scratch):
     (u0, v0, f0, a1, b1, g1, a2, b2, g2, e3, pz, pb, stage_u, stage_f, part_u, part_f, s3, g3, slots, message, mask0, mask1, mask2,
      send_z, recv_z, recv_d, recv_yu, recv_yf,
-     load_sem, out_sem, fine_s, fine_r, send_sem, recv_sem, all_s, all_r, ready) = scratch
+     load_sem, out_sem, fine_s, fine_r, send_sem, recv_sem, all_s, all_r, part_s, part_r, ready) = scratch
     l0, l1, l2 = levels = cfg.levels
     masks = (mask0, mask1, mask2)
     n_x, n_y, n_z = cfg.counts
@@ -105,7 +106,20 @@
     yb = cy * n_x + cx
 
     inner = pl.ds(TILE, l0.nz)
-    loads = [pltpu.make_async_copy(src, dst.at[:, inner], load_sem.at[k]) for k, (src, dst) in enumerate(((start, stage_u), (rhs, stage_f)))]
+    chip_y = n_x * l0.ny
+
+    def load(planes, rows):
+        shifted = pl.ds(rows.start + TILE, rows.size)
+        k = len(loads)
+        loads.append(pltpu.make_async_copy(start.at[planes, rows], stage_u.at[planes, shifted], load_sem.at[k]))
+        loads.append(pltpu.make_async_copy(rhs.at[planes, rows], stage_f.at[planes, shifted], load_sem.at[k + 1]))
+    loads = []
+    between = pl.ds(TILE, l0.nz - 2 * TILE)
+    for row in (0, l0.nz - TILE):
+        load(pl.ds(0, chip_y), pl.ds(row, TILE))
+    for plane in (0, chip_y - l0.wide):
+        load(pl.ds(plane, l0.wide), between)
+    load(pl.ds(l0.wide, chip_y - 2 * l0.wide), between)
     for copy in loads:
         copy.start()
 
@@ -167,7 +181,6 @@
     def drain(index):
         each(lambda d: halo_copy(index, d, False).wait_send())
 
-    chip_y = n_x * l0.ny
     reach = l0.ny + l0.wide
 
     def fine_copies():
@@ -207,11 +220,14 @@
                 got.append((inside(y_step, cy, n_y), has_outer, *made))
         return got
 
-    def partner_copies():
-        other = pl.ds((1 - cx) * (chip_y - reach), reach)
+    chunk = reach // PARTS
+
+    def partner_copies(part):
+        other = pl.ds((1 - cx) * (chip_y - reach) + part * chunk, chunk)
         return [pltpu.make_async_remote_copy(
-            src_ref=stage.at[other, inner], dst_ref=buf, send_sem=fine_s.at[12 + k], recv_sem=fine_r.at[4 + k],
-            device_id={'sx': 1 - cx}, device_id_type=MESH) for k, (stage, buf) in enumerate(((stage_u, part_u), (stage_f, part_f)))]
+            src_ref=stage.at[other, inner], dst_ref=buf.at[pl.ds(part * chunk, chunk)], send_sem=part_s.at[part, k],
+            recv_sem=part_r.at[part, k], device_id={'sx': 1 - cx}, device_id_type=MESH)
+            for k, (stage, buf) in enumerate(((stage_u, part_u), (stage_f, part_f)))]
 
     def begin(copies):
         for sends, _, copy, _ in copies:
@@ -418,12 +434,9 @@
                         put(dst, q, rows, every(lambda x, y: (x + y) * keep, get(dst, q, rows, lv), add))
                     a = b
 
-    partner, row_halo, halo = partner_copies(), row_copies(), fine_copies()
-    for copy in loads:
+    row_halo, halo = row_copies(), fine_copies()
+    for copy in loads[:4]:
         copy.wait()
-    begin(row_halo)
-    for copy in partner:
-        copy.start()
     half = TILE // 2
     upper = rows_of((TILE, LANES)) >= half
 
@@ -433,20 +446,31 @@
             y = i * TILE + j
             for side, row in enumerate((TILE, TILE + l0.nz - half)):
                 send_z[side, y] = jnp.where(upper, stage_f[y, pl.ds(row - half, TILE)], stage_u[y, pl.ds(row, TILE)])
-    begin(halo)
+    begin(halo[4:])
+    for copy in loads[4:]:
+        copy.wait()
+    for part in range(PARTS):
+        for copy in partner_copies(part):
+            copy.start()
+    begin(row_halo)
+    begin(halo[:4])
     for offset in around_me:
         pl.semaphore_signal(ready, inc=1, device_id=peer(offset), device_id_type=MESH)
 
     step = 4
     some = reach // 3
-    for copy in partner:
-        copy.wait_recv()
-    for stage, buf, dst in ((stage_u, part_u, u0), (stage_f, part_f, f0)):
-        @pl.loop(0, reach // step)
-        def _(i, stage=stage, buf=buf, dst=dst):
+
+    @pl.loop(0, PARTS)
+    def _(part):
+        for copy in partner_copies(part):
+            copy.wait_recv()
+
+        @pl.loop(0, chunk // step)
+        def _(i):
             for j in range(step):
-                k = i * step + j
-                put(dst, l0.hx - cx * l0.wide + k, l0.own, split_x(stage[cx * (chip_y - reach) + k, inner], buf[k], cx))
+                k = part * chunk + i * step + j
+                for stage, buf, dst in ((stage_u, part_u, u0), (stage_f, part_f, f0)):
+                    put(dst, l0.hx - cx * l0.wide + k, l0.own, split_x(stage[cx * (chip_y - reach) + k, inner], buf[k], cx))
     arrive(row_halo)
     outer_plane = l0.hx - l0.wide + cx * reach
 
@@ -456,8 +480,9 @@
     arrive(halo)
     finish(row_halo)
     finish(halo)
-    for copy in partner:
-        copy.wait_send()
+    for part in range(PARTS):
+        for copy in partner_copies(part):
+            copy.wait_send()
 
     def put_rows(p, side, buf, k):
         row = l0.z0 + l0.nz if side else l0.z0 - half
@@ -626,7 +651,7 @@
     scratch += [vmem(3, lv.rows, LANES) for lv in (l0, l1, l2)]
     scratch += [vmem(2, chip_y, TILE, LANES), vmem(2, n_x, reach, TILE, LANES), vmem(2, 2, l0.wide, TILE, LANES)]
     scratch += [vmem(2, l0.wide, nz, LANES)] * 2
-    sems = [(2,), (2, l0.ny // 4), (16,), (16,), (2, len(SIDES)), (2, len(SIDES)), (total,), (total,)]
+    sems = [(10,), (2, l0.ny // 4), (16,), (16,), (2, len(SIDES)), (2, len(SIDES)), (total,), (total,), (PARTS, 2), (PARTS, 2)]
     scratch += [pltpu.SemaphoreType.DMA(shape) for shape in sems] + [pltpu.SemaphoreType.REGULAR]
     got = pl.pallas_call(
         functools.partial(kernel, cfg),

time: 53 us -> 51.2 us (0.966)
  Pallas kernels: 53 us -> 51.1 us
    pallas_call x1, Pallas kernels: 51.6 us -> 49.8 us  [local_cycle(): pl.pallas_call(functools.partial(kernel, cfg), out_shape=pltpu.VMEM(rhs.s...]
where the time goes in v6:
time: 51.2 us; the launch traced here: 51.1 us
  Pallas kernels  51.1 us (100%)
    pallas_call x1, Pallas kernels, local_cycle(): pl.pallas_call(functools.partial(kernel, cfg), out_shape=pltpu.VMEM(rhs.s...  49.8 us
    pallas_call x1, Pallas kernels, local_cycle(): pl.pallas_call(write_out, out_shape=jax.ShapeDtypeStruct(rhs.shape, F32),...  1.33 us

profile of v6, /device:TPU:97, one launch (start us, length us, event | category | flops | bytes accessed | tf_op | source)
XLA Modules:
  0.0 51.1 jit_solution(12900312560829708017)
XLA Ops:
  0.0 49.8 %shard_map.28.held = f32[64,64,128]{2,1,0:T(8,128)S(1)} custom-call(f32[64,64,128]{2,1,0:T(8,128)} %bitcast.3, f32[64,64,128]{2,1,0:T(8,128)} %bitcast.4), custom_call_target="tpu_custom_call" | custom-call | tf_op jit(solution)/shard_map/pallas_call | solution.py:656
  49.8 1.3 %shard_map.29 = f32[64,64,128]{2,1,0:T(8,128)} custom-call(f32[64,64,128]{2,1,0:T(8,128)S(1)} %shard_map.28.held), custom_call_target="tpu_custom_call" | custom-call | tf_op jit(solution)/shard_map/pallas_call | solution.py:664

commit v7 on v6

--- a/solution.py
+++ b/solution.py
@@ -285,22 +285,22 @@
 
     middle = LANES // 2
 
-    def lower(shape, core):
-        return lanes_of(shape) // middle == core
+    def towards(core):
+        return 1 + (LANES - 2) * core
 
     def split_x(first, second, core):
         lane = lanes_of(first.shape)
-        pair = 2 * (lane % middle)
-        first, second = pick(first, pair + (lane // middle + core) % 2), pick(second, pair + (lane // middle + 1 - core) % 2)
-        here = lower(first.shape, core)
-        return [jnp.where(here, first, second), roll(jnp.where(here, second, first), middle)]
-
-    def merge_x(even, odd, core):
-        lane = lanes_of(even.shape)
-        odd = roll(odd, middle)
-        here = lower(even.shape, core)
-        spot = lane // 2 + middle * ((lane + core) % 2)
-        return pick(jnp.where(here, even, odd), spot), pick(jnp.where(here, odd, even), (spot + middle) % LANES)
+        near, far = roll(second, towards(core)), roll(first, towards(1 - core))
+        spot = 2 * (lane % middle) + lane // middle
+        return [pick(jnp.where(lane % 2 == core, first, near), spot), pick(jnp.where(lane % 2 == core, far, second), spot)]
+
+    def merge_x(first, second, core):
+        lane = lanes_of(first.shape)
+        spot = lane // 2 + middle * (lane % 2)
+        first, second = pick(first, spot), pick(second, spot)
+        return (jnp.where(lane % 2 == core, first, roll(second, towards(core))),
+                jnp.where(lane % 2 == core, roll(first, towards(1 - core)), second))
+
     pl.semaphore_wait(barrier, len(around_me))
 
     def across(c, lv):
@@ -470,7 +470,8 @@
             for j in range(step):
                 k = part * chunk + i * step + j
                 for stage, buf, dst in ((stage_u, part_u, u0), (stage_f, part_f, f0)):
-                    put(dst, l0.hx - cx * l0.wide + k, l0.own, split_x(stage[cx * (chip_y - reach) + k, inner], buf[k], cx))
+                    p = l0.hx - cx * l0.wide + k
+                    dst[p, cx, l0.own], dst[p, 1 - cx, l0.own] = split_x(stage[cx * (chip_y - reach) + k, inner], buf[k], cx)
     arrive(row_halo)
     outer_plane = l0.hx - l0.wide + cx * reach
 
@@ -611,6 +612,7 @@
             c = get(v0, p, l0.own, l0)
             around = neighbours(v0, p, get(v0, p - 1, l0.own, l0), c, get(v0, p + 1, l0.own, l0), l0, l0.z0, l0.nz)
             got = every(lambda x, y, g: (x + 3.0 * y + g) * (NINTH / cfg.stiffness), around, c, get(f0, p, l0.own, l0))
+            got = [jnp.where(cx == 0, got[0], got[1]), jnp.where(cx == 0, got[1], got[0])]
             out[cx * l0.ny + k], stage_f[k, inner] = merge_x(*got, cx)
         results(i).start()
 

time: 51.2 us -> 53 us (1.035)
  Pallas kernels: 51.1 us -> 52.9 us
    pallas_call x1, Pallas kernels: 49.8 us -> 51.5 us  [local_cycle(): pl.pallas_call(functools.partial(kernel, cfg), out_shape=pltpu.VMEM(rhs.s...]
where the time goes in v7:
time: 53 us; the launch traced here: 52.9 us
  Pallas kernels  52.9 us (100%)
    pallas_call x1, Pallas kernels, local_cycle(): pl.pallas_call(functools.partial(kernel, cfg), out_shape=pltpu.VMEM(rhs.s...  51.5 us
    pallas_call x1, Pallas kernels, local_cycle(): pl.pallas_call(write_out, out_shape=jax.ShapeDtypeStruct(rhs.shape, F32),...  1.33 us

profile of v7, /device:TPU:97, one launch (start us, length us, event | category | flops | bytes accessed | tf_op | source)
XLA Modules:
  0.0 52.9 jit_solution(6679013214167764532)
XLA Ops:
  0.0 51.5 %shard_map.28.held = f32[64,64,128]{2,1,0:T(8,128)S(1)} custom-call(f32[64,64,128]{2,1,0:T(8,128)} %bitcast.3, f32[64,64,128]{2,1,0:T(8,128)} %bitcast.4), custom_call_target="tpu_custom_call" | custom-call | tf_op jit(solution)/shard_map/pallas_call | solution.py:658
  51.6 1.3 %shard_map.29 = f32[64,64,128]{2,1,0:T(8,128)} custom-call(f32[64,64,128]{2,1,0:T(8,128)S(1)} %shard_map.28.held), custom_call_target="tpu_custom_call" | custom-call | tf_op jit(solution)/shard_map/pallas_call | solution.py:666

commit v8 on v6

--- a/solution.py
+++ b/solution.py
@@ -94,7 +94,7 @@
 
 
 def kernel(cfg, rhs, start, out, *scratch):
-    (u0, v0, f0, a1, b1, g1, a2, b2, g2, e3, pz, pb, stage_u, stage_f, part_u, part_f, s3, g3, slots, message, mask0, mask1, mask2,
+    (u0, v0, f0, a1, b1, g1, a2, b2, g2, e3, pz, pb, stage_u, stage_f, part_u, part_f, sorted_u, sorted_f, edge_u, edge_f, s3, g3, slots, message, mask0, mask1, mask2,
      send_z, recv_z, recv_d, recv_yu, recv_yf,
      load_sem, out_sem, fine_s, fine_r, send_sem, recv_sem, all_s, all_r, part_s, part_r, ready) = scratch
     l0, l1, l2 = levels = cfg.levels
@@ -211,12 +211,11 @@
     def row_copies():
         got = []
         for y_side, y_step in enumerate((-1, 1)):
-            edge = pl.ds(0 if y_step < 0 else chip_y - l0.wide, l0.wide)
-            for k, (stage, buf) in enumerate(((stage_u, recv_yu), (stage_f, recv_yf))):
+            for k, (edges, buf) in enumerate(((edge_u, recv_yu), (edge_f, recv_yf))):
                 made = [pltpu.make_async_remote_copy(
                     src_ref=a, dst_ref=b, send_sem=fine_s.at[8 + 2 * y_side + k], recv_sem=fine_r.at[2 * r + k],
                     device_id={'sx': 1 - y_side, 'sy': cy + y_step}, device_id_type=MESH)
-                    for a, b, r in ((stage.at[edge, inner], buf.at[cx], cx), (buf.at[y_side], buf.at[y_side], y_side))]
+                    for a, b, r in ((edges.at[y_side], buf.at[cx], cx), (buf.at[y_side], buf.at[y_side], y_side))]
                 got.append((inside(y_step, cy, n_y), has_outer, *made))
         return got
 
@@ -225,9 +224,9 @@
     def partner_copies(part):
         other = pl.ds((1 - cx) * (chip_y - reach) + part * chunk, chunk)
         return [pltpu.make_async_remote_copy(
-            src_ref=stage.at[other, inner], dst_ref=buf.at[pl.ds(part * chunk, chunk)], send_sem=part_s.at[part, k],
+            src_ref=src.at[other], dst_ref=buf.at[pl.ds(part * chunk, chunk)], send_sem=part_s.at[part, k],
             recv_sem=part_r.at[part, k], device_id={'sx': 1 - cx}, device_id_type=MESH)
-            for k, (stage, buf) in enumerate(((stage_u, part_u), (stage_f, part_f)))]
+            for k, (src, buf) in enumerate(((sorted_u, part_u), (sorted_f, part_f)))]
 
     def begin(copies):
         for sends, _, copy, _ in copies:
@@ -285,22 +284,19 @@
 
     middle = LANES // 2
 
-    def lower(shape, core):
-        return lanes_of(shape) // middle == core
+    def sort_x(x):
+        lane = lanes_of(x.shape)
+        return pick(x, 2 * (lane % middle) + (lane // middle + cx) % 2)
 
     def split_x(first, second, core):
-        lane = lanes_of(first.shape)
-        pair = 2 * (lane % middle)
-        first, second = pick(first, pair + (lane // middle + core) % 2), pick(second, pair + (lane // middle + 1 - core) % 2)
-        here = lower(first.shape, core)
+        here = lanes_of(first.shape) // middle == core
         return [jnp.where(here, first, second), roll(jnp.where(here, second, first), middle)]
 
     def merge_x(even, odd, core):
-        lane = lanes_of(even.shape)
+        here = lanes_of(even.shape) // middle == core
         odd = roll(odd, middle)
-        here = lower(even.shape, core)
-        spot = lane // 2 + middle * ((lane + core) % 2)
-        return pick(jnp.where(here, even, odd), spot), pick(jnp.where(here, odd, even), (spot + middle) % LANES)
+        return jnp.where(here, even, odd), jnp.where(here, odd, even)
+
     pl.semaphore_wait(barrier, len(around_me))
 
     def across(c, lv):
@@ -445,19 +441,36 @@
         for j in range(TILE):
             y = i * TILE + j
             for side, row in enumerate((TILE, TILE + l0.nz - half)):
-                send_z[side, y] = jnp.where(upper, stage_f[y, pl.ds(row - half, TILE)], stage_u[y, pl.ds(row, TILE)])
+                send_z[side, y] = sort_x(jnp.where(upper, stage_f[y, pl.ds(row - half, TILE)], stage_u[y, pl.ds(row, TILE)]))
     begin(halo[4:])
     for copy in loads[4:]:
         copy.wait()
-    for part in range(PARTS):
+    step = 4
+
+    for side, plane in enumerate((0, chip_y - l0.wide)):
+        for j in range(l0.wide):
+            edge_u[side, j] = sort_x(stage_u[plane + j, inner])
+            edge_f[side, j] = sort_x(stage_f[plane + j, inner])
+    begin(row_halo)
+
+    def sort_planes(first, n):
+        @pl.loop(0, n // step)
+        def _(i):
+            for j in range(step):
+                y = first + i * step + j
+                sorted_u[y] = sort_x(stage_u[y, inner])
+                sorted_f[y] = sort_x(stage_f[y, inner])
+
+    @pl.loop(0, PARTS)
+    def _(part):
+        sort_planes((1 - cx) * (chip_y - reach) + part * chunk, chunk)
         for copy in partner_copies(part):
             copy.start()
-    begin(row_halo)
     begin(halo[:4])
+    sort_planes(cx * reach, chip_y - reach)
     for offset in around_me:
         pl.semaphore_signal(ready, inc=1, device_id=peer(offset), device_id_type=MESH)
 
-    step = 4
     some = reach // 3
 
     @pl.loop(0, PARTS)
@@ -469,8 +482,8 @@
         def _(i):
             for j in range(step):
                 k = part * chunk + i * step + j
-                for stage, buf, dst in ((stage_u, part_u, u0), (stage_f, part_f, f0)):
-                    put(dst, l0.hx - cx * l0.wide + k, l0.own, split_x(stage[cx * (chip_y - reach) + k, inner], buf[k], cx))
+                for src, buf, dst in ((sorted_u, part_u, u0), (sorted_f, part_f, f0)):
+                    put(dst, l0.hx - cx * l0.wide + k, l0.own, split_x(src[cx * (chip_y - reach) + k], buf[k], cx))
     arrive(row_halo)
     outer_plane = l0.hx - l0.wide + cx * reach
 
@@ -624,9 +637,22 @@
         gather_copy(k, slot).wait_send()
 
 
-def write_out(held, out, sem):
-    pltpu.make_async_copy(held, out, sem).start()
-    pltpu.make_async_copy(held, out, sem).wait()
+def write_out(held, out, rows, sem):
+    def copy_out(i):
+        planes = pl.ds(i * TILE, TILE)
+        return pltpu.make_async_copy(rows.at[planes], out.at[planes], sem.at[i])
+
+    @pl.loop(0, held.shape[0] // TILE)
+    def _(i):
+        for j in range(TILE):
+            x = held[i * TILE + j]
+            lane = lanes_of(x.shape)
+            rows[i * TILE + j] = pick(x, lane // 2 + LANES // 2 * ((lane + lax.axis_index('sx')) % 2))
+        copy_out(i).start()
+
+    @pl.loop(0, held.shape[0] // TILE)
+    def _(i):
+        copy_out(i).wait()
 
 
 def local_cycle(rhs, start, counts, size):
@@ -646,7 +672,8 @@
     scratch = [vmem(lv.planes, lv.parts, lv.depth, LANES) for lv in (l0, l1, l2) for _ in range(3)]
     reach = l0.ny + l0.wide
     scratch += [vmem(12, 1, 3 * TILE, LANES), vmem(l1.ny + 8, l1.rows, LANES), vmem(2, l1.ny + 8, l0.depth, LANES)]
-    scratch += [vmem(chip_y, l0.depth, LANES)] * 2 + [vmem(reach, nz, LANES)] * 2
+    scratch += [vmem(chip_y, l0.depth, LANES)] * 2 + [vmem(reach, nz, LANES)] * 2 + [vmem(chip_y, nz, LANES)] * 2
+    scratch += [vmem(2, l0.wide, nz, LANES)] * 2
     scratch += [vmem(2, TILE, l2.nz // 2 * n_z + 2 * TILE, LANES), vmem(TILE, l2.nz // 2 * n_z + 2 * TILE, LANES), vmem(total, TILE, LANES), vmem(TILE, LANES)]
     scratch += [vmem(3, lv.rows, LANES) for lv in (l0, l1, l2)]
     scratch += [vmem(2, chip_y, TILE, LANES), vmem(2, n_x, reach, TILE, LANES), vmem(2, 2, l0.wide, TILE, LANES)]
@@ -666,7 +693,7 @@
         out_shape=jax.ShapeDtypeStruct(rhs.shape, F32),
         in_specs=[pl.BlockSpec(memory_space=pltpu.VMEM)],
         out_specs=pl.BlockSpec(memory_space=pl.ANY),
-        scratch_shapes=[pltpu.SemaphoreType.DMA],
+        scratch_shapes=[vmem(*rhs.shape), pltpu.SemaphoreType.DMA((chip_y // TILE,))],
     )(pltpu.with_memory_space_constraint(got, pltpu.VMEM))
     return jnp.transpose(got, (2, 0, 1))
 

time: 51.2 us -> 51 us (level)
    pallas_call x1, Pallas kernels: 49.8 us -> 48.9 us  [local_cycle(): pl.pallas_call(functools.partial(kernel, cfg), out_shape=pltpu.VMEM(rhs.s...]
    pallas_call x1, Pallas kernels: 1.33 us -> 2.01 us  [local_cycle(): pl.pallas_call(write_out, out_shape=jax.ShapeDtypeStruct(rhs.shape, F32),...]
where the time goes in v8:
time: 51 us; the launch traced here: 50.9 us
  Pallas kernels  50.9 us (100%)
    pallas_call x1, Pallas kernels, local_cycle(): pl.pallas_call(functools.partial(kernel, cfg), out_shape=pltpu.VMEM(rhs.s...  48.9 us
    pallas_call x1, Pallas kernels, local_cycle(): pl.pallas_call(write_out, out_shape=jax.ShapeDtypeStruct(rhs.shape, F32),...  2.01 us

profile of v8, /device:TPU:97, one launch (start us, length us, event | category | flops | bytes accessed | tf_op | source)
XLA Modules:
  0.0 50.9 jit_solution(8182767779746096362)
XLA Ops:
  0.0 48.9 %shard_map.28.held = f32[64,64,128]{2,1,0:T(8,128)S(1)} custom-call(f32[64,64,128]{2,1,0:T(8,128)} %bitcast.3, f32[64,64,128]{2,1,0:T(8,128)} %bitcast.4), custom_call_target="tpu_custom_call" | custom-call | tf_op jit(solution)/shard_map/pallas_call | solution.py:683
  48.9 2.0 %shard_map.29 = f32[64,64,128]{2,1,0:T(8,128)} custom-call(f32[64,64,128]{2,1,0:T(8,128)S(1)} %shard_map.28.held), custom_call_target="tpu_custom_call" | custom-call | tf_op jit(solution)/shard_map/pallas_call | solution.py:691

commit v9 on v8

--- a/solution.py
+++ b/solution.py
@@ -28,8 +28,13 @@
     lv.parts = max(nx // LANES, 1)
     lv.own = pl.ds(z0, nz)
     lv.all = pl.ds(top, rows)
-    lv.blocks = [(top + i, min(block, rows - i)) for i in range(0, rows, block)]
+    lv.block = block
+    lv.blocks = cut(lv, top, rows)
     return lv
+
+
+def cut(lv, top, rows):
+    return [(top + i, min(lv.block, rows - i)) for i in range(0, rows, lv.block)]
 
 
 def lanes_of(shape):
@@ -94,7 +99,7 @@
 
 
 def kernel(cfg, rhs, start, out, *scratch):
-    (u0, v0, f0, a1, b1, g1, a2, b2, g2, e3, pz, pb, stage_u, stage_f, part_u, part_f, sorted_u, sorted_f, edge_u, edge_f, s3, g3, slots, message, mask0, mask1, mask2,
+    (u0, v0, f0, w0, a1, b1, g1, a2, b2, g2, e3, pz, pb, stage_u, stage_f, part_u, part_f, sorted_u, sorted_f, edge_u, edge_f, s3, g3, slots, message, mask0, mask1, mask2,
      send_z, recv_z, recv_d, recv_yu, recv_yf,
      load_sem, out_sem, fine_s, fine_r, send_sem, recv_sem, all_s, all_r, part_s, part_r, ready) = scratch
     l0, l1, l2 = levels = cfg.levels
@@ -263,7 +268,7 @@
             def _(index=index, d=d):
                 zero(region(index, d, False))
 
-    for lv, arrays in ((l0, (u0, v0)), (l1, (a1, b1)), (l2, (a2, b2))):
+    for lv, arrays in ((l0, (u0, v0, w0)), (l1, (a1, b1)), (l2, (a2, b2))):
         for arr in arrays:
             for plane, outside in ((lv.hx - 1, yb == 0), (lv.hx + lv.ny, yb == row_blocks - 1)):
                 @pl.when(outside)
@@ -314,11 +319,11 @@
     def table_rows(table, k, lv, top, n):
         return table[k, pl.ds(top - lv.top, n)]
 
-    def sweep(src, dst, rhs_ref, lv, table, scale=None):
-        @pl.loop(0, lv.count)
+    def sweep(src, dst, rhs_ref, lv, table, scale=None, blocks=None, first=None, count=None):
+        @pl.loop(0, count or lv.count)
         def _(g):
-            base = lv.begin + g * lv.group
-            for top, n in lv.blocks:
+            base = (lv.begin if first is None else first) + g * lv.group
+            for top, n in blocks or lv.blocks:
                 rows = pl.ds(top, n)
                 xm, c = get(src, base - 1, rows, lv), get(src, base, rows, lv)
                 for j in range(lv.group):
@@ -484,6 +489,9 @@
                 k = part * chunk + i * step + j
                 for src, buf, dst in ((sorted_u, part_u, u0), (sorted_f, part_f, f0)):
                     put(dst, l0.hx - cx * l0.wide + k, l0.own, split_x(src[cx * (chip_y - reach) + k], buf[k], cx))
+    stages = ((u0, v0, cfg.stiffness), (v0, w0, None))
+    for k, (src, dst, scale) in enumerate(stages):
+        sweep(src, dst, f0, l0, mask0, scale, cut(l0, l0.z0 + k + 1, l0.nz - 2 * (k + 1)))
     arrive(row_halo)
     outer_plane = l0.hx - l0.wide + cx * reach
 
@@ -511,9 +519,11 @@
     for side in range(2):
         for j in range(l0.wide):
             put_rows(outer_plane + j, side, recv_d.at[side], j)
-    sweep(u0, v0, f0, l0, mask0, cfg.stiffness)
-    sweep(v0, u0, f0, l0, mask0)
-    restrict_level(u0, f0, l0, mask0, g1, l1, 4, 4)
+    for k, (src, dst, scale) in enumerate(stages):
+        ring = l0.wide + 1
+        sweep(src, dst, f0, l0, mask0, scale, [(l0.top + k, ring), (l0.z0 + l0.nz - 1 - k, ring)])
+        sweep(src, dst, f0, l0, mask0, scale, first=l0.begin + cx * l0.ny, count=1)
+    restrict_level(w0, f0, l0, mask0, g1, l1, 4, 4)
 
     exchange(1)
     first_sweep(a1, g1, l1, mask1)
@@ -607,8 +617,8 @@
     sweep(b1, a1, g1, l1, mask1)
     sweep(a1, b1, g1, l1, mask1)
     prolong_planes(b1, l1.hx + (l0.begin - l0.hx) // 2, l1.z0, l1.top, l1.rows, l1.nx, 8, 3, l0)
-    correct(u0, l0, mask0, 4)
-    sweep(u0, v0, f0, l0, mask0)
+    correct(w0, l0, mask0, 4)
+    sweep(w0, v0, f0, l0, mask0)
 
     def results(i):
         here, there = pl.ds(i * step, step), pl.ds(cx * l0.ny + i * step, step)
@@ -660,8 +670,8 @@
     n_x, n_y, n_z = counts
     chip_y, nz, nx = rhs.shape
     shapes = [(chip_y // n_x >> k, nz >> k, nx * n_x >> k) for k in range(3)]
-    l0 = make_level(shapes[0], 6, 8, 4, nz + 8, 2, 8, (shapes[0][0] + 8) // 8, 4, 24)
-    l1 = make_level(shapes[1], 8, 16, 8, shapes[1][1] + 16, 2, 14, (shapes[1][0] + 12) // 14, 5, 24)
+    l0 = make_level(shapes[0], 6, 8, 4, nz + 8, 2, 8, (shapes[0][0] + 8) // 8, 4, nz + 8)
+    l1 = make_level(shapes[1], 8, 16, 8, shapes[1][1] + 16, 2, 14, (shapes[1][0] + 12) // 14, 5, 48)
     l2 = make_level(shapes[2], 8, 16, 8, shapes[2][1] + 16, 2, 10, (shapes[2][0] + 12) // 10, 6, 32)
     cfg = types.SimpleNamespace(levels=(l0, l1, l2), counts=counts, stiffness=float((size + 1) ** 2))
     total = n_x * n_y * n_z
@@ -669,7 +679,7 @@
     def vmem(*shape):
         return pltpu.VMEM(shape, F32)
 
-    scratch = [vmem(lv.planes, lv.parts, lv.depth, LANES) for lv in (l0, l1, l2) for _ in range(3)]
+    scratch = [vmem(lv.planes, lv.parts, lv.depth, LANES) for lv, n in ((l0, 4), (l1, 3), (l2, 3)) for _ in range(n)]
     reach = l0.ny + l0.wide
     scratch += [vmem(12, 1, 3 * TILE, LANES), vmem(l1.ny + 8, l1.rows, LANES), vmem(2, l1.ny + 8, l0.depth, LANES)]
     scratch += [vmem(chip_y, l0.depth, LANES)] * 2 + [vmem(reach, nz, LANES)] * 2 + [vmem(chip_y, nz, LANES)] * 2

time: 51 us -> 50.2 us (0.984)
  Pallas kernels: 50.9 us -> 50.1 us
    pallas_call x1, Pallas kernels: 48.9 us -> 48.1 us  [local_cycle(): pl.pallas_call(functools.partial(kernel, cfg), out_shape=pltpu.VMEM(rhs.s...]
where the time goes in v9:
time: 50.2 us; the launch traced here: 50.1 us
  Pallas kernels  50.1 us (100%)
    pallas_call x1, Pallas kernels, local_cycle(): pl.pallas_call(functools.partial(kernel, cfg), out_shape=pltpu.VMEM(rhs.s...  48.1 us
    pallas_call x1, Pallas kernels, local_cycle(): pl.pallas_call(write_out, out_shape=jax.ShapeDtypeStruct(rhs.shape, F32),...  2.01 us

profile of v9, /device:TPU:97, one launch (start us, length us, event | category | flops | bytes accessed | tf_op | source)
XLA Modules:
  0.0 50.1 jit_solution(16977377384536665343)
XLA Ops:
  0.0 48.1 %shard_map.28.held = f32[64,64,128]{2,1,0:T(8,128)S(1)} custom-call(f32[64,64,128]{2,1,0:T(8,128)} %bitcast.3, f32[64,64,128]{2,1,0:T(8,128)} %bitcast.4), custom_call_target="tpu_custom_call" | custom-call | tf_op jit(solution)/shard_map/pallas_call | solution.py:693
  48.1 2.0 %shard_map.29 = f32[64,64,128]{2,1,0:T(8,128)} custom-call(f32[64,64,128]{2,1,0:T(8,128)S(1)} %shard_map.28.held), custom_call_target="tpu_custom_call" | custom-call | tf_op jit(solution)/shard_map/pallas_call | solution.py:701

commit v10 on v9

--- a/solution.py
+++ b/solution.py
@@ -319,14 +319,16 @@
     def table_rows(table, k, lv, top, n):
         return table[k, pl.ds(top - lv.top, n)]
 
-    def sweep(src, dst, rhs_ref, lv, table, scale=None, blocks=None, first=None, count=None):
+    def sweep(src, dst, rhs_ref, lv, table, scale=None, blocks=None, first=None, count=None, group=None):
+        group = group or lv.group
+
         @pl.loop(0, count or lv.count)
         def _(g):
-            base = (lv.begin if first is None else first) + g * lv.group
+            base = (lv.begin if first is None else first) + g * group
             for top, n in blocks or lv.blocks:
                 rows = pl.ds(top, n)
                 xm, c = get(src, base - 1, rows, lv), get(src, base, rows, lv)
-                for j in range(lv.group):
+                for j in range(group):
                     p = base + j
                     xp = get(src, p + 1, rows, lv)
                     t = every(lambda a, b: a + 3.0 * b, neighbours(src, p, xm, c, xp, lv, top, n), c)
@@ -441,12 +443,15 @@
     half = TILE // 2
     upper = rows_of((TILE, LANES)) >= half
 
-    @pl.loop(0, chip_y // TILE)
+    batch = chip_y // 2
+    many = rows_of((batch * TILE, LANES)) % TILE >= half
+
+    @pl.loop(0, chip_y // batch)
     def _(i):
-        for j in range(TILE):
-            y = i * TILE + j
-            for side, row in enumerate((TILE, TILE + l0.nz - half)):
-                send_z[side, y] = sort_x(jnp.where(upper, stage_f[y, pl.ds(row - half, TILE)], stage_u[y, pl.ds(row, TILE)]))
+        planes = pl.ds(i * batch, batch)
+        for side, row in enumerate((TILE, TILE + l0.nz - half)):
+            f, u = (x.reshape(batch * TILE, LANES) for x in (stage_f[planes, pl.ds(row - half, TILE)], stage_u[planes, pl.ds(row, TILE)]))
+            send_z[side, planes] = sort_x(jnp.where(many, f, u)).reshape(batch, TILE, LANES)
     begin(halo[4:])
     for copy in loads[4:]:
         copy.wait()
@@ -521,7 +526,7 @@
             put_rows(outer_plane + j, side, recv_d.at[side], j)
     for k, (src, dst, scale) in enumerate(stages):
         ring = l0.wide + 1
-        sweep(src, dst, f0, l0, mask0, scale, [(l0.top + k, ring), (l0.z0 + l0.nz - 1 - k, ring)])
+        sweep(src, dst, f0, l0, mask0, scale, [(l0.top + k, ring), (l0.z0 + l0.nz - 1 - k, ring)], count=2, group=20)
         sweep(src, dst, f0, l0, mask0, scale, first=l0.begin + cx * l0.ny, count=1)
     restrict_level(w0, f0, l0, mask0, g1, l1, 4, 4)
 
@@ -648,19 +653,21 @@
 
 
 def write_out(held, out, rows, sem):
+    batch = 2 * TILE
+
     def copy_out(i):
-        planes = pl.ds(i * TILE, TILE)
+        planes = pl.ds(i * batch, batch)
         return pltpu.make_async_copy(rows.at[planes], out.at[planes], sem.at[i])
 
-    @pl.loop(0, held.shape[0] // TILE)
+    @pl.loop(0, held.shape[0] // batch)
     def _(i):
-        for j in range(TILE):
-            x = held[i * TILE + j]
+        for j in range(batch):
+            x = held[i * batch + j]
             lane = lanes_of(x.shape)
-            rows[i * TILE + j] = pick(x, lane // 2 + LANES // 2 * ((lane + lax.axis_index('sx')) % 2))
+            rows[i * batch + j] = pick(x, lane // 2 + LANES // 2 * ((lane + lax.axis_index('sx')) % 2))
         copy_out(i).start()
 
-    @pl.loop(0, held.shape[0] // TILE)
+    @pl.loop(0, held.shape[0] // batch)
     def _(i):
         copy_out(i).wait()
 

time: 50.2 us -> 49.1 us (0.978)
  Pallas kernels: 50.1 us -> 49.1 us
    pallas_call x1, Pallas kernels: 48.1 us -> 47.3 us  [local_cycle(): pl.pallas_call(functools.partial(kernel, cfg), out_shape=pltpu.VMEM(rhs.s...]
where the time goes in v10:
time: 49.1 us
  Pallas kernels  49.1 us (100%)
    pallas_call x1, Pallas kernels, local_cycle(): pl.pallas_call(functools.partial(kernel, cfg), out_shape=pltpu.VMEM(rhs.s...  47.3 us
    pallas_call x1, Pallas kernels, local_cycle(): pl.pallas_call(write_out, out_shape=jax.ShapeDtypeStruct(rhs.shape, F32),...  1.75 us

profile of v10, /device:TPU:97, one launch (start us, length us, event | category | flops | bytes accessed | tf_op | source)
XLA Modules:
  0.0 49.1 jit_solution(15272297639054810374)
XLA Ops:
  0.0 47.3 %shard_map.28.held = f32[64,64,128]{2,1,0:T(8,128)S(1)} custom-call(f32[64,64,128]{2,1,0:T(8,128)} %bitcast.3, f32[64,64,128]{2,1,0:T(8,128)} %bitcast.4), custom_call_target="tpu_custom_call" | custom-call | tf_op jit(solution)/shard_map/pallas_call | solution.py:700
  47.3 1.8 %shard_map.29 = f32[64,64,128]{2,1,0:T(8,128)} custom-call(f32[64,64,128]{2,1,0:T(8,128)S(1)} %shard_map.28.held), custom_call_target="tpu_custom_call" | custom-call | tf_op jit(solution)/shard_map/pallas_call | solution.py:708

commit v11 on v10

--- a/solution.py
+++ b/solution.py
@@ -49,12 +49,17 @@
     return pltpu.roll(x, shift, 1)
 
 
-def from_below(x):
-    return jnp.where(lanes_of(x.shape) == 0, 0.0, roll(x, 1))
-
-
-def from_above(x):
-    return jnp.where(lanes_of(x.shape) == LANES - 1, 0.0, roll(x, LANES - 1))
+def ends(n):
+    lane = lanes_of((n, LANES))
+    return lane == 0, lane == LANES - 1, jnp.zeros((n, LANES), F32)
+
+
+def from_below(x, outer):
+    return lax.select(outer[0], outer[2], roll(x, 1))
+
+
+def from_above(x, outer):
+    return lax.select(outer[1], outer[2], roll(x, LANES - 1))
 
 
 def halves(x):
@@ -174,7 +179,7 @@
             device_id={'sx': at % n_x, 'sy': at // n_x, 'sz': cz + STEP_Z[d]}, device_id_type=MESH)
 
     def each(act):
-        for d in (4, 5, 6, 7, 2, 3, 0, 1):
+        for d in (2, 3, 4, 5, 6, 7, 0, 1):
             @pl.when(exists(d))
             def _(d=d):
                 act(d)
@@ -304,34 +309,35 @@
 
     pl.semaphore_wait(barrier, len(around_me))
 
-    def across(c, lv):
+    def across(c, lv, outer):
         if lv.parts > 1:
             even, odd = c
-            return [odd + from_below(odd), even + from_above(even)]
+            return [odd + from_below(odd, outer), even + from_above(even, outer)]
         if lv.nx == LANES:
-            return [from_below(c[0]) + from_above(c[0])]
+            return [from_below(c[0], outer) + from_above(c[0], outer)]
         return [roll(c[0], 1) + roll(c[0], LANES - 1)]
 
-    def neighbours(src, p, xm, c, xp, lv, top, n):
+    def neighbours(src, p, xm, c, xp, lv, top, n, outer):
         zm, zp = get(src, p, pl.ds(top - 1, n), lv), get(src, p, pl.ds(top + 1, n), lv)
-        return every(lambda a, b, d, e, f: ((a + b) + (d + e)) + f, xm, xp, zm, zp, across(c, lv))
+        return every(lambda a, b, d, e, f: ((a + b) + (d + e)) + f, xm, xp, zm, zp, across(c, lv, outer))
 
     def table_rows(table, k, lv, top, n):
         return table[k, pl.ds(top - lv.top, n)]
 
     def sweep(src, dst, rhs_ref, lv, table, scale=None, blocks=None, first=None, count=None, group=None):
-        group = group or lv.group
+        group, blocks = group or lv.group, blocks or lv.blocks
+        outers = {n: ends(n) for _, n in blocks}
 
         @pl.loop(0, count or lv.count)
         def _(g):
             base = (lv.begin if first is None else first) + g * group
-            for top, n in blocks or lv.blocks:
+            for top, n in blocks:
                 rows = pl.ds(top, n)
                 xm, c = get(src, base - 1, rows, lv), get(src, base, rows, lv)
                 for j in range(group):
                     p = base + j
                     xp = get(src, p + 1, rows, lv)
-                    t = every(lambda a, b: a + 3.0 * b, neighbours(src, p, xm, c, xp, lv, top, n), c)
+                    t = every(lambda a, b: a + 3.0 * b, neighbours(src, p, xm, c, xp, lv, top, n, outers[n]), c)
                     if scale is not None:
                         t = [x * scale for x in t]
                     keep = table_rows(table, 2 * valid(lv, p), lv, top, n)
@@ -346,8 +352,10 @@
                 dst[p, 0, lv.all] = rhs_ref[p, 0, lv.all] * table[2 * valid(lv, p)]
 
     def restrict_planes(src, rhs_ref, lv, table, group):
+        outers = {n: ends(n) for _, n in lv.blocks}
+
         def res(p, xm, c, xp, top, n):
-            return every(lambda a, b, d: a + b - 6.0 * d, neighbours(src, p, xm, c, xp, lv, top, n), get(rhs_ref, p, pl.ds(top, n), lv), c)
+            return every(lambda a, b, d: a + b - 6.0 * d, neighbours(src, p, xm, c, xp, lv, top, n, outers[n]), get(rhs_ref, p, pl.ds(top, n), lv), c)
 
         @pl.loop(0, lv.ny // 2 // group)
         def _(i):
@@ -380,6 +388,7 @@
     def restrict_level(src, rhs_ref, lv, table, coarse_rhs, coarse, group, step):
         restrict_planes(src, rhs_ref, lv, table, group)
         lane = lanes_of(square)
+        outer = ends(coarse.nz)
         w = jnp.where(lane < coarse.nx, weights(rows_of(square) - 2 * lane, 2.0 * eighth, eighth), 0.0)
 
         @pl.loop(0, coarse.ny // step)
@@ -387,7 +396,7 @@
             got = [restricted_rows(i * step + j, lv) for j in range(step)]
             if lv.parts > 1:
                 odds = [restricted_rows(i * step + j, lv, 1) for j in range(step)]
-                got = [((odd + from_below(odd)) + 2.0 * even) * eighth for even, odd in zip(got, odds)]
+                got = [((odd + from_below(odd, outer)) + 2.0 * even) * eighth for even, odd in zip(got, odds)]
             else:
                 got = dot(stack(got), w)
                 got = [got[j * coarse.nz:(j + 1) * coarse.nz] for j in range(step)]
@@ -421,7 +430,8 @@
     def correct(dst, lv, table, pairs):
         def load(at, rows):
             a = pb[0, at, rows]
-            return [a, 0.5 * (a + from_above(a))] if lv.parts > 1 else [a]
+            return [a, 0.5 * (a + from_above(a, outers[a.shape[0]]))] if lv.parts > 1 else [a]
+        outers = {n: ends(n) for _, n in lv.blocks}
 
         @pl.loop(0, lv.group * lv.count // (2 * pairs))
         def _(i):
@@ -528,7 +538,7 @@
         ring = l0.wide + 1
         sweep(src, dst, f0, l0, mask0, scale, [(l0.top + k, ring), (l0.z0 + l0.nz - 1 - k, ring)], count=2, group=20)
         sweep(src, dst, f0, l0, mask0, scale, first=l0.begin + cx * l0.ny, count=1)
-    restrict_level(w0, f0, l0, mask0, g1, l1, 4, 4)
+    restrict_level(w0, f0, l0, mask0, g1, l1, 4, 8)
 
     exchange(1)
     first_sweep(a1, g1, l1, mask1)
@@ -613,11 +623,11 @@
         ok = (lanes_of(c.shape) < width) & (y >= 0) & (y < row_blocks * ny3)
         e3[i, 0] = jnp.where(ok, roll(c, back((y + TILE) // TILE * width + LANES - width)), 0.0)
 
-    prolong_planes(e3, 0, TILE, 0, 3 * TILE, width, 6, 2, l2)
+    prolong_planes(e3, 0, TILE, 0, 3 * TILE, width, 12, 1, l2)
     correct(b2, l2, mask2, 5)
     sweep(b2, a2, g2, l2, mask2)
     sweep(a2, b2, g2, l2, mask2)
-    prolong_planes(b2, l2.hx + (l1.begin - l1.hx) // 2, l2.z0, l2.top, l2.rows, l2.nx, 8, 2, l1)
+    prolong_planes(b2, l2.hx + (l1.begin - l1.hx) // 2, l2.z0, l2.top, l2.rows, l2.nx, 16, 1, l1)
     correct(b1, l1, mask1, 7)
     sweep(b1, a1, g1, l1, mask1)
     sweep(a1, b1, g1, l1, mask1)
@@ -631,13 +641,15 @@
             src_ref=stage_f.at[here, inner], dst_ref=out.at[there], send_sem=out_sem.at[0, i], recv_sem=out_sem.at[1, i],
             device_id={'sx': 1 - cx}, device_id_type=MESH)
 
+    outer_lanes = ends(l0.nz)
+
     @pl.loop(0, l0.ny // step)
     def _(i):
         for j in range(step):
             k = i * step + j
             p = l0.hx + k
             c = get(v0, p, l0.own, l0)
-            around = neighbours(v0, p, get(v0, p - 1, l0.own, l0), c, get(v0, p + 1, l0.own, l0), l0, l0.z0, l0.nz)
+            around = neighbours(v0, p, get(v0, p - 1, l0.own, l0), c, get(v0, p + 1, l0.own, l0), l0, l0.z0, l0.nz, outer_lanes)
             got = every(lambda x, y, g: (x + 3.0 * y + g) * (NINTH / cfg.stiffness), around, c, get(f0, p, l0.own, l0))
             out[cx * l0.ny + k], stage_f[k, inner] = merge_x(*got, cx)
         results(i).start()
@@ -679,7 +691,7 @@
     shapes = [(chip_y // n_x >> k, nz >> k, nx * n_x >> k) for k in range(3)]
     l0 = make_level(shapes[0], 6, 8, 4, nz + 8, 2, 8, (shapes[0][0] + 8) // 8, 4, nz + 8)
     l1 = make_level(shapes[1], 8, 16, 8, shapes[1][1] + 16, 2, 14, (shapes[1][0] + 12) // 14, 5, 48)
-    l2 = make_level(shapes[2], 8, 16, 8, shapes[2][1] + 16, 2, 10, (shapes[2][0] + 12) // 10, 6, 32)
+    l2 = make_level(shapes[2], 8, 16, 8, shapes[2][1] + 16, 2, 20, (shapes[2][0] + 12) // 20, 6, 32)
     cfg = types.SimpleNamespace(levels=(l0, l1, l2), counts=counts, stiffness=float((size + 1) ** 2))
     total = n_x * n_y * n_z
 

time: 49.1 us -> 48 us (0.978)
  Pallas kernels: 49.1 us -> 47.9 us
    pallas_call x1, Pallas kernels: 47.3 us -> 46.1 us  [local_cycle(): pl.pallas_call(functools.partial(kernel, cfg), out_shape=pltpu.VMEM(rhs.s...]
where the time goes in v11:
time: 48 us; the launch traced here: 47.9 us
  Pallas kernels  47.9 us (100%)
    pallas_call x1, Pallas kernels, local_cycle(): pl.pallas_call(functools.partial(kernel, cfg), out_shape=pltpu.VMEM(rhs.s...  46.1 us
    pallas_call x1, Pallas kernels, local_cycle(): pl.pallas_call(write_out, out_shape=jax.ShapeDtypeStruct(rhs.shape, F32),...  1.75 us

profile of v11, /device:TPU:97, one launch (start us, length us, event | category | flops | bytes accessed | tf_op | source)
XLA Modules:
  0.0 47.9 jit_solution(13011964236790878241)
XLA Ops:
  0.0 46.1 %shard_map.28.held = f32[64,64,128]{2,1,0:T(8,128)S(1)} custom-call(f32[64,64,128]{2,1,0:T(8,128)} %bitcast.3, f32[64,64,128]{2,1,0:T(8,128)} %bitcast.4), custom_call_target="tpu_custom_call" | custom-call | tf_op jit(solution)/shard_map/pallas_call | solution.py:712
  46.1 1.8 %shard_map.29 = f32[64,64,128]{2,1,0:T(8,128)} custom-call(f32[64,64,128]{2,1,0:T(8,128)S(1)} %shard_map.28.held), custom_call_target="tpu_custom_call" | custom-call | tf_op jit(solution)/shard_map/pallas_call | solution.py:720

commit v12 on v11

--- a/solution.py
+++ b/solution.py
@@ -467,19 +467,20 @@
         copy.wait()
     step = 4
 
+    def sort_planes_of(stage, first, n):
+        return sort_x(stage[pl.ds(first, n), inner].reshape(n * l0.nz, LANES)).reshape(n, l0.nz, LANES)
+
     for side, plane in enumerate((0, chip_y - l0.wide)):
-        for j in range(l0.wide):
-            edge_u[side, j] = sort_x(stage_u[plane + j, inner])
-            edge_f[side, j] = sort_x(stage_f[plane + j, inner])
+        for stage, edges in ((stage_u, edge_u), (stage_f, edge_f)):
+            edges[side] = sort_planes_of(stage, plane, l0.wide)
     begin(row_halo)
 
     def sort_planes(first, n):
         @pl.loop(0, n // step)
         def _(i):
-            for j in range(step):
-                y = first + i * step + j
-                sorted_u[y] = sort_x(stage_u[y, inner])
-                sorted_f[y] = sort_x(stage_f[y, inner])
+            y = first + i * step
+            sorted_u[pl.ds(y, step)] = sort_planes_of(stage_u, y, step)
+            sorted_f[pl.ds(y, step)] = sort_planes_of(stage_f, y, step)
 
     @pl.loop(0, PARTS)
     def _(part):
@@ -538,7 +539,7 @@
         ring = l0.wide + 1
         sweep(src, dst, f0, l0, mask0, scale, [(l0.top + k, ring), (l0.z0 + l0.nz - 1 - k, ring)], count=2, group=20)
         sweep(src, dst, f0, l0, mask0, scale, first=l0.begin + cx * l0.ny, count=1)
-    restrict_level(w0, f0, l0, mask0, g1, l1, 4, 8)
+    restrict_level(w0, f0, l0, mask0, g1, l1, 8, 8)
 
     exchange(1)
     first_sweep(a1, g1, l1, mask1)
@@ -690,7 +691,7 @@
     chip_y, nz, nx = rhs.shape
     shapes = [(chip_y // n_x >> k, nz >> k, nx * n_x >> k) for k in range(3)]
     l0 = make_level(shapes[0], 6, 8, 4, nz + 8, 2, 8, (shapes[0][0] + 8) // 8, 4, nz + 8)
-    l1 = make_level(shapes[1], 8, 16, 8, shapes[1][1] + 16, 2, 14, (shapes[1][0] + 12) // 14, 5, 48)
+    l1 = make_level(shapes[1], 8, 16, 8, shapes[1][1] + 16, 2, 28, (shapes[1][0] + 12) // 28, 5, 48)
     l2 = make_level(shapes[2], 8, 16, 8, shapes[2][1] + 16, 2, 20, (shapes[2][0] + 12) // 20, 6, 32)
     cfg = types.SimpleNamespace(levels=(l0, l1, l2), counts=counts, stiffness=float((size + 1) ** 2))
     total = n_x * n_y * n_z

time: 48 us -> 47.4 us (0.987)
  Pallas kernels: 47.9 us -> 47.3 us
    pallas_call x1, Pallas kernels: 46.1 us -> 45.5 us  [local_cycle(): pl.pallas_call(functools.partial(kernel, cfg), out_shape=pltpu.VMEM(rhs.s...]
where the time goes in v12:
time: 47.4 us; the launch traced here: 47.3 us
  Pallas kernels  47.3 us (100%)
    pallas_call x1, Pallas kernels, local_cycle(): pl.pallas_call(functools.partial(kernel, cfg), out_shape=pltpu.VMEM(rhs.s...  45.5 us
    pallas_call x1, Pallas kernels, local_cycle(): pl.pallas_call(write_out, out_shape=jax.ShapeDtypeStruct(rhs.shape, F32),...  1.75 us

profile of v12, /device:TPU:97, one launch (start us, length us, event | category | flops | bytes accessed | tf_op | source)
XLA Modules:
  0.0 47.3 jit_solution(16453204340750794985)
XLA Ops:
  0.0 45.5 %shard_map.28.held = f32[64,64,128]{2,1,0:T(8,128)S(1)} custom-call(f32[64,64,128]{2,1,0:T(8,128)} %bitcast.3, f32[64,64,128]{2,1,0:T(8,128)} %bitcast.4), custom_call_target="tpu_custom_call" | custom-call | tf_op jit(solution)/shard_map/pallas_call | solution.py:713
  45.5 1.8 %shard_map.29 = f32[64,64,128]{2,1,0:T(8,128)} custom-call(f32[64,64,128]{2,1,0:T(8,128)S(1)} %shard_map.28.held), custom_call_target="tpu_custom_call" | custom-call | tf_op jit(solution)/shard_map/pallas_call | solution.py:721
